TPU v7x, 256 devices: a whole 4x4x8 slice. The times are simulated.
256 devices in a mesh: sector: 8 (over z), op: 32 (over y, x, core).
Axes of the slice: x: 4, y: 4, z: 8, core: 2. Of those that a mesh axis runs over, the one named last changes fastest.
Arguments:
- wavefunction: float32 [8, 512, 512], P('sector', 'op'), may hold values from -6 to 6
- diagonal: float32 [8, 512, 512], P('sector', 'op'), may hold values from 2 to 10
- left_blocks: bfloat16 [256, 512, 512], P('op'), may hold values from -1 to 1
- right_blocks: bfloat16 [256, 512, 512], P('op'), may hold values from -1 to 1
- coupling: int32 [8, 256], replicated, may hold values from 0 to 7
- sector_sizes: int32 [8], replicated, may hold values from 256 to 512
Outputs:
- vector: float32 [8, 512, 512], P('sector', 'op')
- energies: float32 [2], replicated
All inputs are finite; a program needn't handle non-finite values.
Results may differ from a plain program's by a relative error of at most 0.0052.
Values may be sent and summed in bfloat16 or wider, within the bound.
No kernel may reach another device: no remote copies, remote signals or barrier semaphores. Data moves between devices by JAX's collectives and lax.ppermute only.
A program may use at most 64 MiB of HBM per device.

v0:
```python
import jax
import jax.numpy as jnp
from jax import lax
from jax.sharding import Mesh
from jax.sharding import PartitionSpec as P

STEPS = 2
OP = ("op_0", "op_1", "op_2")


def laid_out(blocks, dim):
    blocks = jnp.moveaxis(blocks, 0, dim)
    shape = blocks.shape
    return blocks.reshape(*shape[:dim], shape[dim] * shape[dim + 1], *shape[dim + 2 :])


def from_everyone(x, axis):
    peers = lax.axis_size(axis)
    return lax.all_to_all(jnp.broadcast_to(x[None], (peers, *x.shape)), axis, 0, 0, tiled=True)


def gathered_copies(x, axis, dim):
    return laid_out(from_everyone(x, axis), dim)


def whole_of(x, axes, dim):
    far, near = axes
    blocks = from_everyone(from_everyone(x, far), near)
    return laid_out(blocks.swapaxes(0, 1).reshape(-1, *x.shape), dim)


def cut_along(x, dim, peers):
    before, after = (x.shape[:dim], x.shape[dim + 1 :])
    return jnp.moveaxis(x.reshape(*before, peers, -1, *after), dim, 0)


def sum_at_owner(x, axis, dim):
    blocks = cut_along(x, dim, lax.axis_size(axis))
    arrived = lax.all_to_all(blocks, axis, split_axis=0, concat_axis=0, tiled=True)
    return arrived.sum(axis=0)


def of_everyone(x, axis):
    everything = from_everyone(x, axis)
    return jnp.sum(everything, axis=0)


def over_axes(x, axes):
    far, near = axes
    return of_everyone(of_everyone(x, near), far)


def together(arrays, axis):
    ends = [0]
    for a in arrays:
        ends.append(ends[-1] + a.size)
    running = over_axes(jnp.concatenate([a.ravel() for a in arrays]), axis)
    return tuple((running[b:e].reshape(a.shape) for a, b, e in zip(arrays, ends, ends[1:])))


def shards(wavefunction, diagonal, left_blocks, right_blocks, coupling, sector_sizes):
    sector_count, share_rows, block_width = wavefunction.shape
    pair_count = left_blocks.shape[0]
    op_count = lax.axis_size(OP)
    sector_place = lax.axis_index("sector")
    op_place = lax.axis_index(OP)
    first_sector = sector_place * sector_count
    my_coupling = lax.dynamic_slice_in_dim(coupling, first_sector, sector_count, 0)
    my_sizes = lax.dynamic_slice_in_dim(sector_sizes, first_sector, sector_count, 0)
    columns = jnp.arange(block_width, dtype=jnp.int32)
    row_ids = op_place * share_rows + jnp.arange(share_rows, dtype=jnp.int32)
    bound = my_sizes[:, None, None]
    share_mask = ((row_ids[None, :, None] < bound) & (columns[None, None, :] < bound)).astype(
        jnp.float32
    )
    full_mask = ((columns[None, :, None] < bound) & (columns[None, None, :] < bound)).astype(
        jnp.float32
    )
    entry_total = float(wavefunction.size * lax.axis_size("sector") * op_count)
    current = wavefunction * share_mask
    collected = []
    for iteration in range(STEPS):
        current_low = current.astype(jnp.bfloat16)
        rows_all = gathered_copies(current_low, "sector", 0)
        whole = whole_of(rows_all, (("op_0", "op_1"), "op_2"), 1)
        wanted = lax.dynamic_slice_in_dim(my_coupling, op_place * pair_count, pair_count, 1)
        sources = jnp.take(whole, wanted.reshape(-1), axis=0)
        sources = sources.reshape(sector_count, pair_count, block_width, block_width)
        half = jnp.einsum(
            "bij,abjk->abik", left_blocks, sources, preferred_element_type=jnp.float32
        ).astype(jnp.bfloat16)
        partial_terms = (
            jnp.einsum("abik,blk->ail", half, right_blocks, preferred_element_type=jnp.float32)
            * full_mask
        )
        sigma_share = sum_at_owner(partial_terms, OP, 1)
        numerator, denominator = together(
            (jnp.sum(current * sigma_share), jnp.sum(current * current)),
            (("sector", "op_0"), ("op_1", "op_2")),
        )
        theta = numerator / (denominator + 1e-06)
        collected.append(theta)
        gap = diagonal - theta
        update = current - (sigma_share - theta * current) * gap / (gap * gap + 1.0)
        squares = over_axes(jnp.sum(update * update), (("sector", "op_0"), ("op_1", "op_2")))
        current = update * lax.rsqrt(squares / entry_total + 1e-06)
    return (current, jnp.stack(collected))


def solution(mesh):
    split = Mesh(
        mesh.devices.reshape(mesh.shape["sector"], 4, 4, 2), ("sector", "op_0", "op_1", "op_2")
    )
    in_specs = (
        P("sector", OP, None),
        P("sector", OP, None),
        P(OP, None, None),
        P(OP, None, None),
        P(),
        P(),
    )
    out_specs = (P("sector", OP, None), P())
    return jax.shard_map(
        shards, mesh=split, in_specs=in_specs, out_specs=out_specs, check_vma=False
    )
```

profile of v0, /device:TPU:1, one launch (start us, length us, event | category | flops | bytes accessed | tf_op | source)
XLA Modules:
  0.0 291.2 jit_solution(6224911325497884049)
XLA Ops:
  0.6 1.2 dynamic_slice.8
  1.9 0.6 iota_compare_fusion
  2.6 0.7 add_compare_fusion
  3.2 0.8 fusion.41
  4.1 16.6 %all_to_all.88 = bf16[8,1,16,512]{3,2,1,0:T(8,128)(2,1)S(1)} all-to-all(bf16[8,1,16,512]{3,2,1,0:T(8,128)(2,1)S(1)} %broadcast_in_dim.46), channel_id=1, replica_groups=mesh['sector'=8,'op_0'=4,'op_1'=4,'op_2'=2] {'sector'}, dimensions={0} | all-to-all | bytes 262144 | tf_op jit(solution)/shard_map/all_to_all | solution.py:19
  20.6 1.6 broadcast_in_dim.48
  22.2 6.8 %all-to-all-start.1 = ((bf16[16,8,16,512]{3,2,1,0:T(8,128)(2,1)}), bf16[16,8,16,512]{3,2,1,0:T(8,128)(2,1)S(1)}, u32[]{:S(2)}, u32[]{:S(2)}) async-start(bf16[16,8,16,512]{3,2,1,0:T(8,128)(2,1)} %broadcast_in_dim.48), calls=%async_computation.1 | async-start | bytes 4194304 | tf_op jit(solution)/shard_map/all_to_all | solution.py:19
  29.0 0.8 compare_and_fusion
  29.8 24.9 %all-to-all-done.1 = bf16[16,8,16,512]{3,2,1,0:T(8,128)(2,1)S(1)} async-done(((bf16[16,8,16,512]{3,2,1,0:T(8,128)(2,1)}), bf16[16,8,16,512]{3,2,1,0:T(8,128)(2,1)S(1)}, u32[]{:S(2)}, u32[]{:S(2)}) %all-to-all-start.1) | async-done | bytes 2097184 | tf_op jit(solution)/shard_map/all_to_all | solution.py:19
  55.2 12.4 %all_to_all.89 = bf16[2,16,8,16,512]{4,3,2,1,0:T(8,128)(2,1)S(1)} all-to-all(bf16[2,16,8,16,512]{4,3,2,1,0:T(8,128)(2,1)S(1)} %broadcast_in_dim.49), channel_id=1, replica_groups=mesh['sector'=8,'op_0'=4,'op_1'=4,'op_2'=2] {'op_2'}, dimensions={0} | all-to-all | bytes 8388608 | tf_op jit(solution)/shard_map/all_to_all | solution.py:19
  67.6 0.7 copy.36
  68.3 2.4 copy.37
  70.7 5.0 %gather_fusion = bf16[8,512,512]{2,1,0:T(8,128)(2,1)} fusion(bf16[8,512,512]{2,1,0:T(8,128)(2,1)} %bitcast.94, s32[1024]{0:T(1024)S(1)} %pad_clamp_fusion), kind=kCustom, calls=%fused_computation.clone | custom fusion | bytes 8388640 | tf_op jit(solution)/shard_map/jit(_take)/gather | solution.py:87
  75.7 9.4 %and_select_fusion.1 = f32[512,512]{1,0:T(8,128)S(1)} fusion(bf16[8,512,512]{2,1,0:T(8,128)(2,1)} %param.11, pred[512]{0:T(512)(128)(4,1)S(1)} %iota_compare_fusion, bf16[8,512,512]{2,1,0:T(8,128)(2,1)} %param.10, bf16[8,512,512]{2,1,0:T(8,128)(2,1)} %gather_fusion, pred[8]{0:T(512)(128)(4,1)S(1)} %get-tuple-element.11), kind=kOutput, calls=%fused_computation.19 | convolution fusion | flops 4299685888 | bytes 13632008 | tf_op jit(solution)/shard_map/abik,blk->ail/dot_general | solution.py:93
  85.2 20.2 %all_to_all.90 = f32[32,1,16,512]{3,2,1,0:T(8,128)S(1)} all-to-all(f32[32,1,16,512]{3,2,1,0:T(8,128)S(1)} %bitcast.97), channel_id=1, replica_groups=mesh['sector'=8,'op_0'=4,'op_1'=4,'op_2'=2] {'op_0','op_1','op_2'}, dimensions={0} | all-to-all | bytes 2097152 | tf_op jit(solution)/shard_map/all_to_all | solution.py:39
  105.5 0.7 fusion.36
  106.2 1.4 pad_maximum_fusion
  107.5 7.4 %all_to_all.91 = f32[8,1,2]{2,1,0:T(1,128)S(1)} all-to-all(f32[8,1,2]{2,1,0:T(1,128)S(1)} %broadcast_in_dim.50), channel_id=1, replica_groups=mesh['sector'=8,'op_0'=4,'op_1'=4,'op_2'=2] {'op_1','op_2'}, dimensions={0} | all-to-all | bytes 128 | tf_op jit(solution)/shard_map/all_to_all | solution.py:19
  115.0 12.2 %all_to_all.92 = f32[32,1,2]{2,1,0:T(1,128)S(1)} all-to-all(f32[32,1,2]{2,1,0:T(1,128)S(1)} %broadcast_in_dim.51), channel_id=1, replica_groups=mesh['sector'=8,'op_0'=4,'op_1'=4,'op_2'=2] {'sector','op_0'}, dimensions={0} | all-to-all | bytes 512 | tf_op jit(solution)/shard_map/all_to_all | solution.py:19
  129.2 0.7 multiply_reduce_fusion.2
  129.9 0.6 broadcast_in_dim.52
  130.6 9.1 %all_to_all.93 = f32[8,1,1]{2,1,0:T(1,128)S(1)} all-to-all(f32[8,1,1]{2,1,0:T(1,128)S(1)} %broadcast_in_dim.52), channel_id=1, replica_groups=mesh['sector'=8,'op_0'=4,'op_1'=4,'op_2'=2] {'op_1','op_2'}, dimensions={0} | all-to-all | bytes 64 | tf_op jit(solution)/shard_map/all_to_all | solution.py:19
  139.7 0.6 reduce_sum.155
  140.3 0.7 broadcast_in_dim.53
  140.9 11.6 %all_to_all.94 = f32[32,1,1]{2,1,0:T(1,128)S(1)} all-to-all(f32[32,1,1]{2,1,0:T(1,128)S(1)} %broadcast_in_dim.53), channel_id=1, replica_groups=mesh['sector'=8,'op_0'=4,'op_1'=4,'op_2'=2] {'sector','op_0'}, dimensions={0} | all-to-all | bytes 256 | tf_op jit(solution)/shard_map/all_to_all | solution.py:19
  152.5 0.6 reduce_sum.156
  153.9 10.3 %all_to_all.95 = bf16[8,1,16,512]{3,2,1,0:T(8,128)(2,1)S(1)} all-to-all(bf16[8,1,16,512]{3,2,1,0:T(8,128)(2,1)S(1)} %broadcast_in_dim.55), channel_id=1, replica_groups=mesh['sector'=8,'op_0'=4,'op_1'=4,'op_2'=2] {'sector'}, dimensions={0} | all-to-all | bytes 262144 | tf_op jit(solution)/shard_map/all_to_all | solution.py:19
  164.4 27.8 %all_to_all.96 = bf16[16,8,16,512]{3,2,1,0:T(8,128)(2,1)S(1)} all-to-all(bf16[16,8,16,512]{3,2,1,0:T(8,128)(2,1)S(1)} %broadcast_in_dim.57), channel_id=1, replica_groups=mesh['sector'=8,'op_0'=4,'op_1'=4,'op_2'=2] {'op_0','op_1'}, dimensions={0} | all-to-all | bytes 4194304 | tf_op jit(solution)/shard_map/all_to_all | solution.py:19
  192.3 0.6 broadcast_in_dim.58
  192.9 11.2 %all_to_all.97 = bf16[2,16,8,16,512]{4,3,2,1,0:T(8,128)(2,1)S(1)} all-to-all(bf16[2,16,8,16,512]{4,3,2,1,0:T(8,128)(2,1)S(1)} %broadcast_in_dim.58), channel_id=1, replica_groups=mesh['sector'=8,'op_0'=4,'op_1'=4,'op_2'=2] {'op_2'}, dimensions={0} | all-to-all | bytes 8388608 | tf_op jit(solution)/shard_map/all_to_all | solution.py:19
  204.1 0.7 copy.45
  204.8 2.4 copy.46
  207.2 5.0 %gather_fusion.1 = bf16[8,512,512]{2,1,0:T(8,128)(2,1)} fusion(bf16[8,512,512]{2,1,0:T(8,128)(2,1)} %bitcast.92, s32[1024]{0:T(1024)S(1)} %pad_clamp_fusion), kind=kCustom, calls=%fused_computation.1.clone | custom fusion | bytes 8388640 | tf_op jit(solution)/shard_map/jit(_take)/gather | solution.py:87
  212.2 9.4 %and_select_fusion = f32[512,512]{1,0:T(8,128)S(1)} fusion(bf16[8,512,512]{2,1,0:T(8,128)(2,1)} %param.11, pred[512]{0:T(512)(128)(4,1)S(1)} %iota_compare_fusion, bf16[8,512,512]{2,1,0:T(8,128)(2,1)} %param.10, bf16[8,512,512]{2,1,0:T(8,128)(2,1)} %gather_fusion.1, pred[8]{0:T(512)(128)(4,1)S(1)} %get-tuple-element.11), kind=kOutput, calls=%fused_computation.18 | convolution fusion | flops 4299685888 | bytes 13632008 | tf_op jit(solution)/shard_map/abik,blk->ail/dot_general | solution.py:93
  221.6 20.2 %all_to_all.98 = f32[32,1,16,512]{3,2,1,0:T(8,128)S(1)} all-to-all(f32[32,1,16,512]{3,2,1,0:T(8,128)S(1)} %bitcast.96), channel_id=1, replica_groups=mesh['sector'=8,'op_0'=4,'op_1'=4,'op_2'=2] {'op_0','op_1','op_2'}, dimensions={0} | all-to-all | bytes 2097152 | tf_op jit(solution)/shard_map/all_to_all | solution.py:39
  241.9 0.6 fusion.32
  242.5 1.4 pad_maximum_fusion.1
  243.9 7.4 %all_to_all.99 = f32[8,1,2]{2,1,0:T(1,128)S(1)} all-to-all(f32[8,1,2]{2,1,0:T(1,128)S(1)} %broadcast_in_dim.59), channel_id=1, replica_groups=mesh['sector'=8,'op_0'=4,'op_1'=4,'op_2'=2] {'op_1','op_2'}, dimensions={0} | all-to-all | bytes 128 | tf_op jit(solution)/shard_map/all_to_all | solution.py:19
  251.4 11.6 %all_to_all.100 = f32[32,1,2]{2,1,0:T(1,128)S(1)} all-to-all(f32[32,1,2]{2,1,0:T(1,128)S(1)} %broadcast_in_dim.60), channel_id=1, replica_groups=mesh['sector'=8,'op_0'=4,'op_1'=4,'op_2'=2] {'sector','op_0'}, dimensions={0} | all-to-all | bytes 512 | tf_op jit(solution)/shard_map/all_to_all | solution.py:19
  264.9 0.6 multiply_reduce_fusion
  265.5 0.6 broadcast_in_dim.61
  266.2 8.8 %all_to_all.101 = f32[8,1,1]{2,1,0:T(1,128)S(1)} all-to-all(f32[8,1,1]{2,1,0:T(1,128)S(1)} %broadcast_in_dim.61), channel_id=1, replica_groups=mesh['sector'=8,'op_0'=4,'op_1'=4,'op_2'=2] {'op_1','op_2'}, dimensions={0} | all-to-all | bytes 64 | tf_op jit(solution)/shard_map/all_to_all | solution.py:19
  275.0 0.6 reduce_sum.164
  275.6 1.3 broadcast_in_dim.62
  276.8 3.8 %all-to-all-start.15 = ((f32[32,1,1]{2,1,0:T(1,128)}), f32[32,1,1]{2,1,0:T(1,128)S(1)}, u32[]{:S(2)}, u32[]{:S(2)}) async-start(f32[32,1,1]{2,1,0:T(1,128)} %broadcast_in_dim.62), calls=%async_computation.15 | async-start | bytes 32768 | tf_op jit(solution)/shard_map/all_to_all | solution.py:19
  281.3 8.0 %all-to-all-done.15 = f32[32,1,1]{2,1,0:T(1,128)S(1)} async-done(((f32[32,1,1]{2,1,0:T(1,128)}), f32[32,1,1]{2,1,0:T(1,128)S(1)}, u32[]{:S(2)}, u32[]{:S(2)}) %all-to-all-start.15) | async-done | bytes 160 | tf_op jit(solution)/shard_map/all_to_all | solution.py:19
  289.2 0.6 reduce_sum.165
  290.5 0.6 broadcast_multiply_fusion
  (23 shorter events, 2.9 us)
Async XLA Ops:
  22.2 32.4 %all-to-all-start.1 = ((bf16[16,8,16,512]{3,2,1,0:T(8,128)(2,1)}), bf16[16,8,16,512]{3,2,1,0:T(8,128)(2,1)S(1)}, u32[]{:S(2)}, u32[]{:S(2)}) async-start(bf16[16,8,16,512]{3,2,1,0:T(8,128)(2,1)} %broadcast_in_dim.48), calls=%async_computation.1 | async-start | bytes 4194304 | tf_op jit(solution)/shard_map/all_to_all | solution.py:19
  75.7 29.8 %copy-start = (f32[1,16,512]{2,1,0:T(8,128)S(1)}, f32[1,16,512]{2,1,0:T(8,128)}, u32[]{:S(2)}) copy-start(f32[1,16,512]{2,1,0:T(8,128)} %param.8) | copy-start | bytes 98308
  75.7 53.5 %copy-start.1 = (f32[1,16,512]{2,1,0:T(8,128)S(1)}, f32[1,16,512]{2,1,0:T(8,128)}, u32[]{:S(2)}) copy-start(f32[1,16,512]{2,1,0:T(8,128)} %param.9) | copy-start | bytes 98308
  276.8 12.4 %all-to-all-start.15 = ((f32[32,1,1]{2,1,0:T(1,128)}), f32[32,1,1]{2,1,0:T(1,128)S(1)}, u32[]{:S(2)}, u32[]{:S(2)}) async-start(f32[32,1,1]{2,1,0:T(1,128)} %broadcast_in_dim.62), calls=%async_computation.15 | async-start | bytes 32768 | tf_op jit(solution)/shard_map/all_to_all | solution.py:19
where the time goes:
time: 292 us; the launch traced here: 291 us
  blocking collectives  187 us (64%)
  waiting for transfers between devices  32.8 us (11%)
  local copies, waits for them, and re-layouts  24.9 us (9%)
  matrix products  18.9 us (6%)
  other arithmetic  12.3 us (4%)
  starting transfers between devices  10.6 us (4%)
  between operations  4.83 us (2%)
    all_to_all x12, blocking collectives, from_everyone(): lax.all_to_all(jnp.broadcast_to(x[None], (peers, *x.shape)), axis, 0, 0,...  146 us
    all_to_all x2, blocking collectives, sum_at_owner(): lax.all_to_all(blocks, axis, split_axis=0, concat_axis=0, tiled=True)  40.4 us
    all_to_all x2, waiting for transfers between devices, from_everyone(): lax.all_to_all(jnp.broadcast_to(x[None], (peers, *x.shape)), axis, 0, 0,...  32.8 us
    dot_general x2, matrix products, shards(): jnp.einsum('abik,blk->ail', half, right_blocks, preferred_element_type=jn...  18.9 us
    all_to_all x2, starting transfers between devices, from_everyone(): lax.all_to_all(jnp.broadcast_to(x[None], (peers, *x.shape)), axis, 0, 0,...  10.6 us
    gather x2, local copies, waits for them, and re-layouts, shards(): sources = jnp.take(whole, wanted.reshape(-1), axis=0)  9.94 us
    broadcast_in_dim x14, local copies, waits for them, and re-layouts, from_everyone(): jnp.broadcast_to(x[None], (peers, *x.shape))  6.33 us
  transfers between devices with their start and end apart: 2, of which 2 were waited for; matrix products, arithmetic and copies ran while one was open for 0% of the time, Pallas kernels for 0%

commit v1 on v0

v1 whole, which is shorter than its diff:
```python
import functools
import jax
import jax.numpy as jnp
from jax import lax
from jax.experimental import pallas as pl
from jax.experimental.pallas import tpu as pltpu
from jax.sharding import Mesh
from jax.sharding import PartitionSpec as P

OP = ("op_0", "op_1", "op_2")
CHIP = ("op_0", "op_1")
CORE = "op_2"
COLUMN = ("sector", "op_2")
BF = jnp.bfloat16
F32 = jnp.float32
VMEM = pl.BlockSpec(memory_space=pltpu.VMEM)
SMEM = pl.BlockSpec(memory_space=pltpu.SMEM)
ANY = pl.BlockSpec(memory_space=pl.ANY)


def swap_all(x, axes):
    return lax.all_to_all(x, axes, split_axis=0, concat_axis=0, tiled=True)


def other_core(x):
    return lax.ppermute(x, CORE, [(0, 1), (1, 0)])


def three_way(first, second):
    row = lax.broadcasted_iota(jnp.int32, (16, 128), 0)
    value = jnp.where(row < 3, first, second)
    high = value.astype(BF).astype(F32)
    middle = (value - high).astype(BF).astype(F32)
    low = value - high - middle
    part = jnp.where(row < 3, row, row - 3)
    return jnp.where(part == 0, high, jnp.where(part == 1, middle, low)).astype(BF)


def two_sums(tile):
    first = tile[0:1] + tile[1:2] + tile[2:3]
    second = tile[3:4] + tile[4:5] + tile[5:6]
    return first[:, :1], second[:, :1]


def place():
    z = lax.axis_index("sector")
    chip = lax.axis_index("op_0") * lax.axis_size("op_1") + lax.axis_index("op_1")
    return z, chip, lax.axis_index(CORE)


def live(shape, where_ref):
    first_row, size = where_ref[0], where_ref[1]
    row = lax.broadcasted_iota(jnp.int32, shape, 0) + first_row
    column = lax.broadcasted_iota(jnp.int32, shape, 1)
    return (row < size) & (column < size)


def opening_kernel(where_ref, wave_ref, diag_ref, send_ref, current_ref, square_ref):
    wave = wave_ref[...]
    current = jnp.where(live(wave.shape, where_ref), wave, 0.0)
    current_ref[...] = current
    square_ref[...] = jnp.full((8, 128), jnp.sum(current * current), F32)
    diag = diag_ref[...]
    high = diag.astype(BF)
    low = (diag - high.astype(F32)).astype(BF)
    current_low = current.astype(BF)
    width = wave.shape[1] // 2
    for peer in range(send_ref.shape[0]):
        cut = slice((peer % 2) * width, (peer % 2 + 1) * width)
        send_ref[peer, 0] = current_low[:, cut]
        send_ref[peer, 1] = high[:, cut]
        send_ref[peer, 2] = low[:, cut]


def product_kernel(
    where_ref, coupling_ref, rows_ref, left_a, right_a, left_b, right_b, total_ref, low_ref
):
    pair = pl.program_id(0)
    block = left_a.shape[1]
    halves = []
    for base, left in ((where_ref[3], left_a), (where_ref[4], left_b)):
        source = coupling_ref[where_ref[2], base + pair]
        rows = rows_ref[:, source].reshape(block, -1)
        halves.append(jnp.dot(left[0], rows, preferred_element_type=F32).astype(BF))
    half = jnp.concatenate(halves, axis=1)
    right = jnp.concatenate([right_a[0], right_b[0]], axis=1)
    term = lax.dot_general(half, right, (((1,), (1,)), ((), ())), preferred_element_type=F32)

    @pl.when(pair == 0)
    def _():
        total_ref[...] = term

    @pl.when(pair > 0)
    def _():
        total_ref[...] += term

    @pl.when(pair == pl.num_programs(0) - 1)
    def _():
        low_ref[...] = total_ref[...].astype(BF)


def products(where, coupling, rows, left, right, left_other, right_other):
    pairs, block, _ = left.shape
    width = rows.shape[-1]
    whole = rows.shape
    return pl.pallas_call(
        product_kernel,
        grid_spec=pltpu.PrefetchScalarGridSpec(
            num_scalar_prefetch=2,
            grid=(pairs,),
            in_specs=[
                pl.BlockSpec(whole, lambda p, w, c: (0,) * len(whole), pipeline_mode=pl.Buffered(1)),
                pl.BlockSpec((1, block, block), lambda p, w, c: (p, 0, 0)),
                pl.BlockSpec((1, block, width), lambda p, w, c: (p, 0, w[5])),
                pl.BlockSpec((1, block, block), lambda p, w, c: (p, 0, 0)),
                pl.BlockSpec((1, block, width), lambda p, w, c: (p, 0, w[5])),
            ],
            out_specs=[
                pl.BlockSpec((block, block), lambda p, w, c: (0, 0)),
                pl.BlockSpec((block, block), lambda p, w, c: (0, 0)),
            ],
        ),
        out_shape=[
            jax.ShapeDtypeStruct((block, block), F32),
            jax.ShapeDtypeStruct((block, block), BF),
        ],
        compiler_params=pltpu.CompilerParams(vmem_limit_bytes=40 << 20),
        name="products",
    )(where, coupling, rows, left, right, left_other, right_other)


def parting_kernel(where_ref, total_ref, other_ref, rows_ref, square_ref, send_ref):
    core = where_ref[5]
    block = total_ref.shape[0]
    width = rows_ref.shape[-1]
    cut = pl.ds(pl.multiple_of(core * width, width), width)
    mine = total_ref[:, cut] + other_ref[:, cut].astype(F32)
    vector = rows_ref[:, 0].reshape(block, width).astype(F32)
    extra = three_way(jnp.sum(vector * mine), square_ref[0, 0])
    for chip in range(send_ref.shape[0]):
        rows = pl.ds(pl.multiple_of(chip * 32 + core * 16, 16), 16)
        tile = (total_ref[rows, :] + other_ref[rows, :].astype(F32)).astype(BF)
        for j in range(block // 128):
            send_ref[chip, j * 16 : (j + 1) * 16, :] = tile[:, j * 128 : (j + 1) * 128]
        send_ref[chip, block // 8 : block // 8 + 16, :] = extra


def parting(where, total, other, rows, square):
    block = total.shape[0]
    chips, sectors, share, width = rows.shape
    return pl.pallas_call(
        parting_kernel,
        grid_spec=pltpu.PrefetchScalarGridSpec(
            num_scalar_prefetch=1,
            grid=(1,),
            in_specs=[
                pl.BlockSpec((block, block), lambda i, w: (0, 0)),
                pl.BlockSpec((block, block), lambda i, w: (0, 0)),
                pl.BlockSpec((chips, 1, share, width), lambda i, w: (0, w[2], 0, 0)),
                pl.BlockSpec((8, 128), lambda i, w: (0, 0)),
            ],
            out_specs=pl.BlockSpec((chips, block // 8 + 16, 128), lambda i, w: (0, 0, 0)),
        ),
        out_shape=jax.ShapeDtypeStruct((chips, block // 8 + 16, 128), BF),
        name="parting",
    )(where, total, other, rows, square)


def joining_kernel(where_ref, arrived_ref, sigma_ref, send_ref):
    total = arrived_ref[0].astype(F32)
    for chip in range(1, arrived_ref.shape[0]):
        total = total + arrived_ref[chip].astype(F32)
    parts = (total.shape[0] - 16) // 16
    sigma = jnp.concatenate([total[j * 16 : (j + 1) * 16] for j in range(parts)], axis=1)
    sigma = jnp.where(live(sigma.shape, where_ref), sigma, 0.0)
    sigma_ref[...] = sigma
    first, second = two_sums(total[parts * 16 :])
    extra = three_way(first, second)
    low = sigma.astype(BF)
    each = parts // 2
    for peer in range(send_ref.shape[0]):
        for j in range(each):
            at = ((peer % 2) * each + j) * 128
            send_ref[peer, j * 16 : (j + 1) * 16, :] = low[:, at : at + 128]
        send_ref[peer, each * 16 : each * 16 + 16, :] = extra


def scalars_of(arrived_ref):
    at = arrived_ref.shape[1] - 16
    total = arrived_ref[0, at:].astype(F32)
    for peer in range(1, arrived_ref.shape[0]):
        total = total + arrived_ref[peer, at:].astype(F32)
    return two_sums(total)


def sigma_of(arrived_ref, peer):
    parts = (arrived_ref.shape[1] - 16) // 16
    return jnp.concatenate(
        [arrived_ref[peer, j * 16 : (j + 1) * 16, :] for j in range(parts)], axis=1
    ).astype(F32)


def corrected(current, sigma, diag, theta):
    gap = diag - theta
    return current - (sigma - theta * current) * gap / (gap * gap + 1.0)


def middle_kernel(
    arrived_ref, begun_ref, sigma_ref, current_ref, diag_ref,
    send_ref, all_ref, own_ref, square_ref, theta_ref, low_ref, sems,
):
    first, second = scalars_of(arrived_ref)
    theta = first / (second + 1e-6)
    theta_ref[...] = jnp.broadcast_to(theta, (8, 128))
    for peer in range(arrived_ref.shape[0]):
        current = begun_ref[peer, 0].astype(F32)
        diag = begun_ref[peer, 1].astype(F32) + begun_ref[peer, 2].astype(F32)
        update = corrected(current, sigma_of(arrived_ref, peer), diag, theta)
        all_ref[peer] = update
        low_ref[peer] = update.astype(BF)
    own = corrected(current_ref[...], sigma_ref[...], diag_ref[...], theta)
    own_ref[...] = own
    square_ref[...] = jnp.full((8, 128), jnp.sum(own * own), F32)
    copies = [
        pltpu.make_async_copy(low_ref, send_ref.at[chip], sems.at[chip])
        for chip in range(send_ref.shape[0])
    ]
    for copy in copies:
        copy.start()
    for copy in copies:
        copy.wait()


def closing_kernel(
    entries, arrived_ref, begun_ref, all_ref, sigma_ref, own_ref, diag_ref, before_ref,
    final_ref, send_ref, theta_ref,
):
    first, second = scalars_of(arrived_ref)
    scale = lax.rsqrt(second / entries + 1e-6)
    squared = scale * scale
    theta = squared * first / (squared * second + 1e-6)
    lane = lax.broadcasted_iota(jnp.int32, (8, 128), 1)
    theta_ref[...] = jnp.where(lane == 0, before_ref[...], theta)
    total = jnp.zeros(all_ref.shape[1:], F32)
    for peer in range(arrived_ref.shape[0]):
        diag = begun_ref[peer, 1].astype(F32) + begun_ref[peer, 2].astype(F32)
        update = corrected(scale * all_ref[peer], scale * sigma_of(arrived_ref, peer), diag, theta)
        total = total + update * update
    final_ref[...] = corrected(scale * own_ref[...], scale * sigma_ref[...], diag_ref[...], theta)
    send_ref[...] = jnp.full(send_ref.shape, jnp.sum(total), F32)


def scaling_kernel(entries, arrived_ref, final_ref, vector_ref):
    total = arrived_ref[0]
    for peer in range(1, arrived_ref.shape[0]):
        total = total + arrived_ref[peer]
    vector_ref[...] = final_ref[...] * lax.rsqrt(total[0:1, 0:1] / entries + 1e-6)


def call(kernel, shapes, specs, name, scratch=(), out_specs=None):
    return pl.pallas_call(
        kernel,
        in_specs=specs,
        out_specs=out_specs if out_specs is not None else [VMEM] * len(shapes),
        out_shape=[jax.ShapeDtypeStruct(s, t) for s, t in shapes],
        scratch_shapes=scratch,
        name=name,
    )


def shards(wavefunction, diagonal, left_blocks, right_blocks, coupling, sector_sizes):
    _, share, block = wavefunction.shape
    pairs = left_blocks.shape[0]
    sectors = lax.axis_size("sector")
    chips = lax.axis_size("op_0") * lax.axis_size("op_1")
    width = block // 2
    entries = float(sectors * block * block)
    z, chip, core = place()
    mine = chip * 2 + core
    theirs = chip * 2 + 1 - core
    where = jnp.stack(
        [mine * share, sector_sizes[z], z, mine * pairs, theirs * pairs, core]
    ).astype(jnp.int32)
    wave, diag = wavefunction[0], diagonal[0]
    left_other = other_core(left_blocks)
    right_other = other_core(right_blocks)

    begin, current, square = call(
        opening_kernel,
        [((sectors * 2, 3, share, width), BF), ((share, block), F32), ((8, 128), F32)],
        [SMEM, VMEM, VMEM],
        "opening",
    )(where, wave, diag)
    begun = swap_all(begin, COLUMN)
    outgoing = jnp.broadcast_to(begun[None, :, 0], (chips, sectors * 2, share, width))

    def sigma_step(outgoing, square):
        rows = swap_all(outgoing, CHIP).reshape(chips, sectors, 2 * share, width)
        total, low = products(
            where, coupling, rows, left_blocks, right_blocks, left_other, right_other
        )
        send = parting(where, total, other_core(low), rows, square)
        sigma, send = call(
            joining_kernel,
            [((share, block), F32), ((sectors * 2, width // 8 + 16, 128), BF)],
            [SMEM, VMEM],
            "joining",
        )(where, swap_all(send, CHIP))
        return sigma, swap_all(send, COLUMN)

    sigma, arrived = sigma_step(outgoing, square)
    outgoing, everyone, own, square, theta = call(
        middle_kernel,
        [
            ((chips, sectors * 2, share, width), BF),
            ((sectors * 2, share, width), F32),
            ((share, block), F32),
            ((8, 128), F32),
            ((8, 128), F32),
        ],
        [VMEM] * 5,
        "middle",
        [pltpu.VMEM((sectors * 2, share, width), BF), pltpu.SemaphoreType.DMA((chips,))],
        [ANY, VMEM, VMEM, VMEM, VMEM],
    )(arrived, begun, sigma, current, diag)

    sigma, arrived = sigma_step(outgoing, square)
    final, send, thetas = call(
        functools.partial(closing_kernel, entries),
        [((share, block), F32), ((chips * 2, 8, 128), F32), ((8, 128), F32)],
        [VMEM] * 7,
        "closing",
    )(arrived, begun, everyone, sigma, own, diag, theta)
    (vector,) = call(
        functools.partial(scaling_kernel, entries),
        [((share, block), F32)],
        [VMEM] * 2,
        "scaling",
    )(swap_all(send, OP), final)
    return vector[None], thetas[0, :2]


def solution(mesh):
    split = Mesh(
        mesh.devices.reshape(mesh.shape["sector"], 4, 4, 2), ("sector", "op_0", "op_1", "op_2")
    )
    in_specs = (
        P("sector", OP, None),
        P("sector", OP, None),
        P(OP, None, None),
        P(OP, None, None),
        P(),
        P(),
    )
    out_specs = (P("sector", OP, None), P())
    return jax.shard_map(
        shards, mesh=split, in_specs=in_specs, out_specs=out_specs, check_vma=False
    )
```

time: 292 us -> 221 us (0.76)
  Pallas kernels: 0 us -> 38 us
  blocking collectives: 187 us -> 150 us
  waiting for transfers between devices: 32.8 us -> 9.19 us
  matrix products: 18.9 us -> 0 us
  other arithmetic: 12.3 us -> 0 us
  local copies, waits for them, and re-layouts: 24.9 us -> 14 us
  between operations: 4.83 us -> 0.79 us
    pallas_call x0 -> x10, Pallas kernels: none -> 38 us  [the longest x2 19.2 us: products(): pl.pallas_call(product_kernel, grid_spec=pltpu.PrefetchScalarGridSpec(num...]
    all_to_all x14 -> x7, blocking collectives: 187 us -> 150 us  [swap_all(): return lax.all_to_all(x, axes, split_axis=0, concat_axis=0, tiled=True)]
    all_to_all x2 -> x1, waiting for transfers between devices: 32.8 us -> 6.11 us  [swap_all(): return lax.all_to_all(x, axes, split_axis=0, concat_axis=0, tiled=True)]
    dot_general x2 -> x0, matrix products: 18.9 us -> none  [shards(): jnp.einsum('abik,blk->ail', half, right_blocks, preferred_element_type=jn...]
    unnamed x4 -> x30, local copies, waits for them, and re-layouts: 0.01 us -> 10.1 us
    gather x2 -> x0, local copies, waits for them, and re-layouts: 9.94 us -> none  [shards(): sources = jnp.take(whole, wanted.reshape(-1), axis=0)]
    all_to_all x2 -> x1, starting transfers between devices: 10.6 us -> 3.64 us  [swap_all(): return lax.all_to_all(x, axes, split_axis=0, concat_axis=0, tiled=True)]
    broadcast_in_dim x14 -> x2, local copies, waits for them, and re-layouts: 6.33 us -> 0.21 us  [shards(): jnp.broadcast_to(begun[None, :, 0], (chips, sectors * 2, share, width))]
  transfers between devices with their start and end apart: 2 -> 5, of which waited for: 2 -> 3; matrix products, arithmetic and copies ran while one was open for 0% -> 2% of each run, Pallas kernels for 0% -> 1%
where the time goes in v1:
time: 221 us; the launch traced here: 220 us
  blocking collectives  150 us (68%)
  Pallas kernels  38 us (17%)
  local copies, waits for them, and re-layouts  14 us (6%)
  waiting for transfers between devices  9.19 us (4%)
  starting transfers between devices  8.01 us (4%)
    all_to_all x7, blocking collectives, swap_all(): return lax.all_to_all(x, axes, split_axis=0, concat_axis=0, tiled=True)  150 us
    pallas_call x2, Pallas kernels, products(): pl.pallas_call(product_kernel, grid_spec=pltpu.PrefetchScalarGridSpec(num...  19.2 us
    unnamed x30, local copies, waits for them, and re-layouts  10.1 us
    pallas_call x2, Pallas kernels, parting(): pl.pallas_call(parting_kernel, grid_spec=pltpu.PrefetchScalarGridSpec(num...  6.46 us
    all_to_all x1, waiting for transfers between devices, swap_all(): return lax.all_to_all(x, axes, split_axis=0, concat_axis=0, tiled=True)  6.11 us
  transfers between devices with their start and end apart: 5, of which 3 were waited for; matrix products, arithmetic and copies ran while one was open for 2% of the time, Pallas kernels for 1%

profile of v1, /device:TPU:1, one launch (start us, length us, event | category | flops | bytes accessed | tf_op | source)
XLA Modules:
  0.0 219.9 jit_solution(17478908479777422865)
XLA Ops:
  0.6 0.0 copy-start.10
  0.6 3.3 %collective-permute-start = (bf16[8,512,512]{2,1,0:T(8,128)(2,1)}, bf16[8,512,512]{2,1,0:T(8,128)(2,1)}, u32[]{:S(2)}, u32[]{:S(2)}) collective-permute-start(bf16[8,512,512]{2,1,0:T(8,128)(2,1)} %left_a.3), channel_id=1, source_target_pairs={{0,1},{1,0},{2,3},{3,2},{4,5},{5,4},{6,7},{7,6},{8,9},{9,8},{10,11... | collective-permute-start | bytes 12582920 | tf_op jit(solution)/shard_map/ppermute | solution.py:26
  3.9 0.1 collective-permute-start.1
  4.0 1.3 dynamic_slice.3
  5.3 1.3 stack.23.where_ref
  6.6 1.6 opening.1
  8.2 21.9 %all_to_all.40.begun_ref = bf16[16,3,16,256]{3,2,1,0:T(8,128)(2,1)S(1)} all-to-all(bf16[16,3,16,256]{3,2,1,0:T(8,128)(2,1)} %get-tuple-element.21), channel_id=1, replica_groups=mesh['sector'=8,'op_0'=4,'op_1'=4,'op_2'=2] {'sector','op_2'}, dimensions={0} | all-to-all | bytes 786432 | tf_op jit(solution)/shard_map/all_to_all | solution.py:22
  30.1 0.2 broadcast_in_dim.11
  30.3 36.6 %all_to_all.41 = bf16[16,16,16,256]{3,2,1,0:T(8,128)(2,1)S(1)} all-to-all(bf16[16,16,16,256]{3,2,1,0:T(8,128)(2,1)S(1)} %broadcast_in_dim.11), channel_id=1, replica_groups=mesh['sector'=8,'op_0'=4,'op_1'=4,'op_2'=2] {'op_0','op_1'}, dimensions={0} | all-to-all | bytes 4194304 | tf_op jit(solution)/shard_map/all_to_all | solution.py:22
  66.9 0.0 collective-permute-done.left_b
  66.9 0.0 collective-permute-done.1.right_b
  67.0 0.0 copy-done.10
  67.0 0.0 copy-done.8
  67.0 0.0 copy-done.2
  67.0 0.0 copy-start.4
  67.0 2.9 %copy-done.4 = bf16[8,512,512]{2,1,0:T(8,128)(2,1)S(1)} copy-done((bf16[8,512,512]{2,1,0:T(8,128)(2,1)S(1)}, bf16[8,512,512]{2,1,0:T(8,128)(2,1)}, u32[]{:S(2)}) %copy-start.4) | copy-done | bytes 4194328
  69.9 9.6 %products.2 = (f32[512,512]{1,0:T(8,128)S(1)}, bf16[512,512]{1,0:T(8,128)(2,1)S(1)}) custom-call(s32[6]{0:T(128)S(1)} %copy-done.8, s32[8,256]{1,0:T(8,128)S(1)} %copy-done.10, bf16[16,8,32,256]{3,2,1,0:T(8,128)(2,1)S(1)} %bitcast.14, bf16[8,512,512]{2,1,0:T(8,128)(2,1)S(1)} %copy-done.2, bf16[8,512,512]{2,1,0:T(8,128)(2,1)S(1)} %copy-done.4, ...), custom_call_target="tpu_custom_call" | custom-call | tf_op jit(solution)/shard_map/products/pallas_call | solution.py:106
  79.5 0.0 copy-done.11
  79.5 0.0 copy-done
  79.5 0.0 copy-start.7
  79.5 1.0 copy-done.7
  80.5 0.4 collective-permute-start.2
  80.9 1.5 collective-permute-done.2.other_ref
  82.4 0.8 copy-done.12
  83.2 3.3 %parting.2 = bf16[16,80,128]{2,1,0:T(8,128)(2,1)} custom-call(s32[6]{0:T(128)} %stack.23.where_ref, f32[512,512]{1,0:T(8,128)} %copy-done.7, bf16[512,512]{1,0:T(8,128)(2,1)} %copy-done.12, bf16[16,8,32,256]{3,2,1,0:T(8,128)(2,1)} %bitcast.15, f32[8,128]{1,0:T(8,128)} %get-tuple-element.24.square_ref), custom_call_target="tpu_custom_call" | custom-call | tf_op jit(solution)/shard_map/parting/pallas_call | solution.py:151
  86.5 13.2 %all_to_all.42.arrived_ref = bf16[16,80,128]{2,1,0:T(8,128)(2,1)} all-to-all(bf16[16,80,128]{2,1,0:T(8,128)(2,1)} %parting.2), channel_id=1, replica_groups=mesh['sector'=8,'op_0'=4,'op_1'=4,'op_2'=2] {'op_0','op_1'}, dimensions={0} | all-to-all | bytes 655360 | tf_op jit(solution)/shard_map/all_to_all | solution.py:22
  99.8 1.8 joining.2
  101.5 15.6 %all_to_all.43.arrived_ref = bf16[16,48,128]{2,1,0:T(8,128)(2,1)} all-to-all(bf16[16,48,128]{2,1,0:T(8,128)(2,1)} %get-tuple-element.25), channel_id=1, replica_groups=mesh['sector'=8,'op_0'=4,'op_1'=4,'op_2'=2] {'sector','op_2'}, dimensions={0} | all-to-all | bytes 393216 | tf_op jit(solution)/shard_map/all_to_all | solution.py:22
  117.1 3.5 %middle.1 = (bf16[16,16,16,256]{3,2,1,0:T(8,128)(2,1)}, f32[16,16,256]{2,1,0:T(8,128)}, f32[16,512]{1,0:T(8,128)}, f32[8,128]{1,0:T(8,128)}, f32[8,128]{1,0:T(8,128)}) custom-call(bf16[16,48,128]{2,1,0:T(8,128)(2,1)} %all_to_all.43.arrived_ref, bf16[16,3,16,256]{3,2,1,0:T(8,128)(2,1)} %copy-done.11, f32[16,512]{1,0:T(8,128)} %get-tuple-element.26.sigma_ref, ...), custom_call_target="tpu_custom_call" | custom-call | tf_op jit(solution)/shard_map/middle/pallas_call | solution.py:312
  120.6 0.0 copy-start.3
  120.6 33.7 %all_to_all.44 = bf16[16,16,16,256]{3,2,1,0:T(8,128)(2,1)S(1)} all-to-all(bf16[16,16,16,256]{3,2,1,0:T(8,128)(2,1)} %get-tuple-element.28), channel_id=1, replica_groups=mesh['sector'=8,'op_0'=4,'op_1'=4,'op_2'=2] {'op_0','op_1'}, dimensions={0} | all-to-all | bytes 4194304 | tf_op jit(solution)/shard_map/all_to_all | solution.py:22
  154.3 0.0 copy-done.3
  154.3 2.9 %copy-done.5 = bf16[8,512,512]{2,1,0:T(8,128)(2,1)S(1)} copy-done((bf16[8,512,512]{2,1,0:T(8,128)(2,1)S(1)}, bf16[8,512,512]{2,1,0:T(8,128)(2,1)}, u32[]{:S(2)}) %copy-start.5) | copy-done | bytes 4194328
  157.2 9.6 %products.3 = (f32[512,512]{1,0:T(8,128)S(1)}, bf16[512,512]{1,0:T(8,128)(2,1)S(1)}) custom-call(s32[6]{0:T(128)S(1)} %copy-done.9, s32[8,256]{1,0:T(8,128)S(1)} %copy-done.10, bf16[16,8,32,256]{3,2,1,0:T(8,128)(2,1)S(1)} %bitcast.16, bf16[8,512,512]{2,1,0:T(8,128)(2,1)S(1)} %copy-done.3, bf16[8,512,512]{2,1,0:T(8,128)(2,1)S(1)} %copy-done.5, ...), custom_call_target="tpu_custom_call" | custom-call | tf_op jit(solution)/shard_map/products/pallas_call | solution.py:106
  166.9 1.0 copy-done.6
  167.9 0.6 collective-permute-start.3
  168.5 1.5 collective-permute-done.3.other_ref
  170.0 0.8 copy-done.13
  170.8 3.1 %parting.3 = bf16[16,80,128]{2,1,0:T(8,128)(2,1)} custom-call(s32[6]{0:T(128)} %stack.23.where_ref, f32[512,512]{1,0:T(8,128)} %copy-done.6, bf16[512,512]{1,0:T(8,128)(2,1)} %copy-done.13, bf16[16,8,32,256]{3,2,1,0:T(8,128)(2,1)} %bitcast.17, f32[8,128]{1,0:T(8,128)} %get-tuple-element.31.square_ref), custom_call_target="tpu_custom_call" | custom-call | tf_op jit(solution)/shard_map/parting/pallas_call | solution.py:151
  173.9 13.2 %all_to_all.45.arrived_ref = bf16[16,80,128]{2,1,0:T(8,128)(2,1)} all-to-all(bf16[16,80,128]{2,1,0:T(8,128)(2,1)} %parting.3), channel_id=1, replica_groups=mesh['sector'=8,'op_0'=4,'op_1'=4,'op_2'=2] {'op_0','op_1'}, dimensions={0} | all-to-all | bytes 655360 | tf_op jit(solution)/shard_map/all_to_all | solution.py:22
  187.2 1.8 joining.3
  188.9 15.6 %all_to_all.46.arrived_ref = bf16[16,48,128]{2,1,0:T(8,128)(2,1)} all-to-all(bf16[16,48,128]{2,1,0:T(8,128)(2,1)} %get-tuple-element.32), channel_id=1, replica_groups=mesh['sector'=8,'op_0'=4,'op_1'=4,'op_2'=2] {'sector','op_2'}, dimensions={0} | all-to-all | bytes 393216 | tf_op jit(solution)/shard_map/all_to_all | solution.py:22
  204.5 2.2 closing.1
  206.7 3.6 %all-to-all-start.7 = ((f32[32,8,128]{2,1,0:T(8,128)}), f32[32,8,128]{2,1,0:T(8,128)S(1)}, u32[]{:S(2)}, u32[]{:S(2)}) async-start(f32[32,8,128]{2,1,0:T(8,128)} %get-tuple-element.37), calls=%async_computation.7 | async-start | bytes 262144 | tf_op jit(solution)/shard_map/all_to_all | solution.py:22
  210.3 1.2 slice_bitcast_fusion.1
  211.5 6.1 %all-to-all-done.7.arrived_ref = f32[32,8,128]{2,1,0:T(8,128)S(1)} async-done(((f32[32,8,128]{2,1,0:T(8,128)}), f32[32,8,128]{2,1,0:T(8,128)S(1)}, u32[]{:S(2)}, u32[]{:S(2)}) %all-to-all-start.7) | async-done | bytes 131104 | tf_op jit(solution)/shard_map/all_to_all | solution.py:22
  217.6 0.6 copy-done.14
  218.3 1.6 scaling.1
  (14 shorter events, 0.0 us)
Async XLA Ops:
  0.6 66.3 %copy-start.10 = (s32[8,256]{1,0:T(8,128)S(1)}, s32[8,256]{1,0:T(8,128)}, u32[]{:S(2)}) copy-start(s32[8,256]{1,0:T(8,128)} %coupling_ref.3) | copy-start | bytes 24580
  0.6 66.3 %collective-permute-start = (bf16[8,512,512]{2,1,0:T(8,128)(2,1)}, bf16[8,512,512]{2,1,0:T(8,128)(2,1)}, u32[]{:S(2)}, u32[]{:S(2)}) collective-permute-start(bf16[8,512,512]{2,1,0:T(8,128)(2,1)} %left_a.3), channel_id=1, source_target_pairs={{0,1},{1,0},{2,3},{3,2},{4,5},{5,4},{6,7},{7,6},{8,9},{9,8},{10,11... | collective-permute-start | bytes 12582920 | tf_op jit(solution)/shard_map/ppermute | solution.py:26
  3.9 63.0 %collective-permute-start.1 = (bf16[8,512,512]{2,1,0:T(8,128)(2,1)}, bf16[8,512,512]{2,1,0:T(8,128)(2,1)}, u32[]{:S(2)}, u32[]{:S(2)}) collective-permute-start(bf16[8,512,512]{2,1,0:T(8,128)(2,1)} %right_a.3), channel_id=1, source_target_pairs={{0,1},{1,0},{2,3},{3,2},{4,5},{5,4},{6,7},{7,6},{8,9},{9,8},{10,11... | collective-permute-start | bytes 12582920 | tf_op jit(solution)/shard_map/ppermute | solution.py:26
  6.6 60.4 %copy-start.8 = (s32[6]{0:T(128)S(1)}, s32[6]{0:T(128)}, u32[]{:S(2)}) copy-start(s32[6]{0:T(128)} %stack.23.where_ref) | copy-start | bytes 76
  8.2 58.8 %copy-start.2 = (bf16[8,512,512]{2,1,0:T(8,128)(2,1)S(1)}, bf16[8,512,512]{2,1,0:T(8,128)(2,1)}, u32[]{:S(2)}) copy-start(bf16[8,512,512]{2,1,0:T(8,128)(2,1)} %left_a.3) | copy-start | bytes 12582916
  30.1 49.4 %copy-start.11 = (bf16[16,3,16,256]{3,2,1,0:T(8,128)(2,1)}, bf16[16,3,16,256]{3,2,1,0:T(8,128)(2,1)S(1)}, u32[]{:S(2)}) copy-start(bf16[16,3,16,256]{3,2,1,0:T(8,128)(2,1)S(1)} %all_to_all.40.begun_ref) | copy-start | bytes 1179652
  66.9 12.6 %copy-start = (bf16[16,16,16,256]{3,2,1,0:T(8,128)(2,1)}, bf16[16,16,16,256]{3,2,1,0:T(8,128)(2,1)S(1)}, u32[]{:S(2)}) copy-start(bf16[16,16,16,256]{3,2,1,0:T(8,128)(2,1)S(1)} %all_to_all.41) | copy-start | bytes 6291460
  67.0 2.9 %copy-start.4 = (bf16[8,512,512]{2,1,0:T(8,128)(2,1)S(1)}, bf16[8,512,512]{2,1,0:T(8,128)(2,1)}, u32[]{:S(2)}) copy-start(bf16[8,512,512]{2,1,0:T(8,128)(2,1)} %right_a.3) | copy-start | bytes 12582916
  79.5 1.0 copy-start.7
  80.5 1.9 collective-permute-start.2
  82.4 0.8 copy-start.12
  83.2 71.1 %copy-start.9 = (s32[6]{0:T(128)S(1)}, s32[6]{0:T(128)}, u32[]{:S(2)}) copy-start(s32[6]{0:T(128)} %stack.23.where_ref) | copy-start | bytes 76
  120.6 33.7 %copy-start.3 = (bf16[8,512,512]{2,1,0:T(8,128)(2,1)S(1)}, bf16[8,512,512]{2,1,0:T(8,128)(2,1)}, u32[]{:S(2)}) copy-start(bf16[8,512,512]{2,1,0:T(8,128)(2,1)} %left_a.3) | copy-start | bytes 12582916
  154.3 12.6 %copy-start.1 = (bf16[16,16,16,256]{3,2,1,0:T(8,128)(2,1)}, bf16[16,16,16,256]{3,2,1,0:T(8,128)(2,1)S(1)}, u32[]{:S(2)}) copy-start(bf16[16,16,16,256]{3,2,1,0:T(8,128)(2,1)S(1)} %all_to_all.44) | copy-start | bytes 6291460
  154.3 2.9 %copy-start.5 = (bf16[8,512,512]{2,1,0:T(8,128)(2,1)S(1)}, bf16[8,512,512]{2,1,0:T(8,128)(2,1)}, u32[]{:S(2)}) copy-start(bf16[8,512,512]{2,1,0:T(8,128)(2,1)} %right_a.3) | copy-start | bytes 12582916
  166.8 1.0 copy-start.6
  167.9 2.1 collective-permute-start.3
  170.0 0.8 copy-start.13
  206.7 10.9 %all-to-all-start.7 = ((f32[32,8,128]{2,1,0:T(8,128)}), f32[32,8,128]{2,1,0:T(8,128)S(1)}, u32[]{:S(2)}, u32[]{:S(2)}) async-start(f32[32,8,128]{2,1,0:T(8,128)} %get-tuple-element.37), calls=%async_computation.7 | async-start | bytes 262144 | tf_op jit(solution)/shard_map/all_to_all | solution.py:22
  217.6 0.6 copy-start.14

commit v2 on v1

v2 whole, which is shorter than its diff:
```python
import functools
import jax
import jax.numpy as jnp
from jax import lax
from jax.experimental import pallas as pl
from jax.experimental.pallas import tpu as pltpu
from jax.sharding import Mesh
from jax.sharding import PartitionSpec as P

OP = ("op_0", "op_1", "op_2")
CHIP = ("op_0", "op_1")
CORE = "op_2"
COLUMN = ("sector", "op_2")
BF = jnp.bfloat16
F32 = jnp.float32
VMEM = pl.BlockSpec(memory_space=pltpu.VMEM)
SMEM = pl.BlockSpec(memory_space=pltpu.SMEM)
ANY = pl.BlockSpec(memory_space=pl.ANY)
SHARE = 16
LANES = 128


def swap_all(x, axes):
    return lax.all_to_all(x, axes, split_axis=0, concat_axis=0, tiled=True)


def other_core(x):
    return lax.ppermute(x, CORE, [(0, 1), (1, 0)])


def three_way(first, second):
    row = lax.broadcasted_iota(jnp.int32, (16, 128), 0)
    value = jnp.where(row < 3, first, second)
    high = value.astype(BF).astype(F32)
    middle = (value - high).astype(BF).astype(F32)
    low = value - high - middle
    part = jnp.where(row < 3, row, row - 3)
    return jnp.where(part == 0, high, jnp.where(part == 1, middle, low)).astype(BF)


def two_sums(tile):
    first = tile[0:1] + tile[1:2] + tile[2:3]
    second = tile[3:4] + tile[4:5] + tile[5:6]
    return first[:, :1], second[:, :1]


def place():
    z = lax.axis_index("sector")
    chip = lax.axis_index("op_0") * lax.axis_size("op_1") + lax.axis_index("op_1")
    return z, chip, lax.axis_index(CORE)


def live(shape, first_row, size):
    row = lax.broadcasted_iota(jnp.int32, shape, 0) + first_row
    column = lax.broadcasted_iota(jnp.int32, shape, 1)
    return (row < size) & (column < size)


def stacked(ref, lead, tile):
    rows, block = tile.shape
    for j in range(block // LANES):
        ref[lead, j * rows : (j + 1) * rows, :] = tile[:, j * LANES : (j + 1) * LANES]


def unstacked(value, rows):
    parts = value.shape[0] // rows
    return jnp.concatenate([value[j * rows : (j + 1) * rows] for j in range(parts)], axis=1)


def opening_kernel(sizes_ref, wave_ref, diag_ref, send_ref, current_ref, square_ref):
    z, chip, core = place()
    wave = wave_ref[0]
    inside = live(wave.shape, (chip * 2 + core) * SHARE, sizes_ref[z])
    current = jnp.where(inside, wave, 0.0)
    current_ref[...] = current
    square_ref[...] = jnp.full((8, LANES), jnp.sum(current * current), F32)
    diag = diag_ref[0]
    high = diag.astype(BF)
    low = (diag - high.astype(F32)).astype(BF)
    current_low = current.astype(BF)
    for peer in range(send_ref.shape[0]):
        send_ref[peer, 0] = current_low
        send_ref[peer, 1] = high
        send_ref[peer, 2] = low


def halves_of(z, width):
    half = z % 2
    near = pl.ds(pl.multiple_of(half * width, width), width)
    far = pl.ds(pl.multiple_of((1 - half) * width, width), width)
    return near, far


def slabs(rows_at, send_ref):
    z, _, _ = place()
    chips, count, _, width = send_ref.shape
    near, far = halves_of(z, width)
    for k in range(count):
        if k < count - 2:
            slab = rows_at(k, near)
        else:
            slab = rows_at((z // 2) * 2 + k - (count - 2), far)
        for chip in range(chips):
            send_ref[chip, k] = slab


def spreading_kernel(begun_ref, send_ref):
    slabs(lambda k, cut: begun_ref[k, 0, :, cut], send_ref)


def product_kernel(
    coupling_ref, mine_ref, theirs_ref, left_a, right_a, left_b, right_b, square_ref,
    send_ref, total, rows, sems,
):
    pair = pl.program_id(0)
    z, chip, core = place()
    target = (z // 2) * 2 + core
    block, width = total.shape[0], rows.shape[-1]

    @pl.when(pair == 0)
    def _():
        copies = []
        for k in range(rows.shape[0]):
            for j, (ref, at) in enumerate(((mine_ref, core), (theirs_ref, 1 - core))):
                copies.append(
                    pltpu.make_async_copy(ref.at[:, k], rows.at[k, :, at], sems.at[2 * k + j])
                )
        for copy in copies:
            copy.start()
        for copy in copies:
            copy.wait()

    halves = []
    for owner, left in ((core, left_a), (1 - core, left_b)):
        source = coupling_ref[target, (chip * 2 + owner) * pl.num_programs(0) + pair]
        vector = rows[source].reshape(block, width)
        halves.append(jnp.dot(left[0], vector, preferred_element_type=F32).astype(BF))
    half = jnp.concatenate(halves, axis=1)
    right = jnp.concatenate([right_a[0], right_b[0]], axis=1)
    term = lax.dot_general(half, right, (((1,), (1,)), ((), ())), preferred_element_type=F32)

    @pl.when(pair == 0)
    def _():
        total[...] = term

    @pl.when(pair > 0)
    def _():
        total[...] += term

    @pl.when(pair == pl.num_programs(0) - 1)
    def _():
        near, far = halves_of(z, width)
        here = rows[target].reshape(block, width).astype(F32)
        there = rows[rows.shape[0] - 2 + core].reshape(block, width).astype(F32)
        product = jnp.sum(here * total[:, near] + there * total[:, far])
        extra = three_way(product, square_ref[0, 0])
        for peer in range(send_ref.shape[0]):
            stacked(send_ref, peer, total[peer * 32 : (peer + 1) * 32, :].astype(BF))
            send_ref[peer, block // 4 :, :] = extra


def products(coupling, mine, theirs, left, right, left_other, right_other, square):
    pairs, block, _ = left.shape
    chips, count, share, width = mine.shape
    operator = pl.BlockSpec((1, block, block), lambda p, c: (p, 0, 0))
    columns = pl.BlockSpec((1, block, width), lambda p, c: (p, 0, lax.axis_index("sector") % 2))
    return pl.pallas_call(
        product_kernel,
        grid_spec=pltpu.PrefetchScalarGridSpec(
            num_scalar_prefetch=1,
            grid=(pairs,),
            in_specs=[
                ANY, ANY, operator, columns, operator, columns,
                pl.BlockSpec((8, LANES), lambda p, c: (0, 0)),
            ],
            out_specs=pl.BlockSpec((chips, block // 4 + 16, LANES), lambda p, c: (0, 0, 0)),
            scratch_shapes=[
                pltpu.VMEM((block, block), F32),
                pltpu.VMEM((count, chips, 2, share, width), BF),
                pltpu.SemaphoreType.DMA((2 * count,)),
            ],
        ),
        out_shape=jax.ShapeDtypeStruct((chips, block // 4 + 16, LANES), BF),
        compiler_params=pltpu.CompilerParams(vmem_limit_bytes=60 << 20),
        name="products",
    )(coupling, mine, theirs, left, right, left_other, right_other, square)


def joining_kernel(sizes_ref, arrived_ref, send_ref):
    z, chip, core = place()
    total = arrived_ref[0].astype(F32)
    for peer in range(1, arrived_ref.shape[0]):
        total = total + arrived_ref[peer].astype(F32)
    end = total.shape[0] - 16
    sigma = unstacked(total[:end], 32)
    inside = live(sigma.shape, chip * 32, sizes_ref[(z // 2) * 2 + core])
    low = jnp.where(inside, sigma, 0.0).astype(BF)
    extra = three_way(*two_sums(total[end:]))
    for peer in range(send_ref.shape[0]):
        at = (peer % 2) * SHARE
        stacked(send_ref, peer, low[at : at + SHARE])
        send_ref[peer, end // 2 :, :] = extra


def scalars_of(arrived_ref):
    at = arrived_ref.shape[1] - 16
    total = arrived_ref[0, at:].astype(F32)
    for peer in range(1, arrived_ref.shape[0]):
        total = total + arrived_ref[peer, at:].astype(F32)
    return two_sums(total)


def sigma_of(arrived_ref, target):
    end = arrived_ref.shape[1] - 16
    at = (target // 2) * 4 + target % 2
    both = arrived_ref[at, :end].astype(F32) + arrived_ref[at + 2, :end].astype(F32)
    return unstacked(both, SHARE)


def corrected(current, sigma, diag, theta):
    gap = diag - theta
    return current - (sigma - theta * current) * gap / (gap * gap + 1.0)


def middle_kernel(
    arrived_ref, begun_ref, current_ref, diag_ref,
    send_ref, all_ref, own_ref, square_ref, theta_ref, low_ref,
):
    z, _, _ = place()
    first, second = scalars_of(arrived_ref)
    theta = first / (second + 1e-6)
    theta_ref[...] = jnp.broadcast_to(theta, (8, LANES))
    for k in range(all_ref.shape[0]):
        diag = begun_ref[k, 1].astype(F32) + begun_ref[k, 2].astype(F32)
        update = corrected(begun_ref[k, 0].astype(F32), sigma_of(arrived_ref, k), diag, theta)
        all_ref[k] = update
        low_ref[k] = update.astype(BF)
    own = corrected(current_ref[...], sigma_of(arrived_ref, z), diag_ref[0], theta)
    own_ref[...] = own
    square_ref[...] = jnp.full((8, LANES), jnp.sum(own * own), F32)
    slabs(lambda k, cut: low_ref[k, :, cut], send_ref)


def closing_kernel(
    entries, arrived_ref, begun_ref, all_ref, own_ref, diag_ref, before_ref,
    final_ref, send_ref, theta_ref,
):
    z, _, _ = place()
    first, second = scalars_of(arrived_ref)
    scale = lax.rsqrt(second / entries + 1e-6)
    squared = scale * scale
    theta = squared * first / (squared * second + 1e-6)
    lane = lax.broadcasted_iota(jnp.int32, (8, LANES), 1)
    theta_ref[...] = jnp.where(lane == 0, before_ref[...], theta)
    total = jnp.zeros(all_ref.shape[1:], F32)
    for k in range(all_ref.shape[0]):
        diag = begun_ref[k, 1].astype(F32) + begun_ref[k, 2].astype(F32)
        update = corrected(scale * all_ref[k], scale * sigma_of(arrived_ref, k), diag, theta)
        total = total + update * update
    sigma = sigma_of(arrived_ref, z)
    final_ref[...] = corrected(scale * own_ref[...], scale * sigma, diag_ref[0], theta)
    send_ref[...] = jnp.full(send_ref.shape, jnp.sum(total), F32)


def scaling_kernel(entries, arrived_ref, final_ref, vector_ref):
    total = arrived_ref[0]
    for peer in range(1, arrived_ref.shape[0]):
        total = total + arrived_ref[peer]
    vector_ref[0] = final_ref[...] * lax.rsqrt(total[0:1, 0:1] / entries + 1e-6)


def call(kernel, shapes, specs, name, scratch=()):
    return pl.pallas_call(
        kernel,
        in_specs=specs,
        out_specs=[VMEM] * len(shapes),
        out_shape=[jax.ShapeDtypeStruct(s, t) for s, t in shapes],
        scratch_shapes=scratch,
        compiler_params=pltpu.CompilerParams(vmem_limit_bytes=16 << 20),
        name=name,
    )


def shards(wavefunction, diagonal, left_blocks, right_blocks, coupling, sector_sizes):
    _, share, block = wavefunction.shape
    sectors = lax.axis_size("sector")
    chips = lax.axis_size("op_0") * lax.axis_size("op_1")
    width = block // 2
    entries = float(sectors * block * block)
    left_other = other_core(left_blocks)
    right_other = other_core(right_blocks)
    spread = ((chips, sectors + 2, share, width), BF)
    scalar = ((8, LANES), F32)

    begin, current, square = call(
        opening_kernel,
        [((sectors, 3, share, block), BF), ((share, block), F32), scalar],
        [SMEM, VMEM, VMEM],
        "opening",
    )(sector_sizes, wavefunction, diagonal)
    begun = swap_all(begin, "sector")
    (outgoing,) = call(spreading_kernel, [spread], [VMEM], "spreading")(begun)

    def sigma_step(outgoing, square):
        mine = swap_all(outgoing, CHIP)
        send = products(
            coupling, mine, other_core(mine),
            left_blocks, right_blocks, left_other, right_other, square,
        )
        (send,) = call(
            joining_kernel,
            [((sectors * 2, block // 8 + 16, LANES), BF)],
            [SMEM, VMEM],
            "joining",
        )(sector_sizes, swap_all(send, CHIP))
        return swap_all(send, COLUMN)

    arrived = sigma_step(outgoing, square)
    outgoing, everyone, own, square, theta = call(
        middle_kernel,
        [spread, ((sectors, share, block), F32), ((share, block), F32), scalar, scalar],
        [VMEM] * 4,
        "middle",
        [pltpu.VMEM((sectors, share, block), BF)],
    )(arrived, begun, current, diagonal)

    arrived = sigma_step(outgoing, square)
    final, send, thetas = call(
        functools.partial(closing_kernel, entries),
        [((share, block), F32), ((chips * 2, 8, LANES), F32), scalar],
        [VMEM] * 6,
        "closing",
    )(arrived, begun, everyone, own, diagonal, theta)
    (vector,) = call(
        functools.partial(scaling_kernel, entries),
        [((1, share, block), F32)],
        [VMEM] * 2,
        "scaling",
    )(swap_all(send, OP), final)
    return vector, thetas[0, :2]


def solution(mesh):
    split = Mesh(
        mesh.devices.reshape(mesh.shape["sector"], 4, 4, 2), ("sector", "op_0", "op_1", "op_2")
    )
    in_specs = (
        P("sector", OP, None),
        P("sector", OP, None),
        P(OP, None, None),
        P(OP, None, None),
        P(),
        P(),
    )
    out_specs = (P("sector", OP, None), P())
    return jax.shard_map(
        shards, mesh=split, in_specs=in_specs, out_specs=out_specs, check_vma=False
    )
```

time: 221 us -> 199 us (0.900)
  blocking collectives: 150 us -> 133 us
  Pallas kernels: 38 us -> 32.2 us
  local copies, waits for them, and re-layouts: 14 us -> 8.31 us
  waiting for transfers between devices: 9.19 us -> 12.3 us
  starting transfers between devices: 8.01 us -> 10.7 us
    all_to_all x7, blocking collectives: 150 us -> 133 us  [swap_all(): return lax.all_to_all(x, axes, split_axis=0, concat_axis=0, tiled=True)]
    pallas_call x7 -> x6, Pallas kernels: 16.7 us -> 3.22 us  [the longest x2 1.36 us: sigma_step(): call(joining_kernel, [((sectors * 2, block // 8 + 16, LANES), BF)], [SMEM...]
    pallas_call x2, Pallas kernels: 19.2 us -> 28 us  [products(): pl.pallas_call(product_kernel, grid_spec=pltpu.PrefetchScalarGridSpec(num...]
    ppermute x4, starting transfers between devices: 4.37 us -> 7.02 us  [other_core(): return lax.ppermute(x, CORE, [(0, 1), (1, 0)])]
    unnamed x30 -> x26, local copies, waits for them, and re-layouts: 10.1 us -> 7.79 us
    ppermute x4, waiting for transfers between devices: 3.08 us -> 5.33 us  [other_core(): return lax.ppermute(x, CORE, [(0, 1), (1, 0)])]
  transfers between devices with their start and end apart: 5 -> 5, of which waited for: 3 -> 3; matrix products, arithmetic and copies ran while one was open for 2% -> 0% of each run, Pallas kernels for 1% -> 0%
where the time goes in v2:
time: 199 us; the launch traced here: 198 us
  blocking collectives  133 us (67%)
  Pallas kernels  32.2 us (16%)
  waiting for transfers between devices  12.3 us (6%)
  starting transfers between devices  10.7 us (5%)
  local copies, waits for them, and re-layouts  8.31 us (4%)
    all_to_all x7, blocking collectives, swap_all(): return lax.all_to_all(x, axes, split_axis=0, concat_axis=0, tiled=True)  133 us
    pallas_call x2, Pallas kernels, products(): pl.pallas_call(product_kernel, grid_spec=pltpu.PrefetchScalarGridSpec(num...  28 us
    unnamed x26, local copies, waits for them, and re-layouts  7.79 us
    ppermute x4, starting transfers between devices, other_core(): return lax.ppermute(x, CORE, [(0, 1), (1, 0)])  7.02 us
    all_to_all x1, waiting for transfers between devices, swap_all(): return lax.all_to_all(x, axes, split_axis=0, concat_axis=0, tiled=True)  6.98 us
    ppermute x4, waiting for transfers between devices, other_core(): return lax.ppermute(x, CORE, [(0, 1), (1, 0)])  5.33 us
  transfers between devices with their start and end apart: 5, of which 3 were waited for; matrix products, arithmetic and copies ran while one was open for 0% of the time, Pallas kernels for 0%

profile of v2, /device:TPU:1, one launch (start us, length us, event | category | flops | bytes accessed | tf_op | source)
XLA Modules:
  0.0 197.6 jit_solution(7369372395583437664)
XLA Ops:
  0.6 3.3 %collective-permute-start.1 = (bf16[8,512,512]{2,1,0:T(8,128)(2,1)}, bf16[8,512,512]{2,1,0:T(8,128)(2,1)S(1)}, u32[]{:S(2)}, u32[]{:S(2)}) collective-permute-start(bf16[8,512,512]{2,1,0:T(8,128)(2,1)} %left_a.3), channel_id=1, source_target_pairs={{0,1},{1,0},{2,3},{3,2},{4,5},{5,4},{6,7},{7,6},{8,9},{9,8},{10,11... | collective-permute-start | bytes 12582920 | tf_op jit(solution)/shard_map/ppermute | solution.py:28
  3.9 0.1 collective-permute-start.2
  4.0 0.0 copy-start
  4.0 0.8 copy-done
  4.8 0.0 copy-start.2
  4.8 0.8 copy-done.2
  5.5 0.0 copy-start.3
  5.5 0.7 copy-done.3
  6.2 0.7 opening.1
  6.9 0.0 copy-start.5
  6.9 0.6 copy-done.5
  7.5 20.1 %all_to_all.40.begun_ref = bf16[8,3,16,512]{3,2,1,0:T(8,128)(2,1)S(1)} all-to-all(bf16[8,3,16,512]{3,2,1,0:T(8,128)(2,1)S(1)} %get-tuple-element.13), channel_id=1, replica_groups=mesh['sector'=8,'op_0'=4,'op_1'=4,'op_2'=2] {'sector'}, dimensions={0} | all-to-all | bytes 786432 | tf_op jit(solution)/shard_map/all_to_all | solution.py:24
  27.5 0.1 spreading.1
  27.7 24.5 %all_to_all.41.mine_ref = bf16[16,10,16,256]{3,2,1,0:T(8,128)(2,1)S(1)} all-to-all(bf16[16,10,16,256]{3,2,1,0:T(8,128)(2,1)S(1)} %spreading.1), channel_id=1, replica_groups=mesh['sector'=8,'op_0'=4,'op_1'=4,'op_2'=2] {'op_0','op_1'}, dimensions={0} | all-to-all | bytes 2621440 | tf_op jit(solution)/shard_map/all_to_all | solution.py:24
  52.1 0.0 copy-start.9
  52.1 3.2 %collective-permute-start = (bf16[16,10,16,256]{3,2,1,0:T(8,128)(2,1)S(1)}, bf16[16,10,16,256]{3,2,1,0:T(8,128)(2,1)S(1)}, u32[]{:S(2)}, u32[]{:S(2)}) collective-permute-start(bf16[16,10,16,256]{3,2,1,0:T(8,128)(2,1)S(1)} %all_to_all.41.mine_ref), channel_id=1, source_target_pairs={{0,1},{1,0},{2,3},{3,2},{4,5},{5,4},{6,7},{7,6},{8,9},{9,8},{10,11... | collective-permute-start | bytes 3932168 | tf_op jit(solution)/shard_map/ppermute | solution.py:28
  55.4 2.7 %collective-permute-done.theirs_ref = bf16[16,10,16,256]{3,2,1,0:T(8,128)(2,1)S(1)} collective-permute-done((bf16[16,10,16,256]{3,2,1,0:T(8,128)(2,1)S(1)}, bf16[16,10,16,256]{3,2,1,0:T(8,128)(2,1)S(1)}, u32[]{:S(2)}, u32[]{:S(2)}) %collective-permute-start) | collective-permute-done | bytes 1310752 | tf_op jit(solution)/shard_map/ppermute | solution.py:28
  58.0 0.0 copy-start.11
  58.0 0.0 collective-permute-done.1.left_b
  58.0 0.0 collective-permute-done.2.right_b
  58.0 2.0 copy-done.7
  60.0 2.0 %copy-done.8 = bf16[8,512,512]{2,1,0:T(8,128)(2,1)} copy-done((bf16[8,512,512]{2,1,0:T(8,128)(2,1)}, bf16[8,512,512]{2,1,0:T(8,128)(2,1)S(1)}, u32[]{:S(2)}) %copy-start.8) | copy-done | bytes 4194328
  62.0 0.0 copy-done.9
  62.0 0.0 copy-done.11
  62.0 14.0 %products.2 = bf16[16,144,128]{2,1,0:T(8,128)(2,1)} custom-call(s32[8,256]{1,0:T(8,128)} %coupling_ref.3, bf16[16,10,16,256]{3,2,1,0:T(8,128)(2,1)} %copy-done.9, bf16[16,10,16,256]{3,2,1,0:T(8,128)(2,1)} %copy-done.11, bf16[8,512,512]{2,1,0:T(8,128)(2,1)} %left_a.3, bf16[8,512,512]{2,1,0:T(8,128)(2,1)} %right_a.3, bf16[8,512,512]{2,1,0:T(8,128)(2,1)} %copy-done.7, ...), custom_call_target="tpu_custom_call" | custom-call | tf_op jit(solution)/shard_map/products/pallas_call | solution.py:167
  76.0 0.0 copy-start.1
  76.1 15.2 %all_to_all.42.arrived_ref = bf16[16,144,128]{2,1,0:T(8,128)(2,1)S(1)} all-to-all(bf16[16,144,128]{2,1,0:T(8,128)(2,1)} %products.2), channel_id=1, replica_groups=mesh['sector'=8,'op_0'=4,'op_1'=4,'op_2'=2] {'op_0','op_1'}, dimensions={0} | all-to-all | bytes 1179648 | tf_op jit(solution)/shard_map/all_to_all | solution.py:24
  91.3 0.0 copy-done.4
  91.3 0.7 joining.2
  92.0 17.2 %all_to_all.43.arrived_ref = bf16[16,80,128]{2,1,0:T(8,128)(2,1)S(1)} all-to-all(bf16[16,80,128]{2,1,0:T(8,128)(2,1)S(1)} %joining.2), channel_id=1, replica_groups=mesh['sector'=8,'op_0'=4,'op_1'=4,'op_2'=2] {'sector','op_2'}, dimensions={0} | all-to-all | bytes 655360 | tf_op jit(solution)/shard_map/all_to_all | solution.py:24
  109.2 0.0 copy-done.1
  109.2 0.4 middle.1
  109.6 0.0 copy-start.6
  109.6 24.1 %all_to_all.44.mine_ref = bf16[16,10,16,256]{3,2,1,0:T(8,128)(2,1)S(1)} all-to-all(bf16[16,10,16,256]{3,2,1,0:T(8,128)(2,1)S(1)} %get-tuple-element.16), channel_id=1, replica_groups=mesh['sector'=8,'op_0'=4,'op_1'=4,'op_2'=2] {'op_0','op_1'}, dimensions={0} | all-to-all | bytes 2621440 | tf_op jit(solution)/shard_map/all_to_all | solution.py:24
  133.6 0.0 copy-done.6
  133.6 0.4 collective-permute-start.3
  134.0 2.7 %collective-permute-done.3.theirs_ref = bf16[16,10,16,256]{3,2,1,0:T(8,128)(2,1)S(1)} collective-permute-done((bf16[16,10,16,256]{3,2,1,0:T(8,128)(2,1)S(1)}, bf16[16,10,16,256]{3,2,1,0:T(8,128)(2,1)S(1)}, u32[]{:S(2)}, u32[]{:S(2)}) %collective-permute-start.3) | collective-permute-done | bytes 1310752 | tf_op jit(solution)/shard_map/ppermute | solution.py:28
  136.7 0.0 copy-done.10
  136.7 1.1 copy-done.12
  137.8 13.9 %products.3 = bf16[16,144,128]{2,1,0:T(8,128)(2,1)} custom-call(s32[8,256]{1,0:T(8,128)} %coupling_ref.3, bf16[16,10,16,256]{3,2,1,0:T(8,128)(2,1)} %copy-done.10, bf16[16,10,16,256]{3,2,1,0:T(8,128)(2,1)} %copy-done.12, bf16[8,512,512]{2,1,0:T(8,128)(2,1)} %left_a.3, bf16[8,512,512]{2,1,0:T(8,128)(2,1)} %right_a.3, bf16[8,512,512]{2,1,0:T(8,128)(2,1)} %copy-done.7, ...), custom_call_target="tpu_custom_call" | custom-call | tf_op jit(solution)/shard_map/products/pallas_call | solution.py:167
  151.7 15.2 %all_to_all.45.arrived_ref = bf16[16,144,128]{2,1,0:T(8,128)(2,1)S(1)} all-to-all(bf16[16,144,128]{2,1,0:T(8,128)(2,1)} %products.3), channel_id=1, replica_groups=mesh['sector'=8,'op_0'=4,'op_1'=4,'op_2'=2] {'op_0','op_1'}, dimensions={0} | all-to-all | bytes 1179648 | tf_op jit(solution)/shard_map/all_to_all | solution.py:24
  166.9 0.7 joining.3
  167.6 17.2 %all_to_all.46.arrived_ref = bf16[16,80,128]{2,1,0:T(8,128)(2,1)S(1)} all-to-all(bf16[16,80,128]{2,1,0:T(8,128)(2,1)S(1)} %joining.3), channel_id=1, replica_groups=mesh['sector'=8,'op_0'=4,'op_1'=4,'op_2'=2] {'sector','op_2'}, dimensions={0} | all-to-all | bytes 655360 | tf_op jit(solution)/shard_map/all_to_all | solution.py:24
  184.8 1.0 closing.1
  185.8 3.6 %all-to-all-start.7 = ((f32[32,8,128]{2,1,0:T(8,128)}), f32[32,8,128]{2,1,0:T(8,128)S(1)}, u32[]{:S(2)}, u32[]{:S(2)}) async-start(f32[32,8,128]{2,1,0:T(8,128)} %get-tuple-element.21), calls=%async_computation.7 | async-start | bytes 262144 | tf_op jit(solution)/shard_map/all_to_all | solution.py:24
  189.4 0.5 slice_bitcast_fusion
  189.9 7.0 %all-to-all-done.7.arrived_ref = f32[32,8,128]{2,1,0:T(8,128)S(1)} async-done(((f32[32,8,128]{2,1,0:T(8,128)}), f32[32,8,128]{2,1,0:T(8,128)S(1)}, u32[]{:S(2)}, u32[]{:S(2)}) %all-to-all-start.7) | async-done | bytes 131104 | tf_op jit(solution)/shard_map/all_to_all | solution.py:24
  196.9 0.7 scaling.1
  (5 shorter events, 0.0 us)
Async XLA Ops:
  0.6 57.4 %collective-permute-start.1 = (bf16[8,512,512]{2,1,0:T(8,128)(2,1)}, bf16[8,512,512]{2,1,0:T(8,128)(2,1)S(1)}, u32[]{:S(2)}, u32[]{:S(2)}) collective-permute-start(bf16[8,512,512]{2,1,0:T(8,128)(2,1)} %left_a.3), channel_id=1, source_target_pairs={{0,1},{1,0},{2,3},{3,2},{4,5},{5,4},{6,7},{7,6},{8,9},{9,8},{10,11... | collective-permute-start | bytes 12582920 | tf_op jit(solution)/shard_map/ppermute | solution.py:28
  3.9 54.1 %collective-permute-start.2 = (bf16[8,512,512]{2,1,0:T(8,128)(2,1)}, bf16[8,512,512]{2,1,0:T(8,128)(2,1)S(1)}, u32[]{:S(2)}, u32[]{:S(2)}) collective-permute-start(bf16[8,512,512]{2,1,0:T(8,128)(2,1)} %right_a.3), channel_id=1, source_target_pairs={{0,1},{1,0},{2,3},{3,2},{4,5},{5,4},{6,7},{7,6},{8,9},{9,8},{10,11... | collective-permute-start | bytes 12582920 | tf_op jit(solution)/shard_map/ppermute | solution.py:28
  4.0 0.8 copy-start
  4.8 0.8 copy-start.2
  5.5 0.7 copy-start.3
  6.9 0.6 copy-start.5
  52.1 9.9 %copy-start.9 = (bf16[16,10,16,256]{3,2,1,0:T(8,128)(2,1)}, bf16[16,10,16,256]{3,2,1,0:T(8,128)(2,1)S(1)}, u32[]{:S(2)}) copy-start(bf16[16,10,16,256]{3,2,1,0:T(8,128)(2,1)S(1)} %all_to_all.41.mine_ref) | copy-start | bytes 3932164
  52.1 5.9 %collective-permute-start = (bf16[16,10,16,256]{3,2,1,0:T(8,128)(2,1)S(1)}, bf16[16,10,16,256]{3,2,1,0:T(8,128)(2,1)S(1)}, u32[]{:S(2)}, u32[]{:S(2)}) collective-permute-start(bf16[16,10,16,256]{3,2,1,0:T(8,128)(2,1)S(1)} %all_to_all.41.mine_ref), channel_id=1, source_target_pairs={{0,1},{1,0},{2,3},{3,2},{4,5},{5,4},{6,7},{7,6},{8,9},{9,8},{10,11... | collective-permute-start | bytes 3932168 | tf_op jit(solution)/shard_map/ppermute | solution.py:28
  58.0 4.0 %copy-start.11 = (bf16[16,10,16,256]{3,2,1,0:T(8,128)(2,1)}, bf16[16,10,16,256]{3,2,1,0:T(8,128)(2,1)S(1)}, u32[]{:S(2)}) copy-start(bf16[16,10,16,256]{3,2,1,0:T(8,128)(2,1)S(1)} %collective-permute-done.theirs_ref) | copy-start | bytes 3932164
  58.0 2.0 copy-start.7
  60.0 2.0 %copy-start.8 = (bf16[8,512,512]{2,1,0:T(8,128)(2,1)}, bf16[8,512,512]{2,1,0:T(8,128)(2,1)S(1)}, u32[]{:S(2)}) copy-start(bf16[8,512,512]{2,1,0:T(8,128)(2,1)S(1)} %collective-permute-done.2.right_b) | copy-start | bytes 12582916
  62.0 29.3 %copy-start.4 = (s32[8]{0:T(128)S(1)}, s32[8]{0:T(128)}, u32[]{:S(2)}) copy-start(s32[8]{0:T(128)} %sizes_ref.5) | copy-start | bytes 100
  76.0 33.1 %copy-start.1 = (f32[1,16,512]{2,1,0:T(8,128)S(1)}, f32[1,16,512]{2,1,0:T(8,128)}, u32[]{:S(2)}) copy-start(f32[1,16,512]{2,1,0:T(8,128)} %diag_ref.5) | copy-start | bytes 98308
  109.6 24.1 %copy-start.6 = (f32[8,128]{1,0:T(8,128)}, f32[8,128]{1,0:T(8,128)S(1)}, u32[]{:S(2)}) copy-start(f32[8,128]{1,0:T(8,128)S(1)} %get-tuple-element.17.square_ref) | copy-start | bytes 12292
  133.6 3.1 %copy-start.10 = (bf16[16,10,16,256]{3,2,1,0:T(8,128)(2,1)}, bf16[16,10,16,256]{3,2,1,0:T(8,128)(2,1)S(1)}, u32[]{:S(2)}) copy-start(bf16[16,10,16,256]{3,2,1,0:T(8,128)(2,1)S(1)} %all_to_all.44.mine_ref) | copy-start | bytes 3932164
  133.6 3.1 %collective-permute-start.3 = (bf16[16,10,16,256]{3,2,1,0:T(8,128)(2,1)S(1)}, bf16[16,10,16,256]{3,2,1,0:T(8,128)(2,1)S(1)}, u32[]{:S(2)}, u32[]{:S(2)}) collective-permute-start(bf16[16,10,16,256]{3,2,1,0:T(8,128)(2,1)S(1)} %all_to_all.44.mine_ref), channel_id=1, source_target_pairs={{0,1},{1,0},{2,3},{3,2},{4,5},{5,4},{6,7},{7,6},{8,9},{9,8},{10,11... | collective-permute-start | bytes 3932168 | tf_op jit(solution)/shard_map/ppermute | solution.py:28
  136.7 1.1 copy-start.12
  185.8 11.1 %all-to-all-start.7 = ((f32[32,8,128]{2,1,0:T(8,128)}), f32[32,8,128]{2,1,0:T(8,128)S(1)}, u32[]{:S(2)}, u32[]{:S(2)}) async-start(f32[32,8,128]{2,1,0:T(8,128)} %get-tuple-element.21), calls=%async_computation.7 | async-start | bytes 262144 | tf_op jit(solution)/shard_map/all_to_all | solution.py:24

commit v3 on v2

--- a/solution.py
+++ b/solution.py
@@ -15,7 +15,7 @@
 F32 = jnp.float32
 VMEM = pl.BlockSpec(memory_space=pltpu.VMEM)
 SMEM = pl.BlockSpec(memory_space=pltpu.SMEM)
-ANY = pl.BlockSpec(memory_space=pl.ANY)
+HBM = pl.BlockSpec(memory_space=pltpu.HBM)
 SHARE = 16
 LANES = 128
 
@@ -110,78 +110,85 @@
 
 def product_kernel(
     coupling_ref, mine_ref, theirs_ref, left_a, right_a, left_b, right_b, square_ref,
-    send_ref, total, rows, sems,
+    send_ref, total, rows, lefts, rights, halves, sems,
 ):
-    pair = pl.program_id(0)
     z, chip, core = place()
     target = (z // 2) * 2 + core
     block, width = total.shape[0], rows.shape[-1]
-
-    @pl.when(pair == 0)
-    def _():
-        copies = []
-        for k in range(rows.shape[0]):
-            for j, (ref, at) in enumerate(((mine_ref, core), (theirs_ref, 1 - core))):
-                copies.append(
-                    pltpu.make_async_copy(ref.at[:, k], rows.at[k, :, at], sems.at[2 * k + j])
-                )
-        for copy in copies:
+    pairs = left_a.shape[0]
+    cut, _ = halves_of(z, width)
+
+    def operators(pair):
+        return [
+            pltpu.make_async_copy(left_a.at[pair], lefts.at[pair, 0], sems.at[pair, 0]),
+            pltpu.make_async_copy(left_b.at[pair], lefts.at[pair, 1], sems.at[pair, 1]),
+            pltpu.make_async_copy(
+                right_a.at[pair, :, cut], rights.at[pair, :, :width], sems.at[pair, 2]
+            ),
+            pltpu.make_async_copy(
+                right_b.at[pair, :, cut], rights.at[pair, :, width:], sems.at[pair, 3]
+            ),
+        ]
+
+    for pair in range(pairs):
+        for copy in operators(pair):
             copy.start()
-        for copy in copies:
+    for k in range(rows.shape[0]):
+        for at in range(mine_ref.shape[0]):
+            rows[k, 2 * at + core] = mine_ref[at, k]
+            rows[k, 2 * at + 1 - core] = theirs_ref[at, k]
+    total[...] = jnp.zeros_like(total)
+
+    def first(pair):
+        for copy in operators(pair):
             copy.wait()
-
-    halves = []
-    for owner, left in ((core, left_a), (1 - core, left_b)):
-        source = coupling_ref[target, (chip * 2 + owner) * pl.num_programs(0) + pair]
-        vector = rows[source].reshape(block, width)
-        halves.append(jnp.dot(left[0], vector, preferred_element_type=F32).astype(BF))
-    half = jnp.concatenate(halves, axis=1)
-    right = jnp.concatenate([right_a[0], right_b[0]], axis=1)
-    term = lax.dot_general(half, right, (((1,), (1,)), ((), ())), preferred_element_type=F32)
-
-    @pl.when(pair == 0)
-    def _():
-        total[...] = term
-
-    @pl.when(pair > 0)
-    def _():
-        total[...] += term
-
-    @pl.when(pair == pl.num_programs(0) - 1)
-    def _():
-        near, far = halves_of(z, width)
-        here = rows[target].reshape(block, width).astype(F32)
-        there = rows[rows.shape[0] - 2 + core].reshape(block, width).astype(F32)
-        product = jnp.sum(here * total[:, near] + there * total[:, far])
-        extra = three_way(product, square_ref[0, 0])
-        for peer in range(send_ref.shape[0]):
-            stacked(send_ref, peer, total[peer * 32 : (peer + 1) * 32, :].astype(BF))
-            send_ref[peer, block // 4 :, :] = extra
+        for j, owner in enumerate((core, 1 - core)):
+            source = coupling_ref[target, (chip * 2 + owner) * pairs + pair]
+            vector = rows[source].reshape(block, width)
+            half = jnp.dot(lefts[pair, j], vector, preferred_element_type=F32)
+            halves[pair % 2, :, j * width : (j + 1) * width] = half.astype(BF)
+
+    def second(pair):
+        total[...] += lax.dot_general(
+            halves[pair % 2], rights[pair], (((1,), (1,)), ((), ())), preferred_element_type=F32
+        )
+
+    def both(pair, _):
+        second(pair - 1)
+        first(pair)
+        return 0
+
+    first(0)
+    lax.fori_loop(1, pairs, both, 0)
+    second(pairs - 1)
+
+    near, far = halves_of(z, width)
+    here = rows[target].reshape(block, width).astype(F32)
+    there = rows[rows.shape[0] - 2 + core].reshape(block, width).astype(F32)
+    product = jnp.sum(here * total[:, near] + there * total[:, far])
+    extra = three_way(product, square_ref[0, 0])
+    for peer in range(send_ref.shape[0]):
+        stacked(send_ref, peer, total[peer * 32 : (peer + 1) * 32, :].astype(BF))
+        send_ref[peer, block // 4 :, :] = extra
 
 
 def products(coupling, mine, theirs, left, right, left_other, right_other, square):
     pairs, block, _ = left.shape
     chips, count, share, width = mine.shape
-    operator = pl.BlockSpec((1, block, block), lambda p, c: (p, 0, 0))
-    columns = pl.BlockSpec((1, block, width), lambda p, c: (p, 0, lax.axis_index("sector") % 2))
     return pl.pallas_call(
         product_kernel,
-        grid_spec=pltpu.PrefetchScalarGridSpec(
-            num_scalar_prefetch=1,
-            grid=(pairs,),
-            in_specs=[
-                ANY, ANY, operator, columns, operator, columns,
-                pl.BlockSpec((8, LANES), lambda p, c: (0, 0)),
-            ],
-            out_specs=pl.BlockSpec((chips, block // 4 + 16, LANES), lambda p, c: (0, 0, 0)),
-            scratch_shapes=[
-                pltpu.VMEM((block, block), F32),
-                pltpu.VMEM((count, chips, 2, share, width), BF),
-                pltpu.SemaphoreType.DMA((2 * count,)),
-            ],
-        ),
+        in_specs=[SMEM, VMEM, VMEM, HBM, HBM, HBM, HBM, VMEM],
+        out_specs=VMEM,
+        scratch_shapes=[
+            pltpu.VMEM((block, block), F32),
+            pltpu.VMEM((count, 2 * chips, share, width), BF),
+            pltpu.VMEM((pairs, 2, block, block), BF),
+            pltpu.VMEM((pairs, block, 2 * width), BF),
+            pltpu.VMEM((2, block, 2 * width), BF),
+            pltpu.SemaphoreType.DMA((pairs, 4)),
+        ],
         out_shape=jax.ShapeDtypeStruct((chips, block // 4 + 16, LANES), BF),
-        compiler_params=pltpu.CompilerParams(vmem_limit_bytes=60 << 20),
+        compiler_params=pltpu.CompilerParams(vmem_limit_bytes=28 << 20),
         name="products",
     )(coupling, mine, theirs, left, right, left_other, right_other, square)
 
@@ -269,14 +276,14 @@
     vector_ref[0] = final_ref[...] * lax.rsqrt(total[0:1, 0:1] / entries + 1e-6)
 
 
-def call(kernel, shapes, specs, name, scratch=()):
+def call(kernel, shapes, specs, name, scratch=(), limit=16):
     return pl.pallas_call(
         kernel,
         in_specs=specs,
         out_specs=[VMEM] * len(shapes),
         out_shape=[jax.ShapeDtypeStruct(s, t) for s, t in shapes],
         scratch_shapes=scratch,
-        compiler_params=pltpu.CompilerParams(vmem_limit_bytes=16 << 20),
+        compiler_params=pltpu.CompilerParams(vmem_limit_bytes=limit << 20),
         name=name,
     )
 
@@ -286,6 +293,8 @@
     sectors = lax.axis_size("sector")
     chips = lax.axis_size("op_0") * lax.axis_size("op_1")
     width = block // 2
+    left_blocks = pltpu.with_memory_space_constraint(left_blocks, pltpu.HBM)
+    right_blocks = pltpu.with_memory_space_constraint(right_blocks, pltpu.HBM)
     entries = float(sectors * block * block)
     left_other = other_core(left_blocks)
     right_other = other_core(right_blocks)
@@ -297,6 +306,7 @@
         [((sectors, 3, share, block), BF), ((share, block), F32), scalar],
         [SMEM, VMEM, VMEM],
         "opening",
+        limit=60,
     )(sector_sizes, wavefunction, diagonal)
     begun = swap_all(begin, "sector")
     (outgoing,) = call(spreading_kernel, [spread], [VMEM], "spreading")(begun)

time: 199 us -> 182 us (0.915)
  local copies, waits for them, and re-layouts: 8.31 us -> 0.54 us
  Pallas kernels: 32.2 us -> 25.3 us
    unnamed x26 -> x10, local copies, waits for them, and re-layouts: 7.79 us -> 0.03 us
    pallas_call x2, Pallas kernels: 28 us -> 20.2 us  [products(): pl.pallas_call(product_kernel, in_specs=[SMEM, VMEM, VMEM, HBM, HBM, HBM,...]
  transfers between devices with their start and end apart: 5 -> 5, of which waited for: 3 -> 3; matrix products, arithmetic and copies ran while one was open for 0% -> 0% of each run, Pallas kernels for 0% -> 1%
where the time goes in v3:
time: 182 us; the launch traced here: 181 us
  blocking collectives  132 us (73%)
  Pallas kernels  25.3 us (14%)
  waiting for transfers between devices  12.3 us (7%)
  starting transfers between devices  10.7 us (6%)
    all_to_all x7, blocking collectives, swap_all(): return lax.all_to_all(x, axes, split_axis=0, concat_axis=0, tiled=True)  132 us
    pallas_call x2, Pallas kernels, products(): pl.pallas_call(product_kernel, in_specs=[SMEM, VMEM, VMEM, HBM, HBM, HBM,...  20.2 us
    ppermute x4, starting transfers between devices, other_core(): return lax.ppermute(x, CORE, [(0, 1), (1, 0)])  7.02 us
    all_to_all x1, waiting for transfers between devices, swap_all(): return lax.all_to_all(x, axes, split_axis=0, concat_axis=0, tiled=True)  6.97 us
    ppermute x4, waiting for transfers between devices, other_core(): return lax.ppermute(x, CORE, [(0, 1), (1, 0)])  5.33 us
    all_to_all x1, starting transfers between devices, swap_all(): return lax.all_to_all(x, axes, split_axis=0, concat_axis=0, tiled=True)  3.64 us
  transfers between devices with their start and end apart: 5, of which 3 were waited for; matrix products, arithmetic and copies ran while one was open for 0% of the time, Pallas kernels for 1%

profile of v3, /device:TPU:1, one launch (start us, length us, event | category | flops | bytes accessed | tf_op | source)
XLA Modules:
  0.0 181.3 jit_solution(745618250664381526)
XLA Ops:
  0.6 3.3 %collective-permute-start.1 = (bf16[8,512,512]{2,1,0:T(8,128)(2,1)}, bf16[8,512,512]{2,1,0:T(8,128)(2,1)}, u32[]{:S(2)}, u32[]{:S(2)}) collective-permute-start(bf16[8,512,512]{2,1,0:T(8,128)(2,1)} %left_a.3), channel_id=1, source_target_pairs={{0,1},{1,0},{2,3},{3,2},{4,5},{5,4},{6,7},{7,6},{8,9},{9,8},{10,11... | collective-permute-start | bytes 12582920 | tf_op jit(solution)/shard_map/ppermute | solution.py:28
  3.9 0.1 collective-permute-start.2
  4.0 1.6 opening.1
  5.6 20.3 %all_to_all.40.begun_ref = bf16[8,3,16,512]{3,2,1,0:T(8,128)(2,1)S(1)} all-to-all(bf16[8,3,16,512]{3,2,1,0:T(8,128)(2,1)} %get-tuple-element.13), channel_id=1, replica_groups=mesh['sector'=8,'op_0'=4,'op_1'=4,'op_2'=2] {'sector'}, dimensions={0} | all-to-all | bytes 786432 | tf_op jit(solution)/shard_map/all_to_all | solution.py:24
  25.9 0.1 spreading.1
  26.0 0.0 copy-start.1
  26.0 0.0 copy-start.4
  26.0 24.5 %all_to_all.41.mine_ref = bf16[16,10,16,256]{3,2,1,0:T(8,128)(2,1)S(1)} all-to-all(bf16[16,10,16,256]{3,2,1,0:T(8,128)(2,1)S(1)} %spreading.1), channel_id=1, replica_groups=mesh['sector'=8,'op_0'=4,'op_1'=4,'op_2'=2] {'op_0','op_1'}, dimensions={0} | all-to-all | bytes 2621440 | tf_op jit(solution)/shard_map/all_to_all | solution.py:24
  50.5 3.2 %collective-permute-start = (bf16[16,10,16,256]{3,2,1,0:T(8,128)(2,1)S(1)}, bf16[16,10,16,256]{3,2,1,0:T(8,128)(2,1)S(1)}, u32[]{:S(2)}, u32[]{:S(2)}) collective-permute-start(bf16[16,10,16,256]{3,2,1,0:T(8,128)(2,1)S(1)} %all_to_all.41.mine_ref), channel_id=1, source_target_pairs={{0,1},{1,0},{2,3},{3,2},{4,5},{5,4},{6,7},{7,6},{8,9},{9,8},{10,11... | collective-permute-start | bytes 3932168 | tf_op jit(solution)/shard_map/ppermute | solution.py:28
  53.7 2.7 %collective-permute-done.theirs_ref = bf16[16,10,16,256]{3,2,1,0:T(8,128)(2,1)S(1)} collective-permute-done((bf16[16,10,16,256]{3,2,1,0:T(8,128)(2,1)S(1)}, bf16[16,10,16,256]{3,2,1,0:T(8,128)(2,1)S(1)}, u32[]{:S(2)}, u32[]{:S(2)}) %collective-permute-start) | collective-permute-done | bytes 1310752 | tf_op jit(solution)/shard_map/ppermute | solution.py:28
  56.4 0.0 collective-permute-done.1.left_b
  56.4 0.0 collective-permute-done.2.right_b
  56.4 0.0 copy-done.1
  56.4 0.0 copy-done.4
  56.4 0.0 copy-start.3
  56.4 10.1 %products.2 = bf16[16,144,128]{2,1,0:T(8,128)(2,1)S(1)} custom-call(s32[8,256]{1,0:T(8,128)S(1)} %copy-done.1, bf16[16,10,16,256]{3,2,1,0:T(8,128)(2,1)S(1)} %all_to_all.41.mine_ref, bf16[16,10,16,256]{3,2,1,0:T(8,128)(2,1)S(1)} %collective-permute-done.theirs_ref, bf16[8,512,512]{2,1,0:T(8,128)(2,1)} %left_a.3, bf16[8,512,512]{2,1,0:T(8,128)(2,1)} %right_a.3, ...), custom_call_target="tpu_custom_call" | custom-call | tf_op jit(solution)/shard_map/products/pallas_call | solution.py:178
  66.5 0.0 copy-start
  66.5 0.0 copy-start.2
  66.6 14.1 %all_to_all.42.arrived_ref = bf16[16,144,128]{2,1,0:T(8,128)(2,1)S(1)} all-to-all(bf16[16,144,128]{2,1,0:T(8,128)(2,1)S(1)} %products.2), channel_id=1, replica_groups=mesh['sector'=8,'op_0'=4,'op_1'=4,'op_2'=2] {'op_0','op_1'}, dimensions={0} | all-to-all | bytes 1179648 | tf_op jit(solution)/shard_map/all_to_all | solution.py:24
  80.6 0.0 copy-done.3
  80.6 0.7 joining.2
  81.3 17.4 %all_to_all.43.arrived_ref = bf16[16,80,128]{2,1,0:T(8,128)(2,1)S(1)} all-to-all(bf16[16,80,128]{2,1,0:T(8,128)(2,1)S(1)} %joining.2), channel_id=1, replica_groups=mesh['sector'=8,'op_0'=4,'op_1'=4,'op_2'=2] {'sector','op_2'}, dimensions={0} | all-to-all | bytes 655360 | tf_op jit(solution)/shard_map/all_to_all | solution.py:24
  98.7 0.0 copy-done
  98.7 0.0 copy-done.2
  98.7 0.4 middle.1
  99.1 24.1 %all_to_all.44.mine_ref = bf16[16,10,16,256]{3,2,1,0:T(8,128)(2,1)S(1)} all-to-all(bf16[16,10,16,256]{3,2,1,0:T(8,128)(2,1)S(1)} %get-tuple-element.16), channel_id=1, replica_groups=mesh['sector'=8,'op_0'=4,'op_1'=4,'op_2'=2] {'op_0','op_1'}, dimensions={0} | all-to-all | bytes 2621440 | tf_op jit(solution)/shard_map/all_to_all | solution.py:24
  123.2 0.4 collective-permute-start.3
  123.6 2.7 %collective-permute-done.3.theirs_ref = bf16[16,10,16,256]{3,2,1,0:T(8,128)(2,1)S(1)} collective-permute-done((bf16[16,10,16,256]{3,2,1,0:T(8,128)(2,1)S(1)}, bf16[16,10,16,256]{3,2,1,0:T(8,128)(2,1)S(1)}, u32[]{:S(2)}, u32[]{:S(2)}) %collective-permute-start.3) | collective-permute-done | bytes 1310752 | tf_op jit(solution)/shard_map/ppermute | solution.py:28
  126.2 10.1 %products.3 = bf16[16,144,128]{2,1,0:T(8,128)(2,1)S(1)} custom-call(s32[8,256]{1,0:T(8,128)S(1)} %copy-done.1, bf16[16,10,16,256]{3,2,1,0:T(8,128)(2,1)S(1)} %all_to_all.44.mine_ref, bf16[16,10,16,256]{3,2,1,0:T(8,128)(2,1)S(1)} %collective-permute-done.3.theirs_ref, bf16[8,512,512]{2,1,0:T(8,128)(2,1)} %left_a.3, bf16[8,512,512]{2,1,0:T(8,128)(2,1)} %right_a.3, ...), custom_call_target="tpu_custom_call" | custom-call | tf_op jit(solution)/shard_map/products/pallas_call | solution.py:178
  136.3 14.1 %all_to_all.45.arrived_ref = bf16[16,144,128]{2,1,0:T(8,128)(2,1)S(1)} all-to-all(bf16[16,144,128]{2,1,0:T(8,128)(2,1)S(1)} %products.3), channel_id=1, replica_groups=mesh['sector'=8,'op_0'=4,'op_1'=4,'op_2'=2] {'op_0','op_1'}, dimensions={0} | all-to-all | bytes 1179648 | tf_op jit(solution)/shard_map/all_to_all | solution.py:24
  150.4 0.7 joining.3
  151.1 17.3 %all_to_all.46.arrived_ref = bf16[16,80,128]{2,1,0:T(8,128)(2,1)S(1)} all-to-all(bf16[16,80,128]{2,1,0:T(8,128)(2,1)S(1)} %joining.3), channel_id=1, replica_groups=mesh['sector'=8,'op_0'=4,'op_1'=4,'op_2'=2] {'sector','op_2'}, dimensions={0} | all-to-all | bytes 655360 | tf_op jit(solution)/shard_map/all_to_all | solution.py:24
  168.5 1.0 closing.1
  169.5 3.6 %all-to-all-start.7 = ((f32[32,8,128]{2,1,0:T(8,128)}), f32[32,8,128]{2,1,0:T(8,128)S(1)}, u32[]{:S(2)}, u32[]{:S(2)}) async-start(f32[32,8,128]{2,1,0:T(8,128)} %get-tuple-element.21), calls=%async_computation.7 | async-start | bytes 262144 | tf_op jit(solution)/shard_map/all_to_all | solution.py:24
  173.1 0.5 slice_bitcast_fusion
  173.6 7.0 %all-to-all-done.7.arrived_ref = f32[32,8,128]{2,1,0:T(8,128)S(1)} async-done(((f32[32,8,128]{2,1,0:T(8,128)}), f32[32,8,128]{2,1,0:T(8,128)S(1)}, u32[]{:S(2)}, u32[]{:S(2)}) %all-to-all-start.7) | async-done | bytes 131104 | tf_op jit(solution)/shard_map/all_to_all | solution.py:24
  180.6 0.7 scaling.1
Async XLA Ops:
  0.6 55.8 %collective-permute-start.1 = (bf16[8,512,512]{2,1,0:T(8,128)(2,1)}, bf16[8,512,512]{2,1,0:T(8,128)(2,1)}, u32[]{:S(2)}, u32[]{:S(2)}) collective-permute-start(bf16[8,512,512]{2,1,0:T(8,128)(2,1)} %left_a.3), channel_id=1, source_target_pairs={{0,1},{1,0},{2,3},{3,2},{4,5},{5,4},{6,7},{7,6},{8,9},{9,8},{10,11... | collective-permute-start | bytes 12582920 | tf_op jit(solution)/shard_map/ppermute | solution.py:28
  3.9 52.5 %collective-permute-start.2 = (bf16[8,512,512]{2,1,0:T(8,128)(2,1)}, bf16[8,512,512]{2,1,0:T(8,128)(2,1)}, u32[]{:S(2)}, u32[]{:S(2)}) collective-permute-start(bf16[8,512,512]{2,1,0:T(8,128)(2,1)} %right_a.3), channel_id=1, source_target_pairs={{0,1},{1,0},{2,3},{3,2},{4,5},{5,4},{6,7},{7,6},{8,9},{9,8},{10,11... | collective-permute-start | bytes 12582920 | tf_op jit(solution)/shard_map/ppermute | solution.py:28
  26.0 30.4 %copy-start.1 = (s32[8,256]{1,0:T(8,128)S(1)}, s32[8,256]{1,0:T(8,128)}, u32[]{:S(2)}) copy-start(s32[8,256]{1,0:T(8,128)} %coupling_ref.3) | copy-start | bytes 24580
  26.0 30.4 %copy-start.4 = (f32[8,128]{1,0:T(8,128)S(1)}, f32[8,128]{1,0:T(8,128)}, u32[]{:S(2)}) copy-start(f32[8,128]{1,0:T(8,128)} %get-tuple-element.14.square_ref) | copy-start | bytes 12292
  50.5 5.9 %collective-permute-start = (bf16[16,10,16,256]{3,2,1,0:T(8,128)(2,1)S(1)}, bf16[16,10,16,256]{3,2,1,0:T(8,128)(2,1)S(1)}, u32[]{:S(2)}, u32[]{:S(2)}) collective-permute-start(bf16[16,10,16,256]{3,2,1,0:T(8,128)(2,1)S(1)} %all_to_all.41.mine_ref), channel_id=1, source_target_pairs={{0,1},{1,0},{2,3},{3,2},{4,5},{5,4},{6,7},{7,6},{8,9},{9,8},{10,11... | collective-permute-start | bytes 3932168 | tf_op jit(solution)/shard_map/ppermute | solution.py:28
  56.4 24.2 %copy-start.3 = (s32[8]{0:T(128)S(1)}, s32[8]{0:T(128)}, u32[]{:S(2)}) copy-start(s32[8]{0:T(128)} %sizes_ref.5) | copy-start | bytes 100
  66.5 32.2 %copy-start = (f32[1,16,512]{2,1,0:T(8,128)S(1)}, f32[1,16,512]{2,1,0:T(8,128)}, u32[]{:S(2)}) copy-start(f32[1,16,512]{2,1,0:T(8,128)} %diag_ref.5) | copy-start | bytes 98308
  66.5 32.2 %copy-start.2 = (f32[16,512]{1,0:T(8,128)S(1)}, f32[16,512]{1,0:T(8,128)}, u32[]{:S(2)}) copy-start(f32[16,512]{1,0:T(8,128)} %get-tuple-element.15.current_ref) | copy-start | bytes 98308
  123.2 3.1 %collective-permute-start.3 = (bf16[16,10,16,256]{3,2,1,0:T(8,128)(2,1)S(1)}, bf16[16,10,16,256]{3,2,1,0:T(8,128)(2,1)S(1)}, u32[]{:S(2)}, u32[]{:S(2)}) collective-permute-start(bf16[16,10,16,256]{3,2,1,0:T(8,128)(2,1)S(1)} %all_to_all.44.mine_ref), channel_id=1, source_target_pairs={{0,1},{1,0},{2,3},{3,2},{4,5},{5,4},{6,7},{7,6},{8,9},{9,8},{10,11... | collective-permute-start | bytes 3932168 | tf_op jit(solution)/shard_map/ppermute | solution.py:28
  169.5 11.1 %all-to-all-start.7 = ((f32[32,8,128]{2,1,0:T(8,128)}), f32[32,8,128]{2,1,0:T(8,128)S(1)}, u32[]{:S(2)}, u32[]{:S(2)}) async-start(f32[32,8,128]{2,1,0:T(8,128)} %get-tuple-element.21), calls=%async_computation.7 | async-start | bytes 262144 | tf_op jit(solution)/shard_map/all_to_all | solution.py:24

commit v4 on v3

--- a/solution.py
+++ b/solution.py
@@ -18,6 +18,7 @@
 HBM = pl.BlockSpec(memory_space=pltpu.HBM)
 SHARE = 16
 LANES = 128
+AHEAD = 3
 
 
 def swap_all(x, axes):
@@ -109,30 +110,35 @@
 
 
 def product_kernel(
-    coupling_ref, mine_ref, theirs_ref, left_a, right_a, left_b, right_b, square_ref,
+    coupling_ref, mine_ref, theirs_ref, left_a, left_b, right_a, right_b, square_ref,
     send_ref, total, rows, lefts, rights, halves, sems,
 ):
     z, chip, core = place()
     target = (z // 2) * 2 + core
     block, width = total.shape[0], rows.shape[-1]
     pairs = left_a.shape[0]
-    cut, _ = halves_of(z, width)
-
-    def operators(pair):
+    near, far = halves_of(z, width)
+
+    def fetches(pair):
         return [
-            pltpu.make_async_copy(left_a.at[pair], lefts.at[pair, 0], sems.at[pair, 0]),
-            pltpu.make_async_copy(left_b.at[pair], lefts.at[pair, 1], sems.at[pair, 1]),
             pltpu.make_async_copy(
-                right_a.at[pair, :, cut], rights.at[pair, :, :width], sems.at[pair, 2]
-            ),
-            pltpu.make_async_copy(
-                right_b.at[pair, :, cut], rights.at[pair, :, width:], sems.at[pair, 3]
-            ),
-        ]
-
-    for pair in range(pairs):
-        for copy in operators(pair):
+                right.at[pair, :, near], rights.at[pair, :, side], sems.at[pair, j]
+            )
+            for j, (right, side) in enumerate(
+                ((right_a, slice(0, width)), (right_b, slice(width, 2 * width)))
+            )
+        ] + [pltpu.make_async_copy(left_b.at[pair], lefts.at[pair], sems.at[pair, 2])]
+
+    def fetch(pair):
+        for copy in fetches(pair):
             copy.start()
+
+    def fetched(pair):
+        for copy in fetches(pair):
+            copy.wait()
+
+    for pair in range(AHEAD):
+        fetch(pair)
     for k in range(rows.shape[0]):
         for at in range(mine_ref.shape[0]):
             rows[k, 2 * at + core] = mine_ref[at, k]
@@ -140,12 +146,10 @@
     total[...] = jnp.zeros_like(total)
 
     def first(pair):
-        for copy in operators(pair):
-            copy.wait()
-        for j, owner in enumerate((core, 1 - core)):
+        for j, (owner, left) in enumerate(((core, left_a), (1 - core, lefts))):
             source = coupling_ref[target, (chip * 2 + owner) * pairs + pair]
             vector = rows[source].reshape(block, width)
-            half = jnp.dot(lefts[pair, j], vector, preferred_element_type=F32)
+            half = jnp.dot(left[pair], vector, preferred_element_type=F32)
             halves[pair % 2, :, j * width : (j + 1) * width] = half.astype(BF)
 
     def second(pair):
@@ -154,15 +158,22 @@
         )
 
     def both(pair, _):
+        fetched(pair)
+
+        @pl.when(pair + AHEAD < pairs)
+        def _():
+            fetch(pair + AHEAD)
+
         second(pair - 1)
         first(pair)
         return 0
 
+    fetched(0)
+    fetch(AHEAD)
     first(0)
     lax.fori_loop(1, pairs, both, 0)
     second(pairs - 1)
 
-    near, far = halves_of(z, width)
     here = rows[target].reshape(block, width).astype(F32)
     there = rows[rows.shape[0] - 2 + core].reshape(block, width).astype(F32)
     product = jnp.sum(here * total[:, near] + there * total[:, far])
@@ -177,20 +188,20 @@
     chips, count, share, width = mine.shape
     return pl.pallas_call(
         product_kernel,
-        in_specs=[SMEM, VMEM, VMEM, HBM, HBM, HBM, HBM, VMEM],
+        in_specs=[SMEM, VMEM, VMEM, VMEM, HBM, HBM, HBM, VMEM],
         out_specs=VMEM,
         scratch_shapes=[
             pltpu.VMEM((block, block), F32),
             pltpu.VMEM((count, 2 * chips, share, width), BF),
-            pltpu.VMEM((pairs, 2, block, block), BF),
+            pltpu.VMEM((pairs, block, block), BF),
             pltpu.VMEM((pairs, block, 2 * width), BF),
             pltpu.VMEM((2, block, 2 * width), BF),
-            pltpu.SemaphoreType.DMA((pairs, 4)),
+            pltpu.SemaphoreType.DMA((pairs, 3)),
         ],
         out_shape=jax.ShapeDtypeStruct((chips, block // 4 + 16, LANES), BF),
         compiler_params=pltpu.CompilerParams(vmem_limit_bytes=28 << 20),
         name="products",
-    )(coupling, mine, theirs, left, right, left_other, right_other, square)
+    )(coupling, mine, theirs, left, left_other, right, right_other, square)
 
 
 def joining_kernel(sizes_ref, arrived_ref, send_ref):
@@ -293,7 +304,6 @@
     sectors = lax.axis_size("sector")
     chips = lax.axis_size("op_0") * lax.axis_size("op_1")
     width = block // 2
-    left_blocks = pltpu.with_memory_space_constraint(left_blocks, pltpu.HBM)
     right_blocks = pltpu.with_memory_space_constraint(right_blocks, pltpu.HBM)
     entries = float(sectors * block * block)
     left_other = other_core(left_blocks)

time: 182 us -> 180 us (0.989)
  Pallas kernels: 25.3 us -> 22.9 us
    pallas_call x2, Pallas kernels: 20.2 us -> 17.8 us  [products(): pl.pallas_call(product_kernel, in_specs=[SMEM, VMEM, VMEM, VMEM, HBM, HBM...]
where the time goes in v4:
time: 180 us; the launch traced here: 179 us
  blocking collectives  132 us (73%)
  Pallas kernels  22.9 us (13%)
  waiting for transfers between devices  12.3 us (7%)
  starting transfers between devices  10.6 us (6%)
    all_to_all x7, blocking collectives, swap_all(): return lax.all_to_all(x, axes, split_axis=0, concat_axis=0, tiled=True)  132 us
    pallas_call x2, Pallas kernels, products(): pl.pallas_call(product_kernel, in_specs=[SMEM, VMEM, VMEM, VMEM, HBM, HBM...  17.8 us
    ppermute x4, starting transfers between devices, other_core(): return lax.ppermute(x, CORE, [(0, 1), (1, 0)])  7.02 us
    all_to_all x1, waiting for transfers between devices, swap_all(): return lax.all_to_all(x, axes, split_axis=0, concat_axis=0, tiled=True)  6.99 us
    ppermute x4, waiting for transfers between devices, other_core(): return lax.ppermute(x, CORE, [(0, 1), (1, 0)])  5.33 us
    all_to_all x1, starting transfers between devices, swap_all(): return lax.all_to_all(x, axes, split_axis=0, concat_axis=0, tiled=True)  3.62 us
  transfers between devices with their start and end apart: 5, of which 3 were waited for; matrix products, arithmetic and copies ran while one was open for 0% of the time, Pallas kernels for 1%

profile of v4, /device:TPU:1, one launch (start us, length us, event | category | flops | bytes accessed | tf_op | source)
XLA Modules:
  0.0 179.1 jit_solution(2247048008426752821)
XLA Ops:
  0.6 3.3 %collective-permute-start.1 = (bf16[8,512,512]{2,1,0:T(8,128)(2,1)}, bf16[8,512,512]{2,1,0:T(8,128)(2,1)}, u32[]{:S(2)}, u32[]{:S(2)}) collective-permute-start(bf16[8,512,512]{2,1,0:T(8,128)(2,1)} %left_a.3), channel_id=1, source_target_pairs={{0,1},{1,0},{2,3},{3,2},{4,5},{5,4},{6,7},{7,6},{8,9},{9,8},{10,11... | collective-permute-start | bytes 12582920 | tf_op jit(solution)/shard_map/ppermute | solution.py:29
  3.9 0.1 collective-permute-start.2
  4.0 1.6 opening.1
  5.6 20.3 %all_to_all.40.begun_ref = bf16[8,3,16,512]{3,2,1,0:T(8,128)(2,1)S(1)} all-to-all(bf16[8,3,16,512]{3,2,1,0:T(8,128)(2,1)} %get-tuple-element.13), channel_id=1, replica_groups=mesh['sector'=8,'op_0'=4,'op_1'=4,'op_2'=2] {'sector'}, dimensions={0} | all-to-all | bytes 786432 | tf_op jit(solution)/shard_map/all_to_all | solution.py:25
  25.9 0.0 copy-start
  25.9 0.1 spreading.1
  26.0 0.0 copy-start.2
  26.0 0.0 copy-start.5
  26.0 24.7 %all_to_all.41.mine_ref = bf16[16,10,16,256]{3,2,1,0:T(8,128)(2,1)S(1)} all-to-all(bf16[16,10,16,256]{3,2,1,0:T(8,128)(2,1)S(1)} %spreading.1), channel_id=1, replica_groups=mesh['sector'=8,'op_0'=4,'op_1'=4,'op_2'=2] {'op_0','op_1'}, dimensions={0} | all-to-all | bytes 2621440 | tf_op jit(solution)/shard_map/all_to_all | solution.py:25
  50.8 3.2 %collective-permute-start = (bf16[16,10,16,256]{3,2,1,0:T(8,128)(2,1)S(1)}, bf16[16,10,16,256]{3,2,1,0:T(8,128)(2,1)S(1)}, u32[]{:S(2)}, u32[]{:S(2)}) collective-permute-start(bf16[16,10,16,256]{3,2,1,0:T(8,128)(2,1)S(1)} %all_to_all.41.mine_ref), channel_id=1, source_target_pairs={{0,1},{1,0},{2,3},{3,2},{4,5},{5,4},{6,7},{7,6},{8,9},{9,8},{10,11... | collective-permute-start | bytes 3932168 | tf_op jit(solution)/shard_map/ppermute | solution.py:29
  54.0 2.7 %collective-permute-done.theirs_ref = bf16[16,10,16,256]{3,2,1,0:T(8,128)(2,1)S(1)} collective-permute-done((bf16[16,10,16,256]{3,2,1,0:T(8,128)(2,1)S(1)}, bf16[16,10,16,256]{3,2,1,0:T(8,128)(2,1)S(1)}, u32[]{:S(2)}, u32[]{:S(2)}) %collective-permute-start) | collective-permute-done | bytes 1310752 | tf_op jit(solution)/shard_map/ppermute | solution.py:29
  56.7 0.0 collective-permute-done.1.left_b
  56.7 0.0 collective-permute-done.2.right_b
  56.7 0.0 copy-done
  56.7 0.0 copy-done.2
  56.7 0.0 copy-done.5
  56.7 0.0 copy-start.4
  56.7 8.9 %products.2 = bf16[16,144,128]{2,1,0:T(8,128)(2,1)S(1)} custom-call(s32[8,256]{1,0:T(8,128)S(1)} %copy-done.2, bf16[16,10,16,256]{3,2,1,0:T(8,128)(2,1)S(1)} %all_to_all.41.mine_ref, bf16[16,10,16,256]{3,2,1,0:T(8,128)(2,1)S(1)} %collective-permute-done.theirs_ref, bf16[8,512,512]{2,1,0:T(8,128)(2,1)S(1)} %copy-done, ...), custom_call_target="tpu_custom_call" | custom-call | tf_op jit(solution)/shard_map/products/pallas_call | solution.py:189
  65.6 0.0 copy-start.1
  65.6 0.0 copy-start.3
  65.6 14.1 %all_to_all.42.arrived_ref = bf16[16,144,128]{2,1,0:T(8,128)(2,1)S(1)} all-to-all(bf16[16,144,128]{2,1,0:T(8,128)(2,1)S(1)} %products.2), channel_id=1, replica_groups=mesh['sector'=8,'op_0'=4,'op_1'=4,'op_2'=2] {'op_0','op_1'}, dimensions={0} | all-to-all | bytes 1179648 | tf_op jit(solution)/shard_map/all_to_all | solution.py:25
  79.7 0.0 copy-done.4
  79.7 0.7 joining.2
  80.3 17.4 %all_to_all.43.arrived_ref = bf16[16,80,128]{2,1,0:T(8,128)(2,1)S(1)} all-to-all(bf16[16,80,128]{2,1,0:T(8,128)(2,1)S(1)} %joining.2), channel_id=1, replica_groups=mesh['sector'=8,'op_0'=4,'op_1'=4,'op_2'=2] {'sector','op_2'}, dimensions={0} | all-to-all | bytes 655360 | tf_op jit(solution)/shard_map/all_to_all | solution.py:25
  97.7 0.0 copy-done.1
  97.7 0.0 copy-done.3
  97.8 0.4 middle.1
  98.1 24.1 %all_to_all.44.mine_ref = bf16[16,10,16,256]{3,2,1,0:T(8,128)(2,1)S(1)} all-to-all(bf16[16,10,16,256]{3,2,1,0:T(8,128)(2,1)S(1)} %get-tuple-element.16), channel_id=1, replica_groups=mesh['sector'=8,'op_0'=4,'op_1'=4,'op_2'=2] {'op_0','op_1'}, dimensions={0} | all-to-all | bytes 2621440 | tf_op jit(solution)/shard_map/all_to_all | solution.py:25
  122.2 0.4 collective-permute-start.3
  122.6 2.7 %collective-permute-done.3.theirs_ref = bf16[16,10,16,256]{3,2,1,0:T(8,128)(2,1)S(1)} collective-permute-done((bf16[16,10,16,256]{3,2,1,0:T(8,128)(2,1)S(1)}, bf16[16,10,16,256]{3,2,1,0:T(8,128)(2,1)S(1)}, u32[]{:S(2)}, u32[]{:S(2)}) %collective-permute-start.3) | collective-permute-done | bytes 1310752 | tf_op jit(solution)/shard_map/ppermute | solution.py:29
  125.3 8.9 %products.3 = bf16[16,144,128]{2,1,0:T(8,128)(2,1)S(1)} custom-call(s32[8,256]{1,0:T(8,128)S(1)} %copy-done.2, bf16[16,10,16,256]{3,2,1,0:T(8,128)(2,1)S(1)} %all_to_all.44.mine_ref, bf16[16,10,16,256]{3,2,1,0:T(8,128)(2,1)S(1)} %collective-permute-done.3.theirs_ref, bf16[8,512,512]{2,1,0:T(8,128)(2,1)S(1)} %copy-done, ...), custom_call_target="tpu_custom_call" | custom-call | tf_op jit(solution)/shard_map/products/pallas_call | solution.py:189
  134.2 14.1 %all_to_all.45.arrived_ref = bf16[16,144,128]{2,1,0:T(8,128)(2,1)S(1)} all-to-all(bf16[16,144,128]{2,1,0:T(8,128)(2,1)S(1)} %products.3), channel_id=1, replica_groups=mesh['sector'=8,'op_0'=4,'op_1'=4,'op_2'=2] {'op_0','op_1'}, dimensions={0} | all-to-all | bytes 1179648 | tf_op jit(solution)/shard_map/all_to_all | solution.py:25
  148.3 0.7 joining.3
  149.0 17.3 %all_to_all.46.arrived_ref = bf16[16,80,128]{2,1,0:T(8,128)(2,1)S(1)} all-to-all(bf16[16,80,128]{2,1,0:T(8,128)(2,1)S(1)} %joining.3), channel_id=1, replica_groups=mesh['sector'=8,'op_0'=4,'op_1'=4,'op_2'=2] {'sector','op_2'}, dimensions={0} | all-to-all | bytes 655360 | tf_op jit(solution)/shard_map/all_to_all | solution.py:25
  166.3 1.0 closing.1
  167.3 3.6 %all-to-all-start.7 = ((f32[32,8,128]{2,1,0:T(8,128)}), f32[32,8,128]{2,1,0:T(8,128)S(1)}, u32[]{:S(2)}, u32[]{:S(2)}) async-start(f32[32,8,128]{2,1,0:T(8,128)} %get-tuple-element.21), calls=%async_computation.7 | async-start | bytes 262144 | tf_op jit(solution)/shard_map/all_to_all | solution.py:25
  170.9 0.5 slice_bitcast_fusion
  171.5 7.0 %all-to-all-done.7.arrived_ref = f32[32,8,128]{2,1,0:T(8,128)S(1)} async-done(((f32[32,8,128]{2,1,0:T(8,128)}), f32[32,8,128]{2,1,0:T(8,128)S(1)}, u32[]{:S(2)}, u32[]{:S(2)}) %all-to-all-start.7) | async-done | bytes 131104 | tf_op jit(solution)/shard_map/all_to_all | solution.py:25
  178.5 0.7 scaling.1
Async XLA Ops:
  0.6 56.0 %collective-permute-start.1 = (bf16[8,512,512]{2,1,0:T(8,128)(2,1)}, bf16[8,512,512]{2,1,0:T(8,128)(2,1)}, u32[]{:S(2)}, u32[]{:S(2)}) collective-permute-start(bf16[8,512,512]{2,1,0:T(8,128)(2,1)} %left_a.3), channel_id=1, source_target_pairs={{0,1},{1,0},{2,3},{3,2},{4,5},{5,4},{6,7},{7,6},{8,9},{9,8},{10,11... | collective-permute-start | bytes 12582920 | tf_op jit(solution)/shard_map/ppermute | solution.py:29
  3.9 52.7 %collective-permute-start.2 = (bf16[8,512,512]{2,1,0:T(8,128)(2,1)}, bf16[8,512,512]{2,1,0:T(8,128)(2,1)}, u32[]{:S(2)}, u32[]{:S(2)}) collective-permute-start(bf16[8,512,512]{2,1,0:T(8,128)(2,1)} %right_a.3), channel_id=1, source_target_pairs={{0,1},{1,0},{2,3},{3,2},{4,5},{5,4},{6,7},{7,6},{8,9},{9,8},{10,11... | collective-permute-start | bytes 12582920 | tf_op jit(solution)/shard_map/ppermute | solution.py:29
  25.9 30.8 %copy-start = (bf16[8,512,512]{2,1,0:T(8,128)(2,1)S(1)}, bf16[8,512,512]{2,1,0:T(8,128)(2,1)}, u32[]{:S(2)}) copy-start(bf16[8,512,512]{2,1,0:T(8,128)(2,1)} %left_a.3) | copy-start | bytes 12582916
  26.0 30.7 %copy-start.2 = (s32[8,256]{1,0:T(8,128)S(1)}, s32[8,256]{1,0:T(8,128)}, u32[]{:S(2)}) copy-start(s32[8,256]{1,0:T(8,128)} %coupling_ref.3) | copy-start | bytes 24580
  26.0 30.7 %copy-start.5 = (f32[8,128]{1,0:T(8,128)S(1)}, f32[8,128]{1,0:T(8,128)}, u32[]{:S(2)}) copy-start(f32[8,128]{1,0:T(8,128)} %get-tuple-element.14.square_ref) | copy-start | bytes 12292
  50.8 5.9 %collective-permute-start = (bf16[16,10,16,256]{3,2,1,0:T(8,128)(2,1)S(1)}, bf16[16,10,16,256]{3,2,1,0:T(8,128)(2,1)S(1)}, u32[]{:S(2)}, u32[]{:S(2)}) collective-permute-start(bf16[16,10,16,256]{3,2,1,0:T(8,128)(2,1)S(1)} %all_to_all.41.mine_ref), channel_id=1, source_target_pairs={{0,1},{1,0},{2,3},{3,2},{4,5},{5,4},{6,7},{7,6},{8,9},{9,8},{10,11... | collective-permute-start | bytes 3932168 | tf_op jit(solution)/shard_map/ppermute | solution.py:29
  56.7 23.0 %copy-start.4 = (s32[8]{0:T(128)S(1)}, s32[8]{0:T(128)}, u32[]{:S(2)}) copy-start(s32[8]{0:T(128)} %sizes_ref.5) | copy-start | bytes 100
  65.6 32.2 %copy-start.1 = (f32[1,16,512]{2,1,0:T(8,128)S(1)}, f32[1,16,512]{2,1,0:T(8,128)}, u32[]{:S(2)}) copy-start(f32[1,16,512]{2,1,0:T(8,128)} %diag_ref.5) | copy-start | bytes 98308
  65.6 32.2 %copy-start.3 = (f32[16,512]{1,0:T(8,128)S(1)}, f32[16,512]{1,0:T(8,128)}, u32[]{:S(2)}) copy-start(f32[16,512]{1,0:T(8,128)} %get-tuple-element.15.current_ref) | copy-start | bytes 98308
  122.2 3.1 %collective-permute-start.3 = (bf16[16,10,16,256]{3,2,1,0:T(8,128)(2,1)S(1)}, bf16[16,10,16,256]{3,2,1,0:T(8,128)(2,1)S(1)}, u32[]{:S(2)}, u32[]{:S(2)}) collective-permute-start(bf16[16,10,16,256]{3,2,1,0:T(8,128)(2,1)S(1)} %all_to_all.44.mine_ref), channel_id=1, source_target_pairs={{0,1},{1,0},{2,3},{3,2},{4,5},{5,4},{6,7},{7,6},{8,9},{9,8},{10,11... | collective-permute-start | bytes 3932168 | tf_op jit(solution)/shard_map/ppermute | solution.py:29
  167.3 11.1 %all-to-all-start.7 = ((f32[32,8,128]{2,1,0:T(8,128)}), f32[32,8,128]{2,1,0:T(8,128)S(1)}, u32[]{:S(2)}, u32[]{:S(2)}) async-start(f32[32,8,128]{2,1,0:T(8,128)} %get-tuple-element.21), calls=%async_computation.7 | async-start | bytes 262144 | tf_op jit(solution)/shard_map/all_to_all | solution.py:25

commit v5 on v4

--- a/solution.py
+++ b/solution.py
@@ -18,7 +18,6 @@
 HBM = pl.BlockSpec(memory_space=pltpu.HBM)
 SHARE = 16
 LANES = 128
-AHEAD = 3
 
 
 def swap_all(x, axes):
@@ -111,7 +110,7 @@
 
 def product_kernel(
     coupling_ref, mine_ref, theirs_ref, left_a, left_b, right_a, right_b, square_ref,
-    send_ref, total, rows, lefts, rights, halves, sems,
+    send_ref, total, rows, rights, halves, sems,
 ):
     z, chip, core = place()
     target = (z // 2) * 2 + core
@@ -119,26 +118,11 @@
     pairs = left_a.shape[0]
     near, far = halves_of(z, width)
 
-    def fetches(pair):
-        return [
-            pltpu.make_async_copy(
-                right.at[pair, :, near], rights.at[pair, :, side], sems.at[pair, j]
-            )
-            for j, (right, side) in enumerate(
-                ((right_a, slice(0, width)), (right_b, slice(width, 2 * width)))
-            )
-        ] + [pltpu.make_async_copy(left_b.at[pair], lefts.at[pair], sems.at[pair, 2])]
-
     def fetch(pair):
-        for copy in fetches(pair):
-            copy.start()
-
-    def fetched(pair):
-        for copy in fetches(pair):
-            copy.wait()
-
-    for pair in range(AHEAD):
-        fetch(pair)
+        return pltpu.make_async_copy(right_a.at[pair, :, near], rights.at[pair], sems.at[pair])
+
+    for pair in range(pairs):
+        fetch(pair).start()
     for k in range(rows.shape[0]):
         for at in range(mine_ref.shape[0]):
             rows[k, 2 * at + core] = mine_ref[at, k]
@@ -146,32 +130,27 @@
     total[...] = jnp.zeros_like(total)
 
     def first(pair):
-        for j, (owner, left) in enumerate(((core, left_a), (1 - core, lefts))):
+        for j, (owner, left) in enumerate(((core, left_a), (1 - core, left_b))):
             source = coupling_ref[target, (chip * 2 + owner) * pairs + pair]
             vector = rows[source].reshape(block, width)
             half = jnp.dot(left[pair], vector, preferred_element_type=F32)
             halves[pair % 2, :, j * width : (j + 1) * width] = half.astype(BF)
 
     def second(pair):
+        right = jnp.concatenate([rights[pair], right_b[pair, :, near]], axis=1)
         total[...] += lax.dot_general(
-            halves[pair % 2], rights[pair], (((1,), (1,)), ((), ())), preferred_element_type=F32
+            halves[pair % 2], right, (((1,), (1,)), ((), ())), preferred_element_type=F32
         )
 
     def both(pair, _):
-        fetched(pair)
-
-        @pl.when(pair + AHEAD < pairs)
-        def _():
-            fetch(pair + AHEAD)
-
+        fetch(pair - 1).wait()
         second(pair - 1)
         first(pair)
         return 0
 
-    fetched(0)
-    fetch(AHEAD)
     first(0)
     lax.fori_loop(1, pairs, both, 0)
+    fetch(pairs - 1).wait()
     second(pairs - 1)
 
     here = rows[target].reshape(block, width).astype(F32)
@@ -188,18 +167,17 @@
     chips, count, share, width = mine.shape
     return pl.pallas_call(
         product_kernel,
-        in_specs=[SMEM, VMEM, VMEM, VMEM, HBM, HBM, HBM, VMEM],
+        in_specs=[SMEM, VMEM, VMEM, VMEM, VMEM, HBM, VMEM, VMEM],
         out_specs=VMEM,
         scratch_shapes=[
             pltpu.VMEM((block, block), F32),
             pltpu.VMEM((count, 2 * chips, share, width), BF),
-            pltpu.VMEM((pairs, block, block), BF),
-            pltpu.VMEM((pairs, block, 2 * width), BF),
+            pltpu.VMEM((pairs, block, width), BF),
             pltpu.VMEM((2, block, 2 * width), BF),
-            pltpu.SemaphoreType.DMA((pairs, 3)),
+            pltpu.SemaphoreType.DMA((pairs,)),
         ],
         out_shape=jax.ShapeDtypeStruct((chips, block // 4 + 16, LANES), BF),
-        compiler_params=pltpu.CompilerParams(vmem_limit_bytes=28 << 20),
+        compiler_params=pltpu.CompilerParams(vmem_limit_bytes=16 << 20),
         name="products",
     )(coupling, mine, theirs, left, left_other, right, right_other, square)
 
@@ -304,10 +282,13 @@
     sectors = lax.axis_size("sector")
     chips = lax.axis_size("op_0") * lax.axis_size("op_1")
     width = block // 2
-    right_blocks = pltpu.with_memory_space_constraint(right_blocks, pltpu.HBM)
-    entries = float(sectors * block * block)
     left_other = other_core(left_blocks)
     right_other = other_core(right_blocks)
+    wavefunction, diagonal, sector_sizes, right_blocks = (
+        pltpu.with_memory_space_constraint(x, pltpu.HBM)
+        for x in (wavefunction, diagonal, sector_sizes, right_blocks)
+    )
+    entries = float(sectors * block * block)
     spread = ((chips, sectors + 2, share, width), BF)
     scalar = ((8, LANES), F32)
 
@@ -316,7 +297,6 @@
         [((sectors, 3, share, block), BF), ((share, block), F32), scalar],
         [SMEM, VMEM, VMEM],
         "opening",
-        limit=60,
     )(sector_sizes, wavefunction, diagonal)
     begun = swap_all(begin, "sector")
     (outgoing,) = call(spreading_kernel, [spread], [VMEM], "spreading")(begun)

time: 180 us -> 180 us (level)
  no operation moved by 1% of the time
where the time goes in v5:
time: 180 us; the launch traced here: 179 us
  blocking collectives  132 us (73%)
  Pallas kernels  23.3 us (13%)
  waiting for transfers between devices  12.3 us (7%)
  starting transfers between devices  10.7 us (6%)
    all_to_all x7, blocking collectives, swap_all(): return lax.all_to_all(x, axes, split_axis=0, concat_axis=0, tiled=True)  132 us
    pallas_call x2, Pallas kernels, products(): pl.pallas_call(product_kernel, in_specs=[SMEM, VMEM, VMEM, VMEM, VMEM, HB...  17 us
    ppermute x4, starting transfers between devices, other_core(): return lax.ppermute(x, CORE, [(0, 1), (1, 0)])  7.02 us
    all_to_all x1, waiting for transfers between devices, swap_all(): return lax.all_to_all(x, axes, split_axis=0, concat_axis=0, tiled=True)  6.98 us
    ppermute x4, waiting for transfers between devices, other_core(): return lax.ppermute(x, CORE, [(0, 1), (1, 0)])  5.33 us
    all_to_all x1, starting transfers between devices, swap_all(): return lax.all_to_all(x, axes, split_axis=0, concat_axis=0, tiled=True)  3.63 us
  transfers between devices with their start and end apart: 5, of which 3 were waited for; matrix products, arithmetic and copies ran while one was open for 0% of the time, Pallas kernels for 1%

profile of v5, /device:TPU:1, one launch (start us, length us, event | category | flops | bytes accessed | tf_op | source)
XLA Modules:
  0.0 179.2 jit_solution(2478426664465809166)
XLA Ops:
  0.6 3.3 %collective-permute-start.1 = (bf16[8,512,512]{2,1,0:T(8,128)(2,1)}, bf16[8,512,512]{2,1,0:T(8,128)(2,1)S(1)}, u32[]{:S(2)}, u32[]{:S(2)}) collective-permute-start(bf16[8,512,512]{2,1,0:T(8,128)(2,1)} %left_a.3), channel_id=1, source_target_pairs={{0,1},{1,0},{2,3},{3,2},{4,5},{5,4},{6,7},{7,6},{8,9},{9,8},{10,11... | collective-permute-start | bytes 12582920 | tf_op jit(solution)/shard_map/ppermute | solution.py:28
  3.9 0.1 collective-permute-start.2
  4.0 0.9 opening.1
  5.0 20.1 %all_to_all.40.begun_ref = bf16[8,3,16,512]{3,2,1,0:T(8,128)(2,1)S(1)} all-to-all(bf16[8,3,16,512]{3,2,1,0:T(8,128)(2,1)S(1)} %get-tuple-element.13), channel_id=1, replica_groups=mesh['sector'=8,'op_0'=4,'op_1'=4,'op_2'=2] {'sector'}, dimensions={0} | all-to-all | bytes 786432 | tf_op jit(solution)/shard_map/all_to_all | solution.py:24
  25.0 0.0 copy-start
  25.0 0.1 spreading.1
  25.1 0.0 copy-start.1
  25.2 24.7 %all_to_all.41.mine_ref = bf16[16,10,16,256]{3,2,1,0:T(8,128)(2,1)S(1)} all-to-all(bf16[16,10,16,256]{3,2,1,0:T(8,128)(2,1)S(1)} %spreading.1), channel_id=1, replica_groups=mesh['sector'=8,'op_0'=4,'op_1'=4,'op_2'=2] {'op_0','op_1'}, dimensions={0} | all-to-all | bytes 2621440 | tf_op jit(solution)/shard_map/all_to_all | solution.py:24
  49.9 3.2 %collective-permute-start = (bf16[16,10,16,256]{3,2,1,0:T(8,128)(2,1)S(1)}, bf16[16,10,16,256]{3,2,1,0:T(8,128)(2,1)S(1)}, u32[]{:S(2)}, u32[]{:S(2)}) collective-permute-start(bf16[16,10,16,256]{3,2,1,0:T(8,128)(2,1)S(1)} %all_to_all.41.mine_ref), channel_id=1, source_target_pairs={{0,1},{1,0},{2,3},{3,2},{4,5},{5,4},{6,7},{7,6},{8,9},{9,8},{10,11... | collective-permute-start | bytes 3932168 | tf_op jit(solution)/shard_map/ppermute | solution.py:28
  53.1 2.7 %collective-permute-done.theirs_ref = bf16[16,10,16,256]{3,2,1,0:T(8,128)(2,1)S(1)} collective-permute-done((bf16[16,10,16,256]{3,2,1,0:T(8,128)(2,1)S(1)}, bf16[16,10,16,256]{3,2,1,0:T(8,128)(2,1)S(1)}, u32[]{:S(2)}, u32[]{:S(2)}) %collective-permute-start) | collective-permute-done | bytes 1310752 | tf_op jit(solution)/shard_map/ppermute | solution.py:28
  55.8 0.0 collective-permute-done.1.left_b
  55.8 0.0 collective-permute-done.2.right_b
  55.8 0.0 copy-done
  55.8 0.0 copy-done.1
  55.8 8.5 %products.2 = bf16[16,144,128]{2,1,0:T(8,128)(2,1)S(1)} custom-call(s32[8,256]{1,0:T(8,128)S(1)} %copy-done.1, bf16[16,10,16,256]{3,2,1,0:T(8,128)(2,1)S(1)} %all_to_all.41.mine_ref, bf16[16,10,16,256]{3,2,1,0:T(8,128)(2,1)S(1)} %collective-permute-done.theirs_ref, bf16[8,512,512]{2,1,0:T(8,128)(2,1)S(1)} %copy-done, ...), custom_call_target="tpu_custom_call" | custom-call | tf_op jit(solution)/shard_map/products/pallas_call | solution.py:168
  64.3 14.1 %all_to_all.42.arrived_ref = bf16[16,144,128]{2,1,0:T(8,128)(2,1)S(1)} all-to-all(bf16[16,144,128]{2,1,0:T(8,128)(2,1)S(1)} %products.2), channel_id=1, replica_groups=mesh['sector'=8,'op_0'=4,'op_1'=4,'op_2'=2] {'op_0','op_1'}, dimensions={0} | all-to-all | bytes 1179648 | tf_op jit(solution)/shard_map/all_to_all | solution.py:24
  78.4 0.8 joining.2
  79.2 17.4 %all_to_all.43.arrived_ref = bf16[16,80,128]{2,1,0:T(8,128)(2,1)S(1)} all-to-all(bf16[16,80,128]{2,1,0:T(8,128)(2,1)S(1)} %joining.2), channel_id=1, replica_groups=mesh['sector'=8,'op_0'=4,'op_1'=4,'op_2'=2] {'sector','op_2'}, dimensions={0} | all-to-all | bytes 655360 | tf_op jit(solution)/shard_map/all_to_all | solution.py:24
  96.6 1.1 middle.1
  97.7 24.1 %all_to_all.44.mine_ref = bf16[16,10,16,256]{3,2,1,0:T(8,128)(2,1)S(1)} all-to-all(bf16[16,10,16,256]{3,2,1,0:T(8,128)(2,1)S(1)} %get-tuple-element.16), channel_id=1, replica_groups=mesh['sector'=8,'op_0'=4,'op_1'=4,'op_2'=2] {'op_0','op_1'}, dimensions={0} | all-to-all | bytes 2621440 | tf_op jit(solution)/shard_map/all_to_all | solution.py:24
  121.8 0.4 collective-permute-start.3
  122.2 2.7 %collective-permute-done.3.theirs_ref = bf16[16,10,16,256]{3,2,1,0:T(8,128)(2,1)S(1)} collective-permute-done((bf16[16,10,16,256]{3,2,1,0:T(8,128)(2,1)S(1)}, bf16[16,10,16,256]{3,2,1,0:T(8,128)(2,1)S(1)}, u32[]{:S(2)}, u32[]{:S(2)}) %collective-permute-start.3) | collective-permute-done | bytes 1310752 | tf_op jit(solution)/shard_map/ppermute | solution.py:28
  124.9 8.5 %products.3 = bf16[16,144,128]{2,1,0:T(8,128)(2,1)S(1)} custom-call(s32[8,256]{1,0:T(8,128)S(1)} %copy-done.1, bf16[16,10,16,256]{3,2,1,0:T(8,128)(2,1)S(1)} %all_to_all.44.mine_ref, bf16[16,10,16,256]{3,2,1,0:T(8,128)(2,1)S(1)} %collective-permute-done.3.theirs_ref, bf16[8,512,512]{2,1,0:T(8,128)(2,1)S(1)} %copy-done, ...), custom_call_target="tpu_custom_call" | custom-call | tf_op jit(solution)/shard_map/products/pallas_call | solution.py:168
  133.4 14.1 %all_to_all.45.arrived_ref = bf16[16,144,128]{2,1,0:T(8,128)(2,1)S(1)} all-to-all(bf16[16,144,128]{2,1,0:T(8,128)(2,1)S(1)} %products.3), channel_id=1, replica_groups=mesh['sector'=8,'op_0'=4,'op_1'=4,'op_2'=2] {'op_0','op_1'}, dimensions={0} | all-to-all | bytes 1179648 | tf_op jit(solution)/shard_map/all_to_all | solution.py:24
  147.5 0.8 joining.3
  148.3 17.3 %all_to_all.46.arrived_ref = bf16[16,80,128]{2,1,0:T(8,128)(2,1)S(1)} all-to-all(bf16[16,80,128]{2,1,0:T(8,128)(2,1)S(1)} %joining.3), channel_id=1, replica_groups=mesh['sector'=8,'op_0'=4,'op_1'=4,'op_2'=2] {'sector','op_2'}, dimensions={0} | all-to-all | bytes 655360 | tf_op jit(solution)/shard_map/all_to_all | solution.py:24
  165.7 1.7 closing.1
  167.4 3.6 %all-to-all-start.7 = ((f32[32,8,128]{2,1,0:T(8,128)}), f32[32,8,128]{2,1,0:T(8,128)S(1)}, u32[]{:S(2)}, u32[]{:S(2)}) async-start(f32[32,8,128]{2,1,0:T(8,128)} %get-tuple-element.21), calls=%async_computation.7 | async-start | bytes 262144 | tf_op jit(solution)/shard_map/all_to_all | solution.py:24
  171.1 0.5 slice_bitcast_fusion
  171.6 7.0 %all-to-all-done.7.arrived_ref = f32[32,8,128]{2,1,0:T(8,128)S(1)} async-done(((f32[32,8,128]{2,1,0:T(8,128)}), f32[32,8,128]{2,1,0:T(8,128)S(1)}, u32[]{:S(2)}, u32[]{:S(2)}) %all-to-all-start.7) | async-done | bytes 131104 | tf_op jit(solution)/shard_map/all_to_all | solution.py:24
  178.5 0.7 scaling.1
Async XLA Ops:
  0.6 55.2 %collective-permute-start.1 = (bf16[8,512,512]{2,1,0:T(8,128)(2,1)}, bf16[8,512,512]{2,1,0:T(8,128)(2,1)S(1)}, u32[]{:S(2)}, u32[]{:S(2)}) collective-permute-start(bf16[8,512,512]{2,1,0:T(8,128)(2,1)} %left_a.3), channel_id=1, source_target_pairs={{0,1},{1,0},{2,3},{3,2},{4,5},{5,4},{6,7},{7,6},{8,9},{9,8},{10,11... | collective-permute-start | bytes 12582920 | tf_op jit(solution)/shard_map/ppermute | solution.py:28
  3.9 51.9 %collective-permute-start.2 = (bf16[8,512,512]{2,1,0:T(8,128)(2,1)}, bf16[8,512,512]{2,1,0:T(8,128)(2,1)S(1)}, u32[]{:S(2)}, u32[]{:S(2)}) collective-permute-start(bf16[8,512,512]{2,1,0:T(8,128)(2,1)} %right_a.3), channel_id=1, source_target_pairs={{0,1},{1,0},{2,3},{3,2},{4,5},{5,4},{6,7},{7,6},{8,9},{9,8},{10,11... | collective-permute-start | bytes 12582920 | tf_op jit(solution)/shard_map/ppermute | solution.py:28
  25.0 30.8 %copy-start = (bf16[8,512,512]{2,1,0:T(8,128)(2,1)S(1)}, bf16[8,512,512]{2,1,0:T(8,128)(2,1)}, u32[]{:S(2)}) copy-start(bf16[8,512,512]{2,1,0:T(8,128)(2,1)} %left_a.3) | copy-start | bytes 12582916
  25.1 30.6 %copy-start.1 = (s32[8,256]{1,0:T(8,128)S(1)}, s32[8,256]{1,0:T(8,128)}, u32[]{:S(2)}) copy-start(s32[8,256]{1,0:T(8,128)} %coupling_ref.3) | copy-start | bytes 24580
  49.9 5.9 %collective-permute-start = (bf16[16,10,16,256]{3,2,1,0:T(8,128)(2,1)S(1)}, bf16[16,10,16,256]{3,2,1,0:T(8,128)(2,1)S(1)}, u32[]{:S(2)}, u32[]{:S(2)}) collective-permute-start(bf16[16,10,16,256]{3,2,1,0:T(8,128)(2,1)S(1)} %all_to_all.41.mine_ref), channel_id=1, source_target_pairs={{0,1},{1,0},{2,3},{3,2},{4,5},{5,4},{6,7},{7,6},{8,9},{9,8},{10,11... | collective-permute-start | bytes 3932168 | tf_op jit(solution)/shard_map/ppermute | solution.py:28
  121.8 3.1 %collective-permute-start.3 = (bf16[16,10,16,256]{3,2,1,0:T(8,128)(2,1)S(1)}, bf16[16,10,16,256]{3,2,1,0:T(8,128)(2,1)S(1)}, u32[]{:S(2)}, u32[]{:S(2)}) collective-permute-start(bf16[16,10,16,256]{3,2,1,0:T(8,128)(2,1)S(1)} %all_to_all.44.mine_ref), channel_id=1, source_target_pairs={{0,1},{1,0},{2,3},{3,2},{4,5},{5,4},{6,7},{7,6},{8,9},{9,8},{10,11... | collective-permute-start | bytes 3932168 | tf_op jit(solution)/shard_map/ppermute | solution.py:28
  167.4 11.1 %all-to-all-start.7 = ((f32[32,8,128]{2,1,0:T(8,128)}), f32[32,8,128]{2,1,0:T(8,128)S(1)}, u32[]{:S(2)}, u32[]{:S(2)}) async-start(f32[32,8,128]{2,1,0:T(8,128)} %get-tuple-element.21), calls=%async_computation.7 | async-start | bytes 262144 | tf_op jit(solution)/shard_map/all_to_all | solution.py:24

commit v6 on v5

--- a/solution.py
+++ b/solution.py
@@ -18,6 +18,7 @@
 HBM = pl.BlockSpec(memory_space=pltpu.HBM)
 SHARE = 16
 LANES = 128
+TILE = 8
 
 
 def swap_all(x, axes):
@@ -29,7 +30,7 @@
 
 
 def three_way(first, second):
-    row = lax.broadcasted_iota(jnp.int32, (16, 128), 0)
+    row = lax.broadcasted_iota(jnp.int32, (TILE, LANES), 0)
     value = jnp.where(row < 3, first, second)
     high = value.astype(BF).astype(F32)
     middle = (value - high).astype(BF).astype(F32)
@@ -121,12 +122,13 @@
     def fetch(pair):
         return pltpu.make_async_copy(right_a.at[pair, :, near], rights.at[pair], sems.at[pair])
 
-    for pair in range(pairs):
-        fetch(pair).start()
+    fetch(0).start()
     for k in range(rows.shape[0]):
         for at in range(mine_ref.shape[0]):
             rows[k, 2 * at + core] = mine_ref[at, k]
             rows[k, 2 * at + 1 - core] = theirs_ref[at, k]
+    for pair in range(1, pairs):
+        fetch(pair).start()
     total[...] = jnp.zeros_like(total)
 
     def first(pair):
@@ -176,7 +178,7 @@
             pltpu.VMEM((2, block, 2 * width), BF),
             pltpu.SemaphoreType.DMA((pairs,)),
         ],
-        out_shape=jax.ShapeDtypeStruct((chips, block // 4 + 16, LANES), BF),
+        out_shape=jax.ShapeDtypeStruct((chips, block // 4 + TILE, LANES), BF),
         compiler_params=pltpu.CompilerParams(vmem_limit_bytes=16 << 20),
         name="products",
     )(coupling, mine, theirs, left, left_other, right, right_other, square)
@@ -187,7 +189,7 @@
     total = arrived_ref[0].astype(F32)
     for peer in range(1, arrived_ref.shape[0]):
         total = total + arrived_ref[peer].astype(F32)
-    end = total.shape[0] - 16
+    end = total.shape[0] - TILE
     sigma = unstacked(total[:end], 32)
     inside = live(sigma.shape, chip * 32, sizes_ref[(z // 2) * 2 + core])
     low = jnp.where(inside, sigma, 0.0).astype(BF)
@@ -199,7 +201,7 @@
 
 
 def scalars_of(arrived_ref):
-    at = arrived_ref.shape[1] - 16
+    at = arrived_ref.shape[1] - TILE
     total = arrived_ref[0, at:].astype(F32)
     for peer in range(1, arrived_ref.shape[0]):
         total = total + arrived_ref[peer, at:].astype(F32)
@@ -207,7 +209,7 @@
 
 
 def sigma_of(arrived_ref, target):
-    end = arrived_ref.shape[1] - 16
+    end = arrived_ref.shape[1] - TILE
     at = (target // 2) * 4 + target % 2
     both = arrived_ref[at, :end].astype(F32) + arrived_ref[at + 2, :end].astype(F32)
     return unstacked(both, SHARE)
@@ -225,7 +227,7 @@
     z, _, _ = place()
     first, second = scalars_of(arrived_ref)
     theta = first / (second + 1e-6)
-    theta_ref[...] = jnp.broadcast_to(theta, (8, LANES))
+    theta_ref[0] = theta[0, 0]
     for k in range(all_ref.shape[0]):
         diag = begun_ref[k, 1].astype(F32) + begun_ref[k, 2].astype(F32)
         update = corrected(begun_ref[k, 0].astype(F32), sigma_of(arrived_ref, k), diag, theta)
@@ -246,8 +248,8 @@
     scale = lax.rsqrt(second / entries + 1e-6)
     squared = scale * scale
     theta = squared * first / (squared * second + 1e-6)
-    lane = lax.broadcasted_iota(jnp.int32, (8, LANES), 1)
-    theta_ref[...] = jnp.where(lane == 0, before_ref[...], theta)
+    theta_ref[0] = before_ref[0]
+    theta_ref[1] = theta[0, 0]
     total = jnp.zeros(all_ref.shape[1:], F32)
     for k in range(all_ref.shape[0]):
         diag = begun_ref[k, 1].astype(F32) + begun_ref[k, 2].astype(F32)
@@ -265,14 +267,14 @@
     vector_ref[0] = final_ref[...] * lax.rsqrt(total[0:1, 0:1] / entries + 1e-6)
 
 
-def call(kernel, shapes, specs, name, scratch=(), limit=16):
+def call(kernel, shapes, specs, name, scratch=(), outs=None):
     return pl.pallas_call(
         kernel,
         in_specs=specs,
-        out_specs=[VMEM] * len(shapes),
+        out_specs=outs or [VMEM] * len(shapes),
         out_shape=[jax.ShapeDtypeStruct(s, t) for s, t in shapes],
         scratch_shapes=scratch,
-        compiler_params=pltpu.CompilerParams(vmem_limit_bytes=limit << 20),
+        compiler_params=pltpu.CompilerParams(vmem_limit_bytes=16 << 20),
         name=name,
     )
 
@@ -284,10 +286,11 @@
     width = block // 2
     left_other = other_core(left_blocks)
     right_other = other_core(right_blocks)
-    wavefunction, diagonal, sector_sizes, right_blocks = (
+    opening_inputs = tuple(
         pltpu.with_memory_space_constraint(x, pltpu.HBM)
-        for x in (wavefunction, diagonal, sector_sizes, right_blocks)
-    )
+        for x in (sector_sizes, wavefunction, diagonal)
+    )
+    right_blocks = pltpu.with_memory_space_constraint(right_blocks, pltpu.HBM)
     entries = float(sectors * block * block)
     spread = ((chips, sectors + 2, share, width), BF)
     scalar = ((8, LANES), F32)
@@ -297,7 +300,7 @@
         [((sectors, 3, share, block), BF), ((share, block), F32), scalar],
         [SMEM, VMEM, VMEM],
         "opening",
-    )(sector_sizes, wavefunction, diagonal)
+    )(*opening_inputs)
     begun = swap_all(begin, "sector")
     (outgoing,) = call(spreading_kernel, [spread], [VMEM], "spreading")(begun)
 
@@ -309,7 +312,7 @@
         )
         (send,) = call(
             joining_kernel,
-            [((sectors * 2, block // 8 + 16, LANES), BF)],
+            [((sectors * 2, block // 8 + TILE, LANES), BF)],
             [SMEM, VMEM],
             "joining",
         )(sector_sizes, swap_all(send, CHIP))
@@ -318,18 +321,20 @@
     arrived = sigma_step(outgoing, square)
     outgoing, everyone, own, square, theta = call(
         middle_kernel,
-        [spread, ((sectors, share, block), F32), ((share, block), F32), scalar, scalar],
+        [spread, ((sectors, share, block), F32), ((share, block), F32), scalar, ((1,), F32)],
         [VMEM] * 4,
         "middle",
         [pltpu.VMEM((sectors, share, block), BF)],
+        [VMEM, VMEM, VMEM, VMEM, SMEM],
     )(arrived, begun, current, diagonal)
 
     arrived = sigma_step(outgoing, square)
     final, send, thetas = call(
         functools.partial(closing_kernel, entries),
-        [((share, block), F32), ((chips * 2, 8, LANES), F32), scalar],
-        [VMEM] * 6,
+        [((share, block), F32), ((chips * 2, 8, LANES), F32), ((2,), F32)],
+        [VMEM, VMEM, VMEM, VMEM, VMEM, SMEM],
         "closing",
+        outs=[VMEM, VMEM, SMEM],
     )(arrived, begun, everyone, own, diagonal, theta)
     (vector,) = call(
         functools.partial(scaling_kernel, entries),
@@ -337,7 +342,7 @@
         [VMEM] * 2,
         "scaling",
     )(swap_all(send, OP), final)
-    return vector, thetas[0, :2]
+    return vector, thetas
 
 
 def solution(mesh):

time: 180 us -> 177 us (0.983)
  blocking collectives: 132 us -> 141 us
  waiting for transfers between devices: 12.3 us -> 5.33 us
  starting transfers between devices: 10.7 us -> 7.04 us
    all_to_all x7 -> x8, blocking collectives: 132 us -> 141 us  [swap_all(): return lax.all_to_all(x, axes, split_axis=0, concat_axis=0, tiled=True)]
    all_to_all x1 -> x0, waiting for transfers between devices: 6.98 us -> none  [swap_all(): return lax.all_to_all(x, axes, split_axis=0, concat_axis=0, tiled=True)]
    all_to_all x1 -> x0, starting transfers between devices: 3.63 us -> none  [swap_all(): return lax.all_to_all(x, axes, split_axis=0, concat_axis=0, tiled=True)]
  transfers between devices with their start and end apart: 5 -> 4, of which waited for: 3 -> 2; matrix products, arithmetic and copies ran while one was open for 0% -> 0% of each run, Pallas kernels for 1% -> 1%
where the time goes in v6:
time: 177 us; the launch traced here: 176 us
  blocking collectives  141 us (80%)
  Pallas kernels  22 us (12%)
  starting transfers between devices  7.04 us (4%)
  waiting for transfers between devices  5.33 us (3%)
    all_to_all x8, blocking collectives, swap_all(): return lax.all_to_all(x, axes, split_axis=0, concat_axis=0, tiled=True)  141 us
    pallas_call x2, Pallas kernels, products(): pl.pallas_call(product_kernel, in_specs=[SMEM, VMEM, VMEM, VMEM, VMEM, HB...  16.9 us
    ppermute x4, starting transfers between devices, other_core(): return lax.ppermute(x, CORE, [(0, 1), (1, 0)])  7.04 us
    ppermute x4, waiting for transfers between devices, other_core(): return lax.ppermute(x, CORE, [(0, 1), (1, 0)])  5.33 us
  transfers between devices with their start and end apart: 4, of which 2 were waited for; matrix products, arithmetic and copies ran while one was open for 0% of the time, Pallas kernels for 1%

profile of v6, /device:TPU:1, one launch (start us, length us, event | category | flops | bytes accessed | tf_op | source)
XLA Modules:
  0.0 176.1 jit_solution(16880024440307284280)
XLA Ops:
  0.6 3.3 %collective-permute-start.1 = (bf16[8,512,512]{2,1,0:T(8,128)(2,1)}, bf16[8,512,512]{2,1,0:T(8,128)(2,1)S(1)}, u32[]{:S(2)}, u32[]{:S(2)}) collective-permute-start(bf16[8,512,512]{2,1,0:T(8,128)(2,1)} %left_a.3), channel_id=1, source_target_pairs={{0,1},{1,0},{2,3},{3,2},{4,5},{5,4},{6,7},{7,6},{8,9},{9,8},{10,11... | collective-permute-start | bytes 12582920 | tf_op jit(solution)/shard_map/ppermute | solution.py:29
  3.9 0.1 collective-permute-start.2
  4.0 0.9 opening.1
  5.0 20.1 %all_to_all.40.begun_ref = bf16[8,3,16,512]{3,2,1,0:T(8,128)(2,1)S(1)} all-to-all(bf16[8,3,16,512]{3,2,1,0:T(8,128)(2,1)S(1)} %get-tuple-element.13), channel_id=1, replica_groups=mesh['sector'=8,'op_0'=4,'op_1'=4,'op_2'=2] {'sector'}, dimensions={0} | all-to-all | bytes 786432 | tf_op jit(solution)/shard_map/all_to_all | solution.py:25
  25.0 0.0 copy-start
  25.0 0.1 spreading.1
  25.1 0.0 copy-start.2
  25.2 24.7 %all_to_all.41.mine_ref = bf16[16,10,16,256]{3,2,1,0:T(8,128)(2,1)S(1)} all-to-all(bf16[16,10,16,256]{3,2,1,0:T(8,128)(2,1)S(1)} %spreading.1), channel_id=1, replica_groups=mesh['sector'=8,'op_0'=4,'op_1'=4,'op_2'=2] {'op_0','op_1'}, dimensions={0} | all-to-all | bytes 2621440 | tf_op jit(solution)/shard_map/all_to_all | solution.py:25
  49.9 3.2 %collective-permute-start = (bf16[16,10,16,256]{3,2,1,0:T(8,128)(2,1)S(1)}, bf16[16,10,16,256]{3,2,1,0:T(8,128)(2,1)S(1)}, u32[]{:S(2)}, u32[]{:S(2)}) collective-permute-start(bf16[16,10,16,256]{3,2,1,0:T(8,128)(2,1)S(1)} %all_to_all.41.mine_ref), channel_id=1, source_target_pairs={{0,1},{1,0},{2,3},{3,2},{4,5},{5,4},{6,7},{7,6},{8,9},{9,8},{10,11... | collective-permute-start | bytes 3932168 | tf_op jit(solution)/shard_map/ppermute | solution.py:29
  53.1 2.7 %collective-permute-done.theirs_ref = bf16[16,10,16,256]{3,2,1,0:T(8,128)(2,1)S(1)} collective-permute-done((bf16[16,10,16,256]{3,2,1,0:T(8,128)(2,1)S(1)}, bf16[16,10,16,256]{3,2,1,0:T(8,128)(2,1)S(1)}, u32[]{:S(2)}, u32[]{:S(2)}) %collective-permute-start) | collective-permute-done | bytes 1310752 | tf_op jit(solution)/shard_map/ppermute | solution.py:29
  55.8 0.0 collective-permute-done.1.left_b
  55.8 0.0 collective-permute-done.2.right_b
  55.8 0.0 copy-done
  55.8 0.0 copy-done.2
  55.8 0.0 copy-start.3
  55.8 8.5 %products.2 = bf16[16,136,128]{2,1,0:T(8,128)(2,1)S(1)} custom-call(s32[8,256]{1,0:T(8,128)S(1)} %copy-done.2, bf16[16,10,16,256]{3,2,1,0:T(8,128)(2,1)S(1)} %all_to_all.41.mine_ref, bf16[16,10,16,256]{3,2,1,0:T(8,128)(2,1)S(1)} %collective-permute-done.theirs_ref, bf16[8,512,512]{2,1,0:T(8,128)(2,1)S(1)} %copy-done, ...), custom_call_target="tpu_custom_call" | custom-call | tf_op jit(solution)/shard_map/products/pallas_call | solution.py:170
  64.3 0.0 copy-start.1
  64.3 13.8 %all_to_all.42.arrived_ref = bf16[16,136,128]{2,1,0:T(8,128)(2,1)S(1)} all-to-all(bf16[16,136,128]{2,1,0:T(8,128)(2,1)S(1)} %products.2), channel_id=1, replica_groups=mesh['sector'=8,'op_0'=4,'op_1'=4,'op_2'=2] {'op_0','op_1'}, dimensions={0} | all-to-all | bytes 1114112 | tf_op jit(solution)/shard_map/all_to_all | solution.py:25
  78.1 0.0 copy-done.3
  78.1 0.7 joining.2
  78.8 16.8 %all_to_all.43.arrived_ref = bf16[16,72,128]{2,1,0:T(8,128)(2,1)S(1)} all-to-all(bf16[16,72,128]{2,1,0:T(8,128)(2,1)S(1)} %joining.2), channel_id=1, replica_groups=mesh['sector'=8,'op_0'=4,'op_1'=4,'op_2'=2] {'sector','op_2'}, dimensions={0} | all-to-all | bytes 589824 | tf_op jit(solution)/shard_map/all_to_all | solution.py:25
  95.6 0.0 copy-done.1
  95.6 0.6 middle.1
  96.2 24.2 %all_to_all.44.mine_ref = bf16[16,10,16,256]{3,2,1,0:T(8,128)(2,1)S(1)} all-to-all(bf16[16,10,16,256]{3,2,1,0:T(8,128)(2,1)S(1)} %get-tuple-element.16), channel_id=1, replica_groups=mesh['sector'=8,'op_0'=4,'op_1'=4,'op_2'=2] {'op_0','op_1'}, dimensions={0} | all-to-all | bytes 2621440 | tf_op jit(solution)/shard_map/all_to_all | solution.py:25
  120.4 0.4 collective-permute-start.3
  120.8 2.7 %collective-permute-done.3.theirs_ref = bf16[16,10,16,256]{3,2,1,0:T(8,128)(2,1)S(1)} collective-permute-done((bf16[16,10,16,256]{3,2,1,0:T(8,128)(2,1)S(1)}, bf16[16,10,16,256]{3,2,1,0:T(8,128)(2,1)S(1)}, u32[]{:S(2)}, u32[]{:S(2)}) %collective-permute-start.3) | collective-permute-done | bytes 1310752 | tf_op jit(solution)/shard_map/ppermute | solution.py:29
  123.4 8.5 %products.3 = bf16[16,136,128]{2,1,0:T(8,128)(2,1)S(1)} custom-call(s32[8,256]{1,0:T(8,128)S(1)} %copy-done.2, bf16[16,10,16,256]{3,2,1,0:T(8,128)(2,1)S(1)} %all_to_all.44.mine_ref, bf16[16,10,16,256]{3,2,1,0:T(8,128)(2,1)S(1)} %collective-permute-done.3.theirs_ref, bf16[8,512,512]{2,1,0:T(8,128)(2,1)S(1)} %copy-done, ...), custom_call_target="tpu_custom_call" | custom-call | tf_op jit(solution)/shard_map/products/pallas_call | solution.py:170
  131.9 13.8 %all_to_all.45.arrived_ref = bf16[16,136,128]{2,1,0:T(8,128)(2,1)S(1)} all-to-all(bf16[16,136,128]{2,1,0:T(8,128)(2,1)S(1)} %products.3), channel_id=1, replica_groups=mesh['sector'=8,'op_0'=4,'op_1'=4,'op_2'=2] {'op_0','op_1'}, dimensions={0} | all-to-all | bytes 1114112 | tf_op jit(solution)/shard_map/all_to_all | solution.py:25
  145.7 0.7 joining.3
  146.4 16.8 %all_to_all.46.arrived_ref = bf16[16,72,128]{2,1,0:T(8,128)(2,1)S(1)} all-to-all(bf16[16,72,128]{2,1,0:T(8,128)(2,1)S(1)} %joining.3), channel_id=1, replica_groups=mesh['sector'=8,'op_0'=4,'op_1'=4,'op_2'=2] {'sector','op_2'}, dimensions={0} | all-to-all | bytes 589824 | tf_op jit(solution)/shard_map/all_to_all | solution.py:25
  163.2 1.3 closing.1
  164.5 10.9 %all_to_all.47.arrived_ref = f32[32,8,128]{2,1,0:T(8,128)S(1)} all-to-all(f32[32,8,128]{2,1,0:T(8,128)S(1)} %get-tuple-element.21), channel_id=1, replica_groups=mesh['sector'=8,'op_0'=4,'op_1'=4,'op_2'=2] {'op_0','op_1','op_2'}, dimensions={0} | all-to-all | bytes 262144 | tf_op jit(solution)/shard_map/all_to_all | solution.py:25
  175.4 0.7 scaling.1
Async XLA Ops:
  0.6 55.2 %collective-permute-start.1 = (bf16[8,512,512]{2,1,0:T(8,128)(2,1)}, bf16[8,512,512]{2,1,0:T(8,128)(2,1)S(1)}, u32[]{:S(2)}, u32[]{:S(2)}) collective-permute-start(bf16[8,512,512]{2,1,0:T(8,128)(2,1)} %left_a.3), channel_id=1, source_target_pairs={{0,1},{1,0},{2,3},{3,2},{4,5},{5,4},{6,7},{7,6},{8,9},{9,8},{10,11... | collective-permute-start | bytes 12582920 | tf_op jit(solution)/shard_map/ppermute | solution.py:29
  3.9 51.9 %collective-permute-start.2 = (bf16[8,512,512]{2,1,0:T(8,128)(2,1)}, bf16[8,512,512]{2,1,0:T(8,128)(2,1)S(1)}, u32[]{:S(2)}, u32[]{:S(2)}) collective-permute-start(bf16[8,512,512]{2,1,0:T(8,128)(2,1)} %right_a.3), channel_id=1, source_target_pairs={{0,1},{1,0},{2,3},{3,2},{4,5},{5,4},{6,7},{7,6},{8,9},{9,8},{10,11... | collective-permute-start | bytes 12582920 | tf_op jit(solution)/shard_map/ppermute | solution.py:29
  25.0 30.8 %copy-start = (bf16[8,512,512]{2,1,0:T(8,128)(2,1)S(1)}, bf16[8,512,512]{2,1,0:T(8,128)(2,1)}, u32[]{:S(2)}) copy-start(bf16[8,512,512]{2,1,0:T(8,128)(2,1)} %left_a.3) | copy-start | bytes 12582916
  25.1 30.6 %copy-start.2 = (s32[8,256]{1,0:T(8,128)S(1)}, s32[8,256]{1,0:T(8,128)}, u32[]{:S(2)}) copy-start(s32[8,256]{1,0:T(8,128)} %coupling_ref.3) | copy-start | bytes 24580
  49.9 5.9 %collective-permute-start = (bf16[16,10,16,256]{3,2,1,0:T(8,128)(2,1)S(1)}, bf16[16,10,16,256]{3,2,1,0:T(8,128)(2,1)S(1)}, u32[]{:S(2)}, u32[]{:S(2)}) collective-permute-start(bf16[16,10,16,256]{3,2,1,0:T(8,128)(2,1)S(1)} %all_to_all.41.mine_ref), channel_id=1, source_target_pairs={{0,1},{1,0},{2,3},{3,2},{4,5},{5,4},{6,7},{7,6},{8,9},{9,8},{10,11... | collective-permute-start | bytes 3932168 | tf_op jit(solution)/shard_map/ppermute | solution.py:29
  55.8 22.3 %copy-start.3 = (s32[8]{0:T(128)S(1)}, s32[8]{0:T(128)}, u32[]{:S(2)}) copy-start(s32[8]{0:T(128)} %sizes_ref.5) | copy-start | bytes 100
  64.3 31.3 %copy-start.1 = (f32[1,16,512]{2,1,0:T(8,128)S(1)}, f32[1,16,512]{2,1,0:T(8,128)}, u32[]{:S(2)}) copy-start(f32[1,16,512]{2,1,0:T(8,128)} %diag_ref.5) | copy-start | bytes 98308
  120.4 3.1 %collective-permute-start.3 = (bf16[16,10,16,256]{3,2,1,0:T(8,128)(2,1)S(1)}, bf16[16,10,16,256]{3,2,1,0:T(8,128)(2,1)S(1)}, u32[]{:S(2)}, u32[]{:S(2)}) collective-permute-start(bf16[16,10,16,256]{3,2,1,0:T(8,128)(2,1)S(1)} %all_to_all.44.mine_ref), channel_id=1, source_target_pairs={{0,1},{1,0},{2,3},{3,2},{4,5},{5,4},{6,7},{7,6},{8,9},{9,8},{10,11... | collective-permute-start | bytes 3932168 | tf_op jit(solution)/shard_map/ppermute | solution.py:29

commit v7 on v6

--- a/solution.py
+++ b/solution.py
@@ -19,6 +19,8 @@
 SHARE = 16
 LANES = 128
 TILE = 8
+LAG = 2
+LAG1 = LAG + 1
 
 
 def swap_all(x, axes):
@@ -120,15 +122,24 @@
     near, far = halves_of(z, width)
 
     def fetch(pair):
-        return pltpu.make_async_copy(right_a.at[pair, :, near], rights.at[pair], sems.at[pair])
+        return pltpu.make_async_copy(
+            right_a.at[pair, :, near], rights.at[pair, :, :width], sems.at[pair, 0]
+        )
+
+    def move(pair):
+        return pltpu.make_async_copy(
+            right_b.at[pair, :, near], rights.at[pair, :, width:], sems.at[pair, 1]
+        )
 
     fetch(0).start()
+    move(0).start()
     for k in range(rows.shape[0]):
         for at in range(mine_ref.shape[0]):
             rows[k, 2 * at + core] = mine_ref[at, k]
             rows[k, 2 * at + 1 - core] = theirs_ref[at, k]
     for pair in range(1, pairs):
         fetch(pair).start()
+        move(pair).start()
     total[...] = jnp.zeros_like(total)
 
     def first(pair):
@@ -136,24 +147,28 @@
             source = coupling_ref[target, (chip * 2 + owner) * pairs + pair]
             vector = rows[source].reshape(block, width)
             half = jnp.dot(left[pair], vector, preferred_element_type=F32)
-            halves[pair % 2, :, j * width : (j + 1) * width] = half.astype(BF)
+            halves[pair % LAG1, :, j * width : (j + 1) * width] = half.astype(BF)
 
     def second(pair):
-        right = jnp.concatenate([rights[pair], right_b[pair, :, near]], axis=1)
         total[...] += lax.dot_general(
-            halves[pair % 2], right, (((1,), (1,)), ((), ())), preferred_element_type=F32
+            halves[pair % LAG1], rights[pair], (((1,), (1,)), ((), ())), preferred_element_type=F32
         )
 
     def both(pair, _):
-        fetch(pair - 1).wait()
-        second(pair - 1)
+        fetch(pair - LAG).wait()
+        move(pair - LAG).wait()
+        second(pair - LAG)
         first(pair)
         return 0
 
-    first(0)
-    lax.fori_loop(1, pairs, both, 0)
-    fetch(pairs - 1).wait()
-    second(pairs - 1)
+    for pair in range(LAG):
+        first(pair)
+    lax.fori_loop(LAG, pairs, both, 0)
+    for pair in range(pairs - LAG, pairs):
+        fetch(pair).wait()
+        move(pair).wait()
+    for pair in range(pairs - LAG, pairs):
+        second(pair)
 
     here = rows[target].reshape(block, width).astype(F32)
     there = rows[rows.shape[0] - 2 + core].reshape(block, width).astype(F32)
@@ -174,12 +189,12 @@
         scratch_shapes=[
             pltpu.VMEM((block, block), F32),
             pltpu.VMEM((count, 2 * chips, share, width), BF),
-            pltpu.VMEM((pairs, block, width), BF),
-            pltpu.VMEM((2, block, 2 * width), BF),
-            pltpu.SemaphoreType.DMA((pairs,)),
+            pltpu.VMEM((pairs, block, 2 * width), BF),
+            pltpu.VMEM((LAG1, block, 2 * width), BF),
+            pltpu.SemaphoreType.DMA((pairs, 2)),
         ],
         out_shape=jax.ShapeDtypeStruct((chips, block // 4 + TILE, LANES), BF),
-        compiler_params=pltpu.CompilerParams(vmem_limit_bytes=16 << 20),
+        compiler_params=pltpu.CompilerParams(vmem_limit_bytes=18 << 20),
         name="products",
     )(coupling, mine, theirs, left, left_other, right, right_other, square)
 

time: 177 us -> 175 us (0.989)
  no operation moved by 1% of the time
where the time goes in v7:
time: 175 us; the launch traced here: 174 us
  blocking collectives  141 us (81%)
  Pallas kernels  20.4 us (12%)
  starting transfers between devices  7.04 us (4%)
  waiting for transfers between devices  5.33 us (3%)
    all_to_all x8, blocking collectives, swap_all(): return lax.all_to_all(x, axes, split_axis=0, concat_axis=0, tiled=True)  141 us
    pallas_call x2, Pallas kernels, products(): pl.pallas_call(product_kernel, in_specs=[SMEM, VMEM, VMEM, VMEM, VMEM, HB...  15.4 us
    ppermute x4, starting transfers between devices, other_core(): return lax.ppermute(x, CORE, [(0, 1), (1, 0)])  7.04 us
    ppermute x4, waiting for transfers between devices, other_core(): return lax.ppermute(x, CORE, [(0, 1), (1, 0)])  5.33 us
  transfers between devices with their start and end apart: 4, of which 2 were waited for; matrix products, arithmetic and copies ran while one was open for 0% of the time, Pallas kernels for 1%

profile of v7, /device:TPU:1, one launch (start us, length us, event | category | flops | bytes accessed | tf_op | source)
XLA Modules:
  0.0 174.5 jit_solution(11317122596420402974)
XLA Ops:
  0.6 3.3 %collective-permute-start.1 = (bf16[8,512,512]{2,1,0:T(8,128)(2,1)}, bf16[8,512,512]{2,1,0:T(8,128)(2,1)S(1)}, u32[]{:S(2)}, u32[]{:S(2)}) collective-permute-start(bf16[8,512,512]{2,1,0:T(8,128)(2,1)} %left_a.3), channel_id=1, source_target_pairs={{0,1},{1,0},{2,3},{3,2},{4,5},{5,4},{6,7},{7,6},{8,9},{9,8},{10,11... | collective-permute-start | bytes 12582920 | tf_op jit(solution)/shard_map/ppermute | solution.py:31
  3.9 0.1 collective-permute-start.2
  4.0 0.9 opening.1
  5.0 20.1 %all_to_all.40.begun_ref = bf16[8,3,16,512]{3,2,1,0:T(8,128)(2,1)S(1)} all-to-all(bf16[8,3,16,512]{3,2,1,0:T(8,128)(2,1)S(1)} %get-tuple-element.13), channel_id=1, replica_groups=mesh['sector'=8,'op_0'=4,'op_1'=4,'op_2'=2] {'sector'}, dimensions={0} | all-to-all | bytes 786432 | tf_op jit(solution)/shard_map/all_to_all | solution.py:27
  25.0 0.0 copy-start
  25.0 0.1 spreading.1
  25.1 0.0 copy-start.2
  25.2 24.7 %all_to_all.41.mine_ref = bf16[16,10,16,256]{3,2,1,0:T(8,128)(2,1)S(1)} all-to-all(bf16[16,10,16,256]{3,2,1,0:T(8,128)(2,1)S(1)} %spreading.1), channel_id=1, replica_groups=mesh['sector'=8,'op_0'=4,'op_1'=4,'op_2'=2] {'op_0','op_1'}, dimensions={0} | all-to-all | bytes 2621440 | tf_op jit(solution)/shard_map/all_to_all | solution.py:27
  49.9 3.2 %collective-permute-start = (bf16[16,10,16,256]{3,2,1,0:T(8,128)(2,1)S(1)}, bf16[16,10,16,256]{3,2,1,0:T(8,128)(2,1)S(1)}, u32[]{:S(2)}, u32[]{:S(2)}) collective-permute-start(bf16[16,10,16,256]{3,2,1,0:T(8,128)(2,1)S(1)} %all_to_all.41.mine_ref), channel_id=1, source_target_pairs={{0,1},{1,0},{2,3},{3,2},{4,5},{5,4},{6,7},{7,6},{8,9},{9,8},{10,11... | collective-permute-start | bytes 3932168 | tf_op jit(solution)/shard_map/ppermute | solution.py:31
  53.1 2.7 %collective-permute-done.theirs_ref = bf16[16,10,16,256]{3,2,1,0:T(8,128)(2,1)S(1)} collective-permute-done((bf16[16,10,16,256]{3,2,1,0:T(8,128)(2,1)S(1)}, bf16[16,10,16,256]{3,2,1,0:T(8,128)(2,1)S(1)}, u32[]{:S(2)}, u32[]{:S(2)}) %collective-permute-start) | collective-permute-done | bytes 1310752 | tf_op jit(solution)/shard_map/ppermute | solution.py:31
  55.8 0.0 collective-permute-done.1.left_b
  55.8 0.0 collective-permute-done.2.right_b
  55.8 0.0 copy-done
  55.8 0.0 copy-done.2
  55.8 0.0 copy-start.3
  55.8 7.7 %products.2 = bf16[16,136,128]{2,1,0:T(8,128)(2,1)S(1)} custom-call(s32[8,256]{1,0:T(8,128)S(1)} %copy-done.2, bf16[16,10,16,256]{3,2,1,0:T(8,128)(2,1)S(1)} %all_to_all.41.mine_ref, bf16[16,10,16,256]{3,2,1,0:T(8,128)(2,1)S(1)} %collective-permute-done.theirs_ref, bf16[8,512,512]{2,1,0:T(8,128)(2,1)S(1)} %copy-done, ...), custom_call_target="tpu_custom_call" | custom-call | tf_op jit(solution)/shard_map/products/pallas_call | solution.py:185
  63.5 0.0 copy-start.1
  63.5 13.8 %all_to_all.42.arrived_ref = bf16[16,136,128]{2,1,0:T(8,128)(2,1)S(1)} all-to-all(bf16[16,136,128]{2,1,0:T(8,128)(2,1)S(1)} %products.2), channel_id=1, replica_groups=mesh['sector'=8,'op_0'=4,'op_1'=4,'op_2'=2] {'op_0','op_1'}, dimensions={0} | all-to-all | bytes 1114112 | tf_op jit(solution)/shard_map/all_to_all | solution.py:27
  77.3 0.0 copy-done.3
  77.3 0.7 joining.2
  78.0 16.8 %all_to_all.43.arrived_ref = bf16[16,72,128]{2,1,0:T(8,128)(2,1)S(1)} all-to-all(bf16[16,72,128]{2,1,0:T(8,128)(2,1)S(1)} %joining.2), channel_id=1, replica_groups=mesh['sector'=8,'op_0'=4,'op_1'=4,'op_2'=2] {'sector','op_2'}, dimensions={0} | all-to-all | bytes 589824 | tf_op jit(solution)/shard_map/all_to_all | solution.py:27
  94.7 0.0 copy-done.1
  94.7 0.6 middle.1
  95.3 24.2 %all_to_all.44.mine_ref = bf16[16,10,16,256]{3,2,1,0:T(8,128)(2,1)S(1)} all-to-all(bf16[16,10,16,256]{3,2,1,0:T(8,128)(2,1)S(1)} %get-tuple-element.16), channel_id=1, replica_groups=mesh['sector'=8,'op_0'=4,'op_1'=4,'op_2'=2] {'op_0','op_1'}, dimensions={0} | all-to-all | bytes 2621440 | tf_op jit(solution)/shard_map/all_to_all | solution.py:27
  119.5 0.4 collective-permute-start.3
  120.0 2.7 %collective-permute-done.3.theirs_ref = bf16[16,10,16,256]{3,2,1,0:T(8,128)(2,1)S(1)} collective-permute-done((bf16[16,10,16,256]{3,2,1,0:T(8,128)(2,1)S(1)}, bf16[16,10,16,256]{3,2,1,0:T(8,128)(2,1)S(1)}, u32[]{:S(2)}, u32[]{:S(2)}) %collective-permute-start.3) | collective-permute-done | bytes 1310752 | tf_op jit(solution)/shard_map/ppermute | solution.py:31
  122.6 7.7 %products.3 = bf16[16,136,128]{2,1,0:T(8,128)(2,1)S(1)} custom-call(s32[8,256]{1,0:T(8,128)S(1)} %copy-done.2, bf16[16,10,16,256]{3,2,1,0:T(8,128)(2,1)S(1)} %all_to_all.44.mine_ref, bf16[16,10,16,256]{3,2,1,0:T(8,128)(2,1)S(1)} %collective-permute-done.3.theirs_ref, bf16[8,512,512]{2,1,0:T(8,128)(2,1)S(1)} %copy-done, ...), custom_call_target="tpu_custom_call" | custom-call | tf_op jit(solution)/shard_map/products/pallas_call | solution.py:185
  130.3 13.8 %all_to_all.45.arrived_ref = bf16[16,136,128]{2,1,0:T(8,128)(2,1)S(1)} all-to-all(bf16[16,136,128]{2,1,0:T(8,128)(2,1)S(1)} %products.3), channel_id=1, replica_groups=mesh['sector'=8,'op_0'=4,'op_1'=4,'op_2'=2] {'op_0','op_1'}, dimensions={0} | all-to-all | bytes 1114112 | tf_op jit(solution)/shard_map/all_to_all | solution.py:27
  144.1 0.7 joining.3
  144.8 16.8 %all_to_all.46.arrived_ref = bf16[16,72,128]{2,1,0:T(8,128)(2,1)S(1)} all-to-all(bf16[16,72,128]{2,1,0:T(8,128)(2,1)S(1)} %joining.3), channel_id=1, replica_groups=mesh['sector'=8,'op_0'=4,'op_1'=4,'op_2'=2] {'sector','op_2'}, dimensions={0} | all-to-all | bytes 589824 | tf_op jit(solution)/shard_map/all_to_all | solution.py:27
  161.6 1.3 closing.1
  162.9 10.9 %all_to_all.47.arrived_ref = f32[32,8,128]{2,1,0:T(8,128)S(1)} all-to-all(f32[32,8,128]{2,1,0:T(8,128)S(1)} %get-tuple-element.21), channel_id=1, replica_groups=mesh['sector'=8,'op_0'=4,'op_1'=4,'op_2'=2] {'op_0','op_1','op_2'}, dimensions={0} | all-to-all | bytes 262144 | tf_op jit(solution)/shard_map/all_to_all | solution.py:27
  173.8 0.7 scaling.1
Async XLA Ops:
  0.6 55.2 %collective-permute-start.1 = (bf16[8,512,512]{2,1,0:T(8,128)(2,1)}, bf16[8,512,512]{2,1,0:T(8,128)(2,1)S(1)}, u32[]{:S(2)}, u32[]{:S(2)}) collective-permute-start(bf16[8,512,512]{2,1,0:T(8,128)(2,1)} %left_a.3), channel_id=1, source_target_pairs={{0,1},{1,0},{2,3},{3,2},{4,5},{5,4},{6,7},{7,6},{8,9},{9,8},{10,11... | collective-permute-start | bytes 12582920 | tf_op jit(solution)/shard_map/ppermute | solution.py:31
  3.9 51.9 %collective-permute-start.2 = (bf16[8,512,512]{2,1,0:T(8,128)(2,1)}, bf16[8,512,512]{2,1,0:T(8,128)(2,1)S(1)}, u32[]{:S(2)}, u32[]{:S(2)}) collective-permute-start(bf16[8,512,512]{2,1,0:T(8,128)(2,1)} %right_a.3), channel_id=1, source_target_pairs={{0,1},{1,0},{2,3},{3,2},{4,5},{5,4},{6,7},{7,6},{8,9},{9,8},{10,11... | collective-permute-start | bytes 12582920 | tf_op jit(solution)/shard_map/ppermute | solution.py:31
  25.0 30.8 %copy-start = (bf16[8,512,512]{2,1,0:T(8,128)(2,1)S(1)}, bf16[8,512,512]{2,1,0:T(8,128)(2,1)}, u32[]{:S(2)}) copy-start(bf16[8,512,512]{2,1,0:T(8,128)(2,1)} %left_a.3) | copy-start | bytes 12582916
  25.1 30.6 %copy-start.2 = (s32[8,256]{1,0:T(8,128)S(1)}, s32[8,256]{1,0:T(8,128)}, u32[]{:S(2)}) copy-start(s32[8,256]{1,0:T(8,128)} %coupling_ref.3) | copy-start | bytes 24580
  49.9 5.9 %collective-permute-start = (bf16[16,10,16,256]{3,2,1,0:T(8,128)(2,1)S(1)}, bf16[16,10,16,256]{3,2,1,0:T(8,128)(2,1)S(1)}, u32[]{:S(2)}, u32[]{:S(2)}) collective-permute-start(bf16[16,10,16,256]{3,2,1,0:T(8,128)(2,1)S(1)} %all_to_all.41.mine_ref), channel_id=1, source_target_pairs={{0,1},{1,0},{2,3},{3,2},{4,5},{5,4},{6,7},{7,6},{8,9},{9,8},{10,11... | collective-permute-start | bytes 3932168 | tf_op jit(solution)/shard_map/ppermute | solution.py:31
  55.8 21.5 %copy-start.3 = (s32[8]{0:T(128)S(1)}, s32[8]{0:T(128)}, u32[]{:S(2)}) copy-start(s32[8]{0:T(128)} %sizes_ref.5) | copy-start | bytes 100
  63.5 31.3 %copy-start.1 = (f32[1,16,512]{2,1,0:T(8,128)S(1)}, f32[1,16,512]{2,1,0:T(8,128)}, u32[]{:S(2)}) copy-start(f32[1,16,512]{2,1,0:T(8,128)} %diag_ref.5) | copy-start | bytes 98308
  119.5 3.1 %collective-permute-start.3 = (bf16[16,10,16,256]{3,2,1,0:T(8,128)(2,1)S(1)}, bf16[16,10,16,256]{3,2,1,0:T(8,128)(2,1)S(1)}, u32[]{:S(2)}, u32[]{:S(2)}) collective-permute-start(bf16[16,10,16,256]{3,2,1,0:T(8,128)(2,1)S(1)} %all_to_all.44.mine_ref), channel_id=1, source_target_pairs={{0,1},{1,0},{2,3},{3,2},{4,5},{5,4},{6,7},{7,6},{8,9},{9,8},{10,11... | collective-permute-start | bytes 3932168 | tf_op jit(solution)/shard_map/ppermute | solution.py:31

commit v8 on v7

--- a/solution.py
+++ b/solution.py
@@ -10,7 +10,6 @@
 OP = ("op_0", "op_1", "op_2")
 CHIP = ("op_0", "op_1")
 CORE = "op_2"
-COLUMN = ("sector", "op_2")
 BF = jnp.bfloat16
 F32 = jnp.float32
 VMEM = pl.BlockSpec(memory_space=pltpu.VMEM)
@@ -19,7 +18,7 @@
 SHARE = 16
 LANES = 128
 TILE = 8
-LAG = 2
+LAG = 3
 LAG1 = LAG + 1
 
 
@@ -113,7 +112,7 @@
 
 def product_kernel(
     coupling_ref, mine_ref, theirs_ref, left_a, left_b, right_a, right_b, square_ref,
-    send_ref, total, rows, rights, halves, sems,
+    keep_ref, give_ref, total, rows, rights, halves, sems,
 ):
     z, chip, core = place()
     target = (z // 2) * 2 + core
@@ -174,9 +173,11 @@
     there = rows[rows.shape[0] - 2 + core].reshape(block, width).astype(F32)
     product = jnp.sum(here * total[:, near] + there * total[:, far])
     extra = three_way(product, square_ref[0, 0])
-    for peer in range(send_ref.shape[0]):
-        stacked(send_ref, peer, total[peer * 32 : (peer + 1) * 32, :].astype(BF))
-        send_ref[peer, block // 4 :, :] = extra
+    for peer in range(keep_ref.shape[0]):
+        for ref, side in ((keep_ref, core), (give_ref, 1 - core)):
+            at = pl.multiple_of(peer * 2 * SHARE + side * SHARE, SHARE)
+            stacked(ref, peer, total[pl.ds(at, SHARE), :].astype(BF))
+        give_ref[peer, block // 8 :, :] = extra
 
 
 def products(coupling, mine, theirs, left, right, left_other, right_other, square):
@@ -185,7 +186,7 @@
     return pl.pallas_call(
         product_kernel,
         in_specs=[SMEM, VMEM, VMEM, VMEM, VMEM, HBM, VMEM, VMEM],
-        out_specs=VMEM,
+        out_specs=[VMEM, VMEM],
         scratch_shapes=[
             pltpu.VMEM((block, block), F32),
             pltpu.VMEM((count, 2 * chips, share, width), BF),
@@ -193,10 +194,26 @@
             pltpu.VMEM((LAG1, block, 2 * width), BF),
             pltpu.SemaphoreType.DMA((pairs, 2)),
         ],
-        out_shape=jax.ShapeDtypeStruct((chips, block // 4 + TILE, LANES), BF),
+        out_shape=[
+            jax.ShapeDtypeStruct((chips, block // 8, LANES), BF),
+            jax.ShapeDtypeStruct((chips, block // 8 + TILE, LANES), BF),
+        ],
         compiler_params=pltpu.CompilerParams(vmem_limit_bytes=18 << 20),
         name="products",
     )(coupling, mine, theirs, left, left_other, right, right_other, square)
+
+
+def pairing_kernel(keep_ref, give_ref, got_ref, send_ref):
+    _, _, core = place()
+    half = keep_ref.shape[1]
+    here = pl.ds(pl.multiple_of(core * half, half), half)
+    there = pl.ds(pl.multiple_of((1 - core) * half, half), half)
+    both = give_ref[0, half:].astype(F32) + got_ref[0, half:].astype(F32)
+    extra = three_way(*two_sums(both))
+    for peer in range(send_ref.shape[0]):
+        send_ref[peer, here, :] = keep_ref[peer]
+        send_ref[peer, there, :] = got_ref[peer, :half, :]
+        send_ref[peer, 2 * half :, :] = extra
 
 
 def joining_kernel(sizes_ref, arrived_ref, send_ref):
@@ -205,14 +222,20 @@
     for peer in range(1, arrived_ref.shape[0]):
         total = total + arrived_ref[peer].astype(F32)
     end = total.shape[0] - TILE
-    sigma = unstacked(total[:end], 32)
-    inside = live(sigma.shape, chip * 32, sizes_ref[(z // 2) * 2 + core])
-    low = jnp.where(inside, sigma, 0.0).astype(BF)
+    half = end // 2
     extra = three_way(*two_sums(total[end:]))
+    for j in range(2):
+        sigma = unstacked(total[j * half : (j + 1) * half], SHARE)
+        first_row = (chip * 2 + core) * SHARE
+        inside = live(sigma.shape, first_row, sizes_ref[(z // 2) * 2 + j])
+        low = jnp.where(inside, sigma, 0.0).astype(BF)
+        for k in range(low.shape[1] // LANES):
+            at = j * half + k * SHARE
+            part = low[:, k * LANES : (k + 1) * LANES]
+            for peer in range(send_ref.shape[0]):
+                send_ref[peer, at : at + SHARE, :] = part
     for peer in range(send_ref.shape[0]):
-        at = (peer % 2) * SHARE
-        stacked(send_ref, peer, low[at : at + SHARE])
-        send_ref[peer, end // 2 :, :] = extra
+        send_ref[peer, end:, :] = extra
 
 
 def scalars_of(arrived_ref):
@@ -224,9 +247,13 @@
 
 
 def sigma_of(arrived_ref, target):
-    end = arrived_ref.shape[1] - TILE
-    at = (target // 2) * 4 + target % 2
-    both = arrived_ref[at, :end].astype(F32) + arrived_ref[at + 2, :end].astype(F32)
+    half = (arrived_ref.shape[1] - TILE) // 2
+    at = (target // 2) * 2
+    if isinstance(target, int):
+        part = slice((target % 2) * half, (target % 2 + 1) * half)
+    else:
+        part = pl.ds(pl.multiple_of((target % 2) * half, half), half)
+    both = arrived_ref[at, part, :].astype(F32) + arrived_ref[at + 1, part, :].astype(F32)
     return unstacked(both, SHARE)
 
 
@@ -321,17 +348,23 @@
 
     def sigma_step(outgoing, square):
         mine = swap_all(outgoing, CHIP)
-        send = products(
+        keep, give = products(
             coupling, mine, other_core(mine),
             left_blocks, right_blocks, left_other, right_other, square,
         )
         (send,) = call(
+            pairing_kernel,
+            [((chips, block // 4 + TILE, LANES), BF)],
+            [VMEM] * 3,
+            "pairing",
+        )(keep, give, other_core(give))
+        (send,) = call(
             joining_kernel,
-            [((sectors * 2, block // 8 + TILE, LANES), BF)],
+            [((sectors, block // 4 + TILE, LANES), BF)],
             [SMEM, VMEM],
             "joining",
         )(sector_sizes, swap_all(send, CHIP))
-        return swap_all(send, COLUMN)
+        return swap_all(send, "sector")
 
     arrived = sigma_step(outgoing, square)
     outgoing, everyone, own, square, theta = call(

time: 175 us -> 173 us (0.989)
  blocking collectives: 141 us -> 133 us
  starting transfers between devices: 7.04 us -> 11.4 us
  waiting for transfers between devices: 5.33 us -> 7.75 us
    all_to_all x8, blocking collectives: 141 us -> 133 us  [swap_all(): return lax.all_to_all(x, axes, split_axis=0, concat_axis=0, tiled=True)]
    ppermute x4 -> x6, starting transfers between devices: 7.04 us -> 11.4 us  [other_core(): return lax.ppermute(x, CORE, [(0, 1), (1, 0)])]
    ppermute x4 -> x6, waiting for transfers between devices: 5.33 us -> 7.75 us  [other_core(): return lax.ppermute(x, CORE, [(0, 1), (1, 0)])]
  transfers between devices with their start and end apart: 4 -> 6, of which waited for: 2 -> 4; matrix products, arithmetic and copies ran while one was open for 0% -> 0% of each run, Pallas kernels for 1% -> 1%
where the time goes in v8:
time: 173 us
  blocking collectives  133 us (77%)
  Pallas kernels  20.1 us (12%)
  starting transfers between devices  11.4 us (7%)
  waiting for transfers between devices  7.75 us (4%)
    all_to_all x8, blocking collectives, swap_all(): return lax.all_to_all(x, axes, split_axis=0, concat_axis=0, tiled=True)  133 us
    pallas_call x2, Pallas kernels, products(): pl.pallas_call(product_kernel, in_specs=[SMEM, VMEM, VMEM, VMEM, VMEM, HB...  15 us
    ppermute x6, starting transfers between devices, other_core(): return lax.ppermute(x, CORE, [(0, 1), (1, 0)])  11.4 us
    ppermute x6, waiting for transfers between devices, other_core(): return lax.ppermute(x, CORE, [(0, 1), (1, 0)])  7.75 us
  transfers between devices with their start and end apart: 6, of which 4 were waited for; matrix products, arithmetic and copies ran while one was open for 0% of the time, Pallas kernels for 1%

profile of v8, /device:TPU:1, one launch (start us, length us, event | category | flops | bytes accessed | tf_op | source)
XLA Modules:
  0.0 172.8 jit_solution(14671675158341033701)
XLA Ops:
  0.6 3.3 %collective-permute-start.1 = (bf16[8,512,512]{2,1,0:T(8,128)(2,1)}, bf16[8,512,512]{2,1,0:T(8,128)(2,1)S(1)}, u32[]{:S(2)}, u32[]{:S(2)}) collective-permute-start(bf16[8,512,512]{2,1,0:T(8,128)(2,1)} %left_a.3), channel_id=1, source_target_pairs={{0,1},{1,0},{2,3},{3,2},{4,5},{5,4},{6,7},{7,6},{8,9},{9,8},{10,11... | collective-permute-start | bytes 12582920 | tf_op jit(solution)/shard_map/ppermute | solution.py:30
  3.9 0.1 collective-permute-start.2
  4.0 0.9 opening.1
  5.0 20.1 %all_to_all.40.begun_ref = bf16[8,3,16,512]{3,2,1,0:T(8,128)(2,1)S(1)} all-to-all(bf16[8,3,16,512]{3,2,1,0:T(8,128)(2,1)S(1)} %get-tuple-element.17), channel_id=1, replica_groups=mesh['sector'=8,'op_0'=4,'op_1'=4,'op_2'=2] {'sector'}, dimensions={0} | all-to-all | bytes 786432 | tf_op jit(solution)/shard_map/all_to_all | solution.py:26
  25.0 0.0 copy-start
  25.0 0.1 spreading.1
  25.1 0.0 copy-start.2
  25.2 24.7 %all_to_all.41.mine_ref = bf16[16,10,16,256]{3,2,1,0:T(8,128)(2,1)S(1)} all-to-all(bf16[16,10,16,256]{3,2,1,0:T(8,128)(2,1)S(1)} %spreading.1), channel_id=1, replica_groups=mesh['sector'=8,'op_0'=4,'op_1'=4,'op_2'=2] {'op_0','op_1'}, dimensions={0} | all-to-all | bytes 2621440 | tf_op jit(solution)/shard_map/all_to_all | solution.py:26
  49.9 3.2 %collective-permute-start = (bf16[16,10,16,256]{3,2,1,0:T(8,128)(2,1)S(1)}, bf16[16,10,16,256]{3,2,1,0:T(8,128)(2,1)S(1)}, u32[]{:S(2)}, u32[]{:S(2)}) collective-permute-start(bf16[16,10,16,256]{3,2,1,0:T(8,128)(2,1)S(1)} %all_to_all.41.mine_ref), channel_id=1, source_target_pairs={{0,1},{1,0},{2,3},{3,2},{4,5},{5,4},{6,7},{7,6},{8,9},{9,8},{10,11... | collective-permute-start | bytes 3932168 | tf_op jit(solution)/shard_map/ppermute | solution.py:30
  53.1 2.7 %collective-permute-done.theirs_ref = bf16[16,10,16,256]{3,2,1,0:T(8,128)(2,1)S(1)} collective-permute-done((bf16[16,10,16,256]{3,2,1,0:T(8,128)(2,1)S(1)}, bf16[16,10,16,256]{3,2,1,0:T(8,128)(2,1)S(1)}, u32[]{:S(2)}, u32[]{:S(2)}) %collective-permute-start) | collective-permute-done | bytes 1310752 | tf_op jit(solution)/shard_map/ppermute | solution.py:30
  55.8 0.0 collective-permute-done.1.left_b
  55.8 0.0 collective-permute-done.2.right_b
  55.8 0.0 copy-done
  55.8 0.0 copy-done.2
  55.8 7.5 %products.2 = (bf16[16,64,128]{2,1,0:T(8,128)(2,1)S(1)}, bf16[16,72,128]{2,1,0:T(8,128)(2,1)S(1)}) custom-call(s32[8,256]{1,0:T(8,128)S(1)} %copy-done.2, bf16[16,10,16,256]{3,2,1,0:T(8,128)(2,1)S(1)} %all_to_all.41.mine_ref, bf16[16,10,16,256]{3,2,1,0:T(8,128)(2,1)S(1)} %collective-permute-done.theirs_ref, bf16[8,512,512]{2,1,0:T(8,128)(2,1)S(1)} %copy-done, ...), custom_call_target="tpu_custom_call" | custom-call | tf_op jit(solution)/shard_map/products/pallas_call | solution.py:186
  63.3 0.0 copy-start.3
  63.3 0.5 collective-permute-start.3
  63.7 1.2 collective-permute-done.3.got_ref
  65.0 0.1 pairing.2
  65.1 0.0 copy-start.1
  65.1 13.8 %all_to_all.42.arrived_ref = bf16[16,136,128]{2,1,0:T(8,128)(2,1)S(1)} all-to-all(bf16[16,136,128]{2,1,0:T(8,128)(2,1)S(1)} %pairing.2), channel_id=1, replica_groups=mesh['sector'=8,'op_0'=4,'op_1'=4,'op_2'=2] {'op_0','op_1'}, dimensions={0} | all-to-all | bytes 1114112 | tf_op jit(solution)/shard_map/all_to_all | solution.py:26
  78.8 0.0 copy-done.3
  78.8 0.7 joining.2
  79.5 12.3 %all_to_all.43.arrived_ref = bf16[8,136,128]{2,1,0:T(8,128)(2,1)S(1)} all-to-all(bf16[8,136,128]{2,1,0:T(8,128)(2,1)S(1)} %joining.2), channel_id=1, replica_groups=mesh['sector'=8,'op_0'=4,'op_1'=4,'op_2'=2] {'sector'}, dimensions={0} | all-to-all | bytes 557056 | tf_op jit(solution)/shard_map/all_to_all | solution.py:26
  91.8 0.0 copy-done.1
  91.8 0.6 middle.1
  92.4 20.8 %all_to_all.44.mine_ref = bf16[16,10,16,256]{3,2,1,0:T(8,128)(2,1)S(1)} all-to-all(bf16[16,10,16,256]{3,2,1,0:T(8,128)(2,1)S(1)} %get-tuple-element.22), channel_id=1, replica_groups=mesh['sector'=8,'op_0'=4,'op_1'=4,'op_2'=2] {'op_0','op_1'}, dimensions={0} | all-to-all | bytes 2621440 | tf_op jit(solution)/shard_map/all_to_all | solution.py:26
  113.2 3.9 %collective-permute-start.4 = (bf16[16,10,16,256]{3,2,1,0:T(8,128)(2,1)S(1)}, bf16[16,10,16,256]{3,2,1,0:T(8,128)(2,1)S(1)}, u32[]{:S(2)}, u32[]{:S(2)}) collective-permute-start(bf16[16,10,16,256]{3,2,1,0:T(8,128)(2,1)S(1)} %all_to_all.44.mine_ref), channel_id=1, source_target_pairs={{0,1},{1,0},{2,3},{3,2},{4,5},{5,4},{6,7},{7,6},{8,9},{9,8},{10,11... | collective-permute-start | bytes 3932168 | tf_op jit(solution)/shard_map/ppermute | solution.py:30
  117.1 2.7 %collective-permute-done.4.theirs_ref = bf16[16,10,16,256]{3,2,1,0:T(8,128)(2,1)S(1)} collective-permute-done((bf16[16,10,16,256]{3,2,1,0:T(8,128)(2,1)S(1)}, bf16[16,10,16,256]{3,2,1,0:T(8,128)(2,1)S(1)}, u32[]{:S(2)}, u32[]{:S(2)}) %collective-permute-start.4) | collective-permute-done | bytes 1310752 | tf_op jit(solution)/shard_map/ppermute | solution.py:30
  119.8 7.5 %products.3 = (bf16[16,64,128]{2,1,0:T(8,128)(2,1)S(1)}, bf16[16,72,128]{2,1,0:T(8,128)(2,1)S(1)}) custom-call(s32[8,256]{1,0:T(8,128)S(1)} %copy-done.2, bf16[16,10,16,256]{3,2,1,0:T(8,128)(2,1)S(1)} %all_to_all.44.mine_ref, bf16[16,10,16,256]{3,2,1,0:T(8,128)(2,1)S(1)} %collective-permute-done.4.theirs_ref, bf16[8,512,512]{2,1,0:T(8,128)(2,1)S(1)} %copy-done, ...), custom_call_target="tpu_custom_call" | custom-call | tf_op jit(solution)/shard_map/products/pallas_call | solution.py:186
  127.3 0.5 collective-permute-start.5
  127.7 1.2 collective-permute-done.5.got_ref
  128.9 0.1 pairing.3
  129.0 13.8 %all_to_all.45.arrived_ref = bf16[16,136,128]{2,1,0:T(8,128)(2,1)S(1)} all-to-all(bf16[16,136,128]{2,1,0:T(8,128)(2,1)S(1)} %pairing.3), channel_id=1, replica_groups=mesh['sector'=8,'op_0'=4,'op_1'=4,'op_2'=2] {'op_0','op_1'}, dimensions={0} | all-to-all | bytes 1114112 | tf_op jit(solution)/shard_map/all_to_all | solution.py:26
  142.8 0.7 joining.3
  143.5 12.1 %all_to_all.46.arrived_ref = bf16[8,136,128]{2,1,0:T(8,128)(2,1)S(1)} all-to-all(bf16[8,136,128]{2,1,0:T(8,128)(2,1)S(1)} %joining.3), channel_id=1, replica_groups=mesh['sector'=8,'op_0'=4,'op_1'=4,'op_2'=2] {'sector'}, dimensions={0} | all-to-all | bytes 557056 | tf_op jit(solution)/shard_map/all_to_all | solution.py:26
  155.6 1.3 closing.1
  157.0 15.1 %all_to_all.47.arrived_ref = f32[32,8,128]{2,1,0:T(8,128)S(1)} all-to-all(f32[32,8,128]{2,1,0:T(8,128)S(1)} %get-tuple-element.29), channel_id=1, replica_groups=mesh['sector'=8,'op_0'=4,'op_1'=4,'op_2'=2] {'op_0','op_1','op_2'}, dimensions={0} | all-to-all | bytes 262144 | tf_op jit(solution)/shard_map/all_to_all | solution.py:26
  172.1 0.7 scaling.1
Async XLA Ops:
  0.6 55.2 %collective-permute-start.1 = (bf16[8,512,512]{2,1,0:T(8,128)(2,1)}, bf16[8,512,512]{2,1,0:T(8,128)(2,1)S(1)}, u32[]{:S(2)}, u32[]{:S(2)}) collective-permute-start(bf16[8,512,512]{2,1,0:T(8,128)(2,1)} %left_a.3), channel_id=1, source_target_pairs={{0,1},{1,0},{2,3},{3,2},{4,5},{5,4},{6,7},{7,6},{8,9},{9,8},{10,11... | collective-permute-start | bytes 12582920 | tf_op jit(solution)/shard_map/ppermute | solution.py:30
  3.9 51.9 %collective-permute-start.2 = (bf16[8,512,512]{2,1,0:T(8,128)(2,1)}, bf16[8,512,512]{2,1,0:T(8,128)(2,1)S(1)}, u32[]{:S(2)}, u32[]{:S(2)}) collective-permute-start(bf16[8,512,512]{2,1,0:T(8,128)(2,1)} %right_a.3), channel_id=1, source_target_pairs={{0,1},{1,0},{2,3},{3,2},{4,5},{5,4},{6,7},{7,6},{8,9},{9,8},{10,11... | collective-permute-start | bytes 12582920 | tf_op jit(solution)/shard_map/ppermute | solution.py:30
  25.0 30.8 %copy-start = (bf16[8,512,512]{2,1,0:T(8,128)(2,1)S(1)}, bf16[8,512,512]{2,1,0:T(8,128)(2,1)}, u32[]{:S(2)}) copy-start(bf16[8,512,512]{2,1,0:T(8,128)(2,1)} %left_a.3) | copy-start | bytes 12582916
  25.1 30.6 %copy-start.2 = (s32[8,256]{1,0:T(8,128)S(1)}, s32[8,256]{1,0:T(8,128)}, u32[]{:S(2)}) copy-start(s32[8,256]{1,0:T(8,128)} %coupling_ref.3) | copy-start | bytes 24580
  49.9 5.9 %collective-permute-start = (bf16[16,10,16,256]{3,2,1,0:T(8,128)(2,1)S(1)}, bf16[16,10,16,256]{3,2,1,0:T(8,128)(2,1)S(1)}, u32[]{:S(2)}, u32[]{:S(2)}) collective-permute-start(bf16[16,10,16,256]{3,2,1,0:T(8,128)(2,1)S(1)} %all_to_all.41.mine_ref), channel_id=1, source_target_pairs={{0,1},{1,0},{2,3},{3,2},{4,5},{5,4},{6,7},{7,6},{8,9},{9,8},{10,11... | collective-permute-start | bytes 3932168 | tf_op jit(solution)/shard_map/ppermute | solution.py:30
  63.3 15.6 %copy-start.3 = (s32[8]{0:T(128)S(1)}, s32[8]{0:T(128)}, u32[]{:S(2)}) copy-start(s32[8]{0:T(128)} %sizes_ref.5) | copy-start | bytes 100
  63.3 1.7 collective-permute-start.3
  65.1 26.8 %copy-start.1 = (f32[1,16,512]{2,1,0:T(8,128)S(1)}, f32[1,16,512]{2,1,0:T(8,128)}, u32[]{:S(2)}) copy-start(f32[1,16,512]{2,1,0:T(8,128)} %diag_ref.5) | copy-start | bytes 98308
  113.2 6.5 %collective-permute-start.4 = (bf16[16,10,16,256]{3,2,1,0:T(8,128)(2,1)S(1)}, bf16[16,10,16,256]{3,2,1,0:T(8,128)(2,1)S(1)}, u32[]{:S(2)}, u32[]{:S(2)}) collective-permute-start(bf16[16,10,16,256]{3,2,1,0:T(8,128)(2,1)S(1)} %all_to_all.44.mine_ref), channel_id=1, source_target_pairs={{0,1},{1,0},{2,3},{3,2},{4,5},{5,4},{6,7},{7,6},{8,9},{9,8},{10,11... | collective-permute-start | bytes 3932168 | tf_op jit(solution)/shard_map/ppermute | solution.py:30
  127.3 1.7 collective-permute-start.5

commit v9 on v7

--- a/solution.py
+++ b/solution.py
@@ -10,7 +10,6 @@
 OP = ("op_0", "op_1", "op_2")
 CHIP = ("op_0", "op_1")
 CORE = "op_2"
-COLUMN = ("sector", "op_2")
 BF = jnp.bfloat16
 F32 = jnp.float32
 VMEM = pl.BlockSpec(memory_space=pltpu.VMEM)
@@ -19,7 +18,7 @@
 SHARE = 16
 LANES = 128
 TILE = 8
-LAG = 2
+LAG = 3
 LAG1 = LAG + 1
 
 
@@ -175,8 +174,8 @@
     product = jnp.sum(here * total[:, near] + there * total[:, far])
     extra = three_way(product, square_ref[0, 0])
     for peer in range(send_ref.shape[0]):
-        stacked(send_ref, peer, total[peer * 32 : (peer + 1) * 32, :].astype(BF))
-        send_ref[peer, block // 4 :, :] = extra
+        stacked(send_ref, peer, total[peer * SHARE : (peer + 1) * SHARE, :].astype(BF))
+        send_ref[peer, block // 8 :, :] = extra
 
 
 def products(coupling, mine, theirs, left, right, left_other, right_other, square):
@@ -193,7 +192,7 @@
             pltpu.VMEM((LAG1, block, 2 * width), BF),
             pltpu.SemaphoreType.DMA((pairs, 2)),
         ],
-        out_shape=jax.ShapeDtypeStruct((chips, block // 4 + TILE, LANES), BF),
+        out_shape=jax.ShapeDtypeStruct((2 * chips, block // 8 + TILE, LANES), BF),
         compiler_params=pltpu.CompilerParams(vmem_limit_bytes=18 << 20),
         name="products",
     )(coupling, mine, theirs, left, left_other, right, right_other, square)
@@ -201,18 +200,26 @@
 
 def joining_kernel(sizes_ref, arrived_ref, send_ref):
     z, chip, core = place()
-    total = arrived_ref[0].astype(F32)
-    for peer in range(1, arrived_ref.shape[0]):
-        total = total + arrived_ref[peer].astype(F32)
-    end = total.shape[0] - TILE
-    sigma = unstacked(total[:end], 32)
-    inside = live(sigma.shape, chip * 32, sizes_ref[(z // 2) * 2 + core])
-    low = jnp.where(inside, sigma, 0.0).astype(BF)
-    extra = three_way(*two_sums(total[end:]))
+    totals = []
+    for j in range(2):
+        total = arrived_ref[j].astype(F32)
+        for peer in range(2 + j, arrived_ref.shape[0], 2):
+            total = total + arrived_ref[peer].astype(F32)
+        totals.append(total)
+    half = totals[0].shape[0] - TILE
+    extra = three_way(*two_sums(totals[0][half:] + totals[1][half:]))
+    for j, total in enumerate(totals):
+        sigma = unstacked(total[:half], SHARE)
+        first_row = (chip * 2 + core) * SHARE
+        inside = live(sigma.shape, first_row, sizes_ref[(z // 2) * 2 + j])
+        low = jnp.where(inside, sigma, 0.0).astype(BF)
+        for k in range(low.shape[1] // LANES):
+            at = j * half + k * SHARE
+            part = low[:, k * LANES : (k + 1) * LANES]
+            for peer in range(send_ref.shape[0]):
+                send_ref[peer, at : at + SHARE, :] = part
     for peer in range(send_ref.shape[0]):
-        at = (peer % 2) * SHARE
-        stacked(send_ref, peer, low[at : at + SHARE])
-        send_ref[peer, end // 2 :, :] = extra
+        send_ref[peer, 2 * half :, :] = extra
 
 
 def scalars_of(arrived_ref):
@@ -224,9 +231,13 @@
 
 
 def sigma_of(arrived_ref, target):
-    end = arrived_ref.shape[1] - TILE
-    at = (target // 2) * 4 + target % 2
-    both = arrived_ref[at, :end].astype(F32) + arrived_ref[at + 2, :end].astype(F32)
+    half = (arrived_ref.shape[1] - TILE) // 2
+    at = (target // 2) * 2
+    if isinstance(target, int):
+        part = slice((target % 2) * half, (target % 2 + 1) * half)
+    else:
+        part = pl.ds(pl.multiple_of((target % 2) * half, half), half)
+    both = arrived_ref[at, part, :].astype(F32) + arrived_ref[at + 1, part, :].astype(F32)
     return unstacked(both, SHARE)
 
 
@@ -327,11 +338,11 @@
         )
         (send,) = call(
             joining_kernel,
-            [((sectors * 2, block // 8 + TILE, LANES), BF)],
+            [((sectors, block // 4 + TILE, LANES), BF)],
             [SMEM, VMEM],
             "joining",
-        )(sector_sizes, swap_all(send, CHIP))
-        return swap_all(send, COLUMN)
+        )(sector_sizes, swap_all(send, OP))
+        return swap_all(send, "sector")
 
     arrived = sigma_step(outgoing, square)
     outgoing, everyone, own, square, theta = call(

time: 175 us -> 174 us (level)
  no operation moved by 1% of the time
where the time goes in v9:
time: 174 us
  blocking collectives  140 us (80%)
  Pallas kernels  19.9 us (11%)
  starting transfers between devices  8.12 us (5%)
  waiting for transfers between devices  5.33 us (3%)
    all_to_all x8, blocking collectives, swap_all(): return lax.all_to_all(x, axes, split_axis=0, concat_axis=0, tiled=True)  140 us
    pallas_call x2, Pallas kernels, products(): pl.pallas_call(product_kernel, in_specs=[SMEM, VMEM, VMEM, VMEM, VMEM, HB...  14.9 us
    ppermute x4, starting transfers between devices, other_core(): return lax.ppermute(x, CORE, [(0, 1), (1, 0)])  8.12 us
    ppermute x4, waiting for transfers between devices, other_core(): return lax.ppermute(x, CORE, [(0, 1), (1, 0)])  5.33 us
  transfers between devices with their start and end apart: 4, of which 2 were waited for; matrix products, arithmetic and copies ran while one was open for 0% of the time, Pallas kernels for 1%

profile of v9, /device:TPU:1, one launch (start us, length us, event | category | flops | bytes accessed | tf_op | source)
XLA Modules:
  0.0 174.0 jit_solution(7358785476270348507)
XLA Ops:
  0.6 3.3 %collective-permute-start.1 = (bf16[8,512,512]{2,1,0:T(8,128)(2,1)}, bf16[8,512,512]{2,1,0:T(8,128)(2,1)S(1)}, u32[]{:S(2)}, u32[]{:S(2)}) collective-permute-start(bf16[8,512,512]{2,1,0:T(8,128)(2,1)} %left_a.3), channel_id=1, source_target_pairs={{0,1},{1,0},{2,3},{3,2},{4,5},{5,4},{6,7},{7,6},{8,9},{9,8},{10,11... | collective-permute-start | bytes 12582920 | tf_op jit(solution)/shard_map/ppermute | solution.py:30
  3.9 0.1 collective-permute-start.2
  4.0 0.9 opening.1
  5.0 20.1 %all_to_all.40.begun_ref = bf16[8,3,16,512]{3,2,1,0:T(8,128)(2,1)S(1)} all-to-all(bf16[8,3,16,512]{3,2,1,0:T(8,128)(2,1)S(1)} %get-tuple-element.13), channel_id=1, replica_groups=mesh['sector'=8,'op_0'=4,'op_1'=4,'op_2'=2] {'sector'}, dimensions={0} | all-to-all | bytes 786432 | tf_op jit(solution)/shard_map/all_to_all | solution.py:26
  25.0 0.0 copy-start
  25.0 0.1 spreading.1
  25.1 0.0 copy-start.2
  25.2 24.7 %all_to_all.41.mine_ref = bf16[16,10,16,256]{3,2,1,0:T(8,128)(2,1)S(1)} all-to-all(bf16[16,10,16,256]{3,2,1,0:T(8,128)(2,1)S(1)} %spreading.1), channel_id=1, replica_groups=mesh['sector'=8,'op_0'=4,'op_1'=4,'op_2'=2] {'op_0','op_1'}, dimensions={0} | all-to-all | bytes 2621440 | tf_op jit(solution)/shard_map/all_to_all | solution.py:26
  49.9 3.2 %collective-permute-start = (bf16[16,10,16,256]{3,2,1,0:T(8,128)(2,1)S(1)}, bf16[16,10,16,256]{3,2,1,0:T(8,128)(2,1)S(1)}, u32[]{:S(2)}, u32[]{:S(2)}) collective-permute-start(bf16[16,10,16,256]{3,2,1,0:T(8,128)(2,1)S(1)} %all_to_all.41.mine_ref), channel_id=1, source_target_pairs={{0,1},{1,0},{2,3},{3,2},{4,5},{5,4},{6,7},{7,6},{8,9},{9,8},{10,11... | collective-permute-start | bytes 3932168 | tf_op jit(solution)/shard_map/ppermute | solution.py:30
  53.1 2.7 %collective-permute-done.theirs_ref = bf16[16,10,16,256]{3,2,1,0:T(8,128)(2,1)S(1)} collective-permute-done((bf16[16,10,16,256]{3,2,1,0:T(8,128)(2,1)S(1)}, bf16[16,10,16,256]{3,2,1,0:T(8,128)(2,1)S(1)}, u32[]{:S(2)}, u32[]{:S(2)}) %collective-permute-start) | collective-permute-done | bytes 1310752 | tf_op jit(solution)/shard_map/ppermute | solution.py:30
  55.8 0.0 collective-permute-done.1.left_b
  55.8 0.0 collective-permute-done.2.right_b
  55.8 0.0 copy-done
  55.8 0.0 copy-done.2
  55.8 0.0 copy-start.3
  55.8 7.4 %products.2 = bf16[32,72,128]{2,1,0:T(8,128)(2,1)S(1)} custom-call(s32[8,256]{1,0:T(8,128)S(1)} %copy-done.2, bf16[16,10,16,256]{3,2,1,0:T(8,128)(2,1)S(1)} %all_to_all.41.mine_ref, bf16[16,10,16,256]{3,2,1,0:T(8,128)(2,1)S(1)} %collective-permute-done.theirs_ref, bf16[8,512,512]{2,1,0:T(8,128)(2,1)S(1)} %copy-done, ...), custom_call_target="tpu_custom_call" | custom-call | tf_op jit(solution)/shard_map/products/pallas_call | solution.py:184
  63.2 0.0 copy-start.1
  63.3 15.4 %all_to_all.42.arrived_ref = bf16[32,72,128]{2,1,0:T(8,128)(2,1)S(1)} all-to-all(bf16[32,72,128]{2,1,0:T(8,128)(2,1)S(1)} %products.2), channel_id=1, replica_groups=mesh['sector'=8,'op_0'=4,'op_1'=4,'op_2'=2] {'op_0','op_1','op_2'}, dimensions={0} | all-to-all | bytes 1179648 | tf_op jit(solution)/shard_map/all_to_all | solution.py:26
  78.6 0.0 copy-done.3
  78.6 0.7 joining.2
  79.3 15.0 %all_to_all.43.arrived_ref = bf16[8,136,128]{2,1,0:T(8,128)(2,1)S(1)} all-to-all(bf16[8,136,128]{2,1,0:T(8,128)(2,1)S(1)} %joining.2), channel_id=1, replica_groups=mesh['sector'=8,'op_0'=4,'op_1'=4,'op_2'=2] {'sector'}, dimensions={0} | all-to-all | bytes 557056 | tf_op jit(solution)/shard_map/all_to_all | solution.py:26
  94.3 0.0 copy-done.1
  94.3 0.6 middle.1
  94.9 22.7 %all_to_all.44.mine_ref = bf16[16,10,16,256]{3,2,1,0:T(8,128)(2,1)S(1)} all-to-all(bf16[16,10,16,256]{3,2,1,0:T(8,128)(2,1)S(1)} %get-tuple-element.16), channel_id=1, replica_groups=mesh['sector'=8,'op_0'=4,'op_1'=4,'op_2'=2] {'op_0','op_1'}, dimensions={0} | all-to-all | bytes 2621440 | tf_op jit(solution)/shard_map/all_to_all | solution.py:26
  117.6 1.5 collective-permute-start.3
  119.1 2.7 %collective-permute-done.3.theirs_ref = bf16[16,10,16,256]{3,2,1,0:T(8,128)(2,1)S(1)} collective-permute-done((bf16[16,10,16,256]{3,2,1,0:T(8,128)(2,1)S(1)}, bf16[16,10,16,256]{3,2,1,0:T(8,128)(2,1)S(1)}, u32[]{:S(2)}, u32[]{:S(2)}) %collective-permute-start.3) | collective-permute-done | bytes 1310752 | tf_op jit(solution)/shard_map/ppermute | solution.py:30
  121.7 7.5 %products.3 = bf16[32,72,128]{2,1,0:T(8,128)(2,1)S(1)} custom-call(s32[8,256]{1,0:T(8,128)S(1)} %copy-done.2, bf16[16,10,16,256]{3,2,1,0:T(8,128)(2,1)S(1)} %all_to_all.44.mine_ref, bf16[16,10,16,256]{3,2,1,0:T(8,128)(2,1)S(1)} %collective-permute-done.3.theirs_ref, bf16[8,512,512]{2,1,0:T(8,128)(2,1)S(1)} %copy-done, ...), custom_call_target="tpu_custom_call" | custom-call | tf_op jit(solution)/shard_map/products/pallas_call | solution.py:184
  129.2 15.4 %all_to_all.45.arrived_ref = bf16[32,72,128]{2,1,0:T(8,128)(2,1)S(1)} all-to-all(bf16[32,72,128]{2,1,0:T(8,128)(2,1)S(1)} %products.3), channel_id=1, replica_groups=mesh['sector'=8,'op_0'=4,'op_1'=4,'op_2'=2] {'op_0','op_1','op_2'}, dimensions={0} | all-to-all | bytes 1179648 | tf_op jit(solution)/shard_map/all_to_all | solution.py:26
  144.7 0.7 joining.3
  145.3 15.0 %all_to_all.46.arrived_ref = bf16[8,136,128]{2,1,0:T(8,128)(2,1)S(1)} all-to-all(bf16[8,136,128]{2,1,0:T(8,128)(2,1)S(1)} %joining.3), channel_id=1, replica_groups=mesh['sector'=8,'op_0'=4,'op_1'=4,'op_2'=2] {'sector'}, dimensions={0} | all-to-all | bytes 557056 | tf_op jit(solution)/shard_map/all_to_all | solution.py:26
  160.3 1.3 closing.1
  161.7 11.6 %all_to_all.47.arrived_ref = f32[32,8,128]{2,1,0:T(8,128)S(1)} all-to-all(f32[32,8,128]{2,1,0:T(8,128)S(1)} %get-tuple-element.21), channel_id=1, replica_groups=mesh['sector'=8,'op_0'=4,'op_1'=4,'op_2'=2] {'op_0','op_1','op_2'}, dimensions={0} | all-to-all | bytes 262144 | tf_op jit(solution)/shard_map/all_to_all | solution.py:26
  173.3 0.7 scaling.1
Async XLA Ops:
  0.6 55.2 %collective-permute-start.1 = (bf16[8,512,512]{2,1,0:T(8,128)(2,1)}, bf16[8,512,512]{2,1,0:T(8,128)(2,1)S(1)}, u32[]{:S(2)}, u32[]{:S(2)}) collective-permute-start(bf16[8,512,512]{2,1,0:T(8,128)(2,1)} %left_a.3), channel_id=1, source_target_pairs={{0,1},{1,0},{2,3},{3,2},{4,5},{5,4},{6,7},{7,6},{8,9},{9,8},{10,11... | collective-permute-start | bytes 12582920 | tf_op jit(solution)/shard_map/ppermute | solution.py:30
  3.9 51.9 %collective-permute-start.2 = (bf16[8,512,512]{2,1,0:T(8,128)(2,1)}, bf16[8,512,512]{2,1,0:T(8,128)(2,1)S(1)}, u32[]{:S(2)}, u32[]{:S(2)}) collective-permute-start(bf16[8,512,512]{2,1,0:T(8,128)(2,1)} %right_a.3), channel_id=1, source_target_pairs={{0,1},{1,0},{2,3},{3,2},{4,5},{5,4},{6,7},{7,6},{8,9},{9,8},{10,11... | collective-permute-start | bytes 12582920 | tf_op jit(solution)/shard_map/ppermute | solution.py:30
  25.0 30.8 %copy-start = (bf16[8,512,512]{2,1,0:T(8,128)(2,1)S(1)}, bf16[8,512,512]{2,1,0:T(8,128)(2,1)}, u32[]{:S(2)}) copy-start(bf16[8,512,512]{2,1,0:T(8,128)(2,1)} %left_a.3) | copy-start | bytes 12582916
  25.1 30.6 %copy-start.2 = (s32[8,256]{1,0:T(8,128)S(1)}, s32[8,256]{1,0:T(8,128)}, u32[]{:S(2)}) copy-start(s32[8,256]{1,0:T(8,128)} %coupling_ref.3) | copy-start | bytes 24580
  49.9 5.9 %collective-permute-start = (bf16[16,10,16,256]{3,2,1,0:T(8,128)(2,1)S(1)}, bf16[16,10,16,256]{3,2,1,0:T(8,128)(2,1)S(1)}, u32[]{:S(2)}, u32[]{:S(2)}) collective-permute-start(bf16[16,10,16,256]{3,2,1,0:T(8,128)(2,1)S(1)} %all_to_all.41.mine_ref), channel_id=1, source_target_pairs={{0,1},{1,0},{2,3},{3,2},{4,5},{5,4},{6,7},{7,6},{8,9},{9,8},{10,11... | collective-permute-start | bytes 3932168 | tf_op jit(solution)/shard_map/ppermute | solution.py:30
  55.8 22.8 %copy-start.3 = (s32[8]{0:T(128)S(1)}, s32[8]{0:T(128)}, u32[]{:S(2)}) copy-start(s32[8]{0:T(128)} %sizes_ref.5) | copy-start | bytes 100
  63.2 31.0 %copy-start.1 = (f32[1,16,512]{2,1,0:T(8,128)S(1)}, f32[1,16,512]{2,1,0:T(8,128)}, u32[]{:S(2)}) copy-start(f32[1,16,512]{2,1,0:T(8,128)} %diag_ref.5) | copy-start | bytes 98308
  117.6 4.1 %collective-permute-start.3 = (bf16[16,10,16,256]{3,2,1,0:T(8,128)(2,1)S(1)}, bf16[16,10,16,256]{3,2,1,0:T(8,128)(2,1)S(1)}, u32[]{:S(2)}, u32[]{:S(2)}) collective-permute-start(bf16[16,10,16,256]{3,2,1,0:T(8,128)(2,1)S(1)} %all_to_all.44.mine_ref), channel_id=1, source_target_pairs={{0,1},{1,0},{2,3},{3,2},{4,5},{5,4},{6,7},{7,6},{8,9},{9,8},{10,11... | collective-permute-start | bytes 3932168 | tf_op jit(solution)/shard_map/ppermute | solution.py:30

commit v10 on v8

--- a/solution.py
+++ b/solution.py
@@ -8,7 +8,7 @@
 from jax.sharding import PartitionSpec as P
 
 OP = ("op_0", "op_1", "op_2")
-CHIP = ("op_0", "op_1")
+CHIP = ("op_1", "op_0")
 CORE = "op_2"
 BF = jnp.bfloat16
 F32 = jnp.float32
@@ -134,8 +134,9 @@
     move(0).start()
     for k in range(rows.shape[0]):
         for at in range(mine_ref.shape[0]):
-            rows[k, 2 * at + core] = mine_ref[at, k]
-            rows[k, 2 * at + 1 - core] = theirs_ref[at, k]
+            turned = (at % 4) * 4 + at // 4
+            rows[k, 2 * turned + core] = mine_ref[at, k]
+            rows[k, 2 * turned + 1 - core] = theirs_ref[at, k]
     for pair in range(1, pairs):
         fetch(pair).start()
         move(pair).start()
@@ -211,8 +212,9 @@
     both = give_ref[0, half:].astype(F32) + got_ref[0, half:].astype(F32)
     extra = three_way(*two_sums(both))
     for peer in range(send_ref.shape[0]):
-        send_ref[peer, here, :] = keep_ref[peer]
-        send_ref[peer, there, :] = got_ref[peer, :half, :]
+        turned = (peer % 4) * 4 + peer // 4
+        send_ref[peer, here, :] = keep_ref[turned]
+        send_ref[peer, there, :] = got_ref[turned, :half, :]
         send_ref[peer, 2 * half :, :] = extra
 
 

time: 173 us -> 173 us (level)
  no operation moved by 1% of the time
where the time goes in v10:
time: 173 us
  blocking collectives  132 us (76%)
  Pallas kernels  20.1 us (12%)
  starting transfers between devices  12 us (7%)
  waiting for transfers between devices  7.75 us (4%)
    all_to_all x8, blocking collectives, swap_all(): return lax.all_to_all(x, axes, split_axis=0, concat_axis=0, tiled=True)  132 us
    pallas_call x2, Pallas kernels, products(): pl.pallas_call(product_kernel, in_specs=[SMEM, VMEM, VMEM, VMEM, VMEM, HB...  14.9 us
    ppermute x6, starting transfers between devices, other_core(): return lax.ppermute(x, CORE, [(0, 1), (1, 0)])  12 us
    ppermute x6, waiting for transfers between devices, other_core(): return lax.ppermute(x, CORE, [(0, 1), (1, 0)])  7.75 us
  transfers between devices with their start and end apart: 6, of which 4 were waited for; matrix products, arithmetic and copies ran while one was open for 0% of the time, Pallas kernels for 1%

profile of v10, /device:TPU:1, one launch (start us, length us, event | category | flops | bytes accessed | tf_op | source)
XLA Modules:
  0.0 172.7 jit_solution(2417504346850974408)
XLA Ops:
  0.6 3.3 %collective-permute-start.1 = (bf16[8,512,512]{2,1,0:T(8,128)(2,1)}, bf16[8,512,512]{2,1,0:T(8,128)(2,1)S(1)}, u32[]{:S(2)}, u32[]{:S(2)}) collective-permute-start(bf16[8,512,512]{2,1,0:T(8,128)(2,1)} %left_a.3), channel_id=1, source_target_pairs={{0,1},{1,0},{2,3},{3,2},{4,5},{5,4},{6,7},{7,6},{8,9},{9,8},{10,11... | collective-permute-start | bytes 12582920 | tf_op jit(solution)/shard_map/ppermute | solution.py:30
  3.9 0.1 collective-permute-start.2
  4.0 0.9 opening.1
  5.0 20.1 %all_to_all.40.begun_ref = bf16[8,3,16,512]{3,2,1,0:T(8,128)(2,1)S(1)} all-to-all(bf16[8,3,16,512]{3,2,1,0:T(8,128)(2,1)S(1)} %get-tuple-element.17), channel_id=1, replica_groups=mesh['sector'=8,'op_0'=4,'op_1'=4,'op_2'=2] {'sector'}, dimensions={0} | all-to-all | bytes 786432 | tf_op jit(solution)/shard_map/all_to_all | solution.py:26
  25.0 0.0 copy-start
  25.0 0.1 spreading.1
  25.1 0.0 copy-start.2
  25.2 24.2 %all_to_all.41.mine_ref = bf16[16,10,16,256]{3,2,1,0:T(8,128)(2,1)S(1)} all-to-all(bf16[16,10,16,256]{3,2,1,0:T(8,128)(2,1)S(1)} %spreading.1), channel_id=1, replica_groups=mesh['sector'=8,'op_0'=4,'op_1'=4,'op_2'=2] {'op_1','op_0'}, dimensions={0} | all-to-all | bytes 2621440 | tf_op jit(solution)/shard_map/all_to_all | solution.py:26
  49.4 3.3 %collective-permute-start = (bf16[16,10,16,256]{3,2,1,0:T(8,128)(2,1)S(1)}, bf16[16,10,16,256]{3,2,1,0:T(8,128)(2,1)S(1)}, u32[]{:S(2)}, u32[]{:S(2)}) collective-permute-start(bf16[16,10,16,256]{3,2,1,0:T(8,128)(2,1)S(1)} %all_to_all.41.mine_ref), channel_id=1, source_target_pairs={{0,1},{1,0},{2,3},{3,2},{4,5},{5,4},{6,7},{7,6},{8,9},{9,8},{10,11... | collective-permute-start | bytes 3932168 | tf_op jit(solution)/shard_map/ppermute | solution.py:30
  52.7 2.7 %collective-permute-done.theirs_ref = bf16[16,10,16,256]{3,2,1,0:T(8,128)(2,1)S(1)} collective-permute-done((bf16[16,10,16,256]{3,2,1,0:T(8,128)(2,1)S(1)}, bf16[16,10,16,256]{3,2,1,0:T(8,128)(2,1)S(1)}, u32[]{:S(2)}, u32[]{:S(2)}) %collective-permute-start) | collective-permute-done | bytes 1310752 | tf_op jit(solution)/shard_map/ppermute | solution.py:30
  55.3 0.0 collective-permute-done.1.left_b
  55.3 0.0 collective-permute-done.2.right_b
  55.3 0.0 copy-done
  55.3 0.0 copy-done.2
  55.4 7.5 %products.2 = (bf16[16,64,128]{2,1,0:T(8,128)(2,1)S(1)}, bf16[16,72,128]{2,1,0:T(8,128)(2,1)S(1)}) custom-call(s32[8,256]{1,0:T(8,128)S(1)} %copy-done.2, bf16[16,10,16,256]{3,2,1,0:T(8,128)(2,1)S(1)} %all_to_all.41.mine_ref, bf16[16,10,16,256]{3,2,1,0:T(8,128)(2,1)S(1)} %collective-permute-done.theirs_ref, bf16[8,512,512]{2,1,0:T(8,128)(2,1)S(1)} %copy-done, ...), custom_call_target="tpu_custom_call" | custom-call | tf_op jit(solution)/shard_map/products/pallas_call | solution.py:187
  62.8 0.0 copy-start.3
  62.8 0.5 collective-permute-start.3
  63.3 1.2 collective-permute-done.3.got_ref
  64.5 0.1 pairing.2
  64.6 0.0 copy-start.1
  64.6 14.7 %all_to_all.42.arrived_ref = bf16[16,136,128]{2,1,0:T(8,128)(2,1)S(1)} all-to-all(bf16[16,136,128]{2,1,0:T(8,128)(2,1)S(1)} %pairing.2), channel_id=1, replica_groups=mesh['sector'=8,'op_0'=4,'op_1'=4,'op_2'=2] {'op_1','op_0'}, dimensions={0} | all-to-all | bytes 1114112 | tf_op jit(solution)/shard_map/all_to_all | solution.py:26
  79.3 0.0 copy-done.3
  79.3 0.7 joining.2
  79.9 12.7 %all_to_all.43.arrived_ref = bf16[8,136,128]{2,1,0:T(8,128)(2,1)S(1)} all-to-all(bf16[8,136,128]{2,1,0:T(8,128)(2,1)S(1)} %joining.2), channel_id=1, replica_groups=mesh['sector'=8,'op_0'=4,'op_1'=4,'op_2'=2] {'sector'}, dimensions={0} | all-to-all | bytes 557056 | tf_op jit(solution)/shard_map/all_to_all | solution.py:26
  92.7 0.0 copy-done.1
  92.7 0.6 middle.1
  93.3 19.0 %all_to_all.44.mine_ref = bf16[16,10,16,256]{3,2,1,0:T(8,128)(2,1)S(1)} all-to-all(bf16[16,10,16,256]{3,2,1,0:T(8,128)(2,1)S(1)} %get-tuple-element.22), channel_id=1, replica_groups=mesh['sector'=8,'op_0'=4,'op_1'=4,'op_2'=2] {'op_1','op_0'}, dimensions={0} | all-to-all | bytes 2621440 | tf_op jit(solution)/shard_map/all_to_all | solution.py:26
  112.3 4.5 %collective-permute-start.4 = (bf16[16,10,16,256]{3,2,1,0:T(8,128)(2,1)S(1)}, bf16[16,10,16,256]{3,2,1,0:T(8,128)(2,1)S(1)}, u32[]{:S(2)}, u32[]{:S(2)}) collective-permute-start(bf16[16,10,16,256]{3,2,1,0:T(8,128)(2,1)S(1)} %all_to_all.44.mine_ref), channel_id=1, source_target_pairs={{0,1},{1,0},{2,3},{3,2},{4,5},{5,4},{6,7},{7,6},{8,9},{9,8},{10,11... | collective-permute-start | bytes 3932168 | tf_op jit(solution)/shard_map/ppermute | solution.py:30
  116.7 2.7 %collective-permute-done.4.theirs_ref = bf16[16,10,16,256]{3,2,1,0:T(8,128)(2,1)S(1)} collective-permute-done((bf16[16,10,16,256]{3,2,1,0:T(8,128)(2,1)S(1)}, bf16[16,10,16,256]{3,2,1,0:T(8,128)(2,1)S(1)}, u32[]{:S(2)}, u32[]{:S(2)}) %collective-permute-start.4) | collective-permute-done | bytes 1310752 | tf_op jit(solution)/shard_map/ppermute | solution.py:30
  119.4 7.5 %products.3 = (bf16[16,64,128]{2,1,0:T(8,128)(2,1)S(1)}, bf16[16,72,128]{2,1,0:T(8,128)(2,1)S(1)}) custom-call(s32[8,256]{1,0:T(8,128)S(1)} %copy-done.2, bf16[16,10,16,256]{3,2,1,0:T(8,128)(2,1)S(1)} %all_to_all.44.mine_ref, bf16[16,10,16,256]{3,2,1,0:T(8,128)(2,1)S(1)} %collective-permute-done.4.theirs_ref, bf16[8,512,512]{2,1,0:T(8,128)(2,1)S(1)} %copy-done, ...), custom_call_target="tpu_custom_call" | custom-call | tf_op jit(solution)/shard_map/products/pallas_call | solution.py:187
  126.9 0.5 collective-permute-start.5
  127.3 1.2 collective-permute-done.5.got_ref
  128.5 0.1 pairing.3
  128.6 14.6 %all_to_all.45.arrived_ref = bf16[16,136,128]{2,1,0:T(8,128)(2,1)S(1)} all-to-all(bf16[16,136,128]{2,1,0:T(8,128)(2,1)S(1)} %pairing.3), channel_id=1, replica_groups=mesh['sector'=8,'op_0'=4,'op_1'=4,'op_2'=2] {'op_1','op_0'}, dimensions={0} | all-to-all | bytes 1114112 | tf_op jit(solution)/shard_map/all_to_all | solution.py:26
  143.2 0.7 joining.3
  143.9 12.8 %all_to_all.46.arrived_ref = bf16[8,136,128]{2,1,0:T(8,128)(2,1)S(1)} all-to-all(bf16[8,136,128]{2,1,0:T(8,128)(2,1)S(1)} %joining.3), channel_id=1, replica_groups=mesh['sector'=8,'op_0'=4,'op_1'=4,'op_2'=2] {'sector'}, dimensions={0} | all-to-all | bytes 557056 | tf_op jit(solution)/shard_map/all_to_all | solution.py:26
  156.7 1.3 closing.1
  158.0 14.0 %all_to_all.47.arrived_ref = f32[32,8,128]{2,1,0:T(8,128)S(1)} all-to-all(f32[32,8,128]{2,1,0:T(8,128)S(1)} %get-tuple-element.29), channel_id=1, replica_groups=mesh['sector'=8,'op_0'=4,'op_1'=4,'op_2'=2] {'op_0','op_1','op_2'}, dimensions={0} | all-to-all | bytes 262144 | tf_op jit(solution)/shard_map/all_to_all | solution.py:26
  172.0 0.7 scaling.1
Async XLA Ops:
  0.6 54.7 %collective-permute-start.1 = (bf16[8,512,512]{2,1,0:T(8,128)(2,1)}, bf16[8,512,512]{2,1,0:T(8,128)(2,1)S(1)}, u32[]{:S(2)}, u32[]{:S(2)}) collective-permute-start(bf16[8,512,512]{2,1,0:T(8,128)(2,1)} %left_a.3), channel_id=1, source_target_pairs={{0,1},{1,0},{2,3},{3,2},{4,5},{5,4},{6,7},{7,6},{8,9},{9,8},{10,11... | collective-permute-start | bytes 12582920 | tf_op jit(solution)/shard_map/ppermute | solution.py:30
  3.9 51.4 %collective-permute-start.2 = (bf16[8,512,512]{2,1,0:T(8,128)(2,1)}, bf16[8,512,512]{2,1,0:T(8,128)(2,1)S(1)}, u32[]{:S(2)}, u32[]{:S(2)}) collective-permute-start(bf16[8,512,512]{2,1,0:T(8,128)(2,1)} %right_a.3), channel_id=1, source_target_pairs={{0,1},{1,0},{2,3},{3,2},{4,5},{5,4},{6,7},{7,6},{8,9},{9,8},{10,11... | collective-permute-start | bytes 12582920 | tf_op jit(solution)/shard_map/ppermute | solution.py:30
  25.0 30.3 %copy-start = (bf16[8,512,512]{2,1,0:T(8,128)(2,1)S(1)}, bf16[8,512,512]{2,1,0:T(8,128)(2,1)}, u32[]{:S(2)}) copy-start(bf16[8,512,512]{2,1,0:T(8,128)(2,1)} %left_a.3) | copy-start | bytes 12582916
  25.1 30.2 %copy-start.2 = (s32[8,256]{1,0:T(8,128)S(1)}, s32[8,256]{1,0:T(8,128)}, u32[]{:S(2)}) copy-start(s32[8,256]{1,0:T(8,128)} %coupling_ref.3) | copy-start | bytes 24580
  49.4 5.9 %collective-permute-start = (bf16[16,10,16,256]{3,2,1,0:T(8,128)(2,1)S(1)}, bf16[16,10,16,256]{3,2,1,0:T(8,128)(2,1)S(1)}, u32[]{:S(2)}, u32[]{:S(2)}) collective-permute-start(bf16[16,10,16,256]{3,2,1,0:T(8,128)(2,1)S(1)} %all_to_all.41.mine_ref), channel_id=1, source_target_pairs={{0,1},{1,0},{2,3},{3,2},{4,5},{5,4},{6,7},{7,6},{8,9},{9,8},{10,11... | collective-permute-start | bytes 3932168 | tf_op jit(solution)/shard_map/ppermute | solution.py:30
  62.8 16.4 %copy-start.3 = (s32[8]{0:T(128)S(1)}, s32[8]{0:T(128)}, u32[]{:S(2)}) copy-start(s32[8]{0:T(128)} %sizes_ref.5) | copy-start | bytes 100
  62.8 1.7 collective-permute-start.3
  64.6 28.1 %copy-start.1 = (f32[1,16,512]{2,1,0:T(8,128)S(1)}, f32[1,16,512]{2,1,0:T(8,128)}, u32[]{:S(2)}) copy-start(f32[1,16,512]{2,1,0:T(8,128)} %diag_ref.5) | copy-start | bytes 98308
  112.3 7.1 %collective-permute-start.4 = (bf16[16,10,16,256]{3,2,1,0:T(8,128)(2,1)S(1)}, bf16[16,10,16,256]{3,2,1,0:T(8,128)(2,1)S(1)}, u32[]{:S(2)}, u32[]{:S(2)}) collective-permute-start(bf16[16,10,16,256]{3,2,1,0:T(8,128)(2,1)S(1)} %all_to_all.44.mine_ref), channel_id=1, source_target_pairs={{0,1},{1,0},{2,3},{3,2},{4,5},{5,4},{6,7},{7,6},{8,9},{9,8},{10,11... | collective-permute-start | bytes 3932168 | tf_op jit(solution)/shard_map/ppermute | solution.py:30
  126.9 1.7 collective-permute-start.5

commit v11 on v10

--- a/solution.py
+++ b/solution.py
@@ -271,7 +271,7 @@
     z, _, _ = place()
     first, second = scalars_of(arrived_ref)
     theta = first / (second + 1e-6)
-    theta_ref[0] = theta[0, 0]
+    theta_ref[...] = jnp.broadcast_to(theta, (8, LANES))
     for k in range(all_ref.shape[0]):
         diag = begun_ref[k, 1].astype(F32) + begun_ref[k, 2].astype(F32)
         update = corrected(begun_ref[k, 0].astype(F32), sigma_of(arrived_ref, k), diag, theta)
@@ -292,8 +292,8 @@
     scale = lax.rsqrt(second / entries + 1e-6)
     squared = scale * scale
     theta = squared * first / (squared * second + 1e-6)
-    theta_ref[0] = before_ref[0]
-    theta_ref[1] = theta[0, 0]
+    lane = lax.broadcasted_iota(jnp.int32, (8, LANES), 1)
+    theta_ref[...] = jnp.where(lane == 0, before_ref[...], theta)
     total = jnp.zeros(all_ref.shape[1:], F32)
     for k in range(all_ref.shape[0]):
         diag = begun_ref[k, 1].astype(F32) + begun_ref[k, 2].astype(F32)
@@ -304,7 +304,9 @@
     send_ref[...] = jnp.full(send_ref.shape, jnp.sum(total), F32)
 
 
-def scaling_kernel(entries, arrived_ref, final_ref, vector_ref):
+def scaling_kernel(entries, arrived_ref, final_ref, theta_ref, vector_ref, energies_ref):
+    energies_ref[0] = theta_ref[0, 0]
+    energies_ref[1] = theta_ref[0, 1]
     total = arrived_ref[0]
     for peer in range(1, arrived_ref.shape[0]):
         total = total + arrived_ref[peer]
@@ -371,28 +373,27 @@
     arrived = sigma_step(outgoing, square)
     outgoing, everyone, own, square, theta = call(
         middle_kernel,
-        [spread, ((sectors, share, block), F32), ((share, block), F32), scalar, ((1,), F32)],
+        [spread, ((sectors, share, block), F32), ((share, block), F32), scalar, scalar],
         [VMEM] * 4,
         "middle",
         [pltpu.VMEM((sectors, share, block), BF)],
-        [VMEM, VMEM, VMEM, VMEM, SMEM],
     )(arrived, begun, current, diagonal)
 
     arrived = sigma_step(outgoing, square)
     final, send, thetas = call(
         functools.partial(closing_kernel, entries),
-        [((share, block), F32), ((chips * 2, 8, LANES), F32), ((2,), F32)],
-        [VMEM, VMEM, VMEM, VMEM, VMEM, SMEM],
+        [((share, block), F32), ((chips * 2, 8, LANES), F32), scalar],
+        [VMEM] * 6,
         "closing",
-        outs=[VMEM, VMEM, SMEM],
     )(arrived, begun, everyone, own, diagonal, theta)
-    (vector,) = call(
+    vector, energies = call(
         functools.partial(scaling_kernel, entries),
-        [((1, share, block), F32)],
-        [VMEM] * 2,
+        [((1, share, block), F32), ((2,), F32)],
+        [VMEM] * 3,
         "scaling",
-    )(swap_all(send, OP), final)
-    return vector, thetas
+        outs=[VMEM, SMEM],
+    )(swap_all(send, OP), final, thetas)
+    return vector, energies
 
 
 def solution(mesh):

time: 173 us -> 172 us (level)
  no operation moved by 1% of the time
where the time goes in v11:
time: 172 us
  blocking collectives  132 us (77%)
  Pallas kernels  18.9 us (11%)
  starting transfers between devices  12 us (7%)
  waiting for transfers between devices  7.75 us (5%)
    all_to_all x8, blocking collectives, swap_all(): return lax.all_to_all(x, axes, split_axis=0, concat_axis=0, tiled=True)  132 us
    pallas_call x2, Pallas kernels, products(): pl.pallas_call(product_kernel, in_specs=[SMEM, VMEM, VMEM, VMEM, VMEM, HB...  14.9 us
    ppermute x6, starting transfers between devices, other_core(): return lax.ppermute(x, CORE, [(0, 1), (1, 0)])  12 us
    ppermute x6, waiting for transfers between devices, other_core(): return lax.ppermute(x, CORE, [(0, 1), (1, 0)])  7.75 us
  transfers between devices with their start and end apart: 6, of which 4 were waited for; matrix products, arithmetic and copies ran while one was open for 0% of the time, Pallas kernels for 1%

profile of v11, /device:TPU:1, one launch (start us, length us, event | category | flops | bytes accessed | tf_op | source)
XLA Modules:
  0.0 171.5 jit_solution(5347726842530724069)
XLA Ops:
  0.6 3.3 %collective-permute-start.1 = (bf16[8,512,512]{2,1,0:T(8,128)(2,1)}, bf16[8,512,512]{2,1,0:T(8,128)(2,1)S(1)}, u32[]{:S(2)}, u32[]{:S(2)}) collective-permute-start(bf16[8,512,512]{2,1,0:T(8,128)(2,1)} %left_a.3), channel_id=1, source_target_pairs={{0,1},{1,0},{2,3},{3,2},{4,5},{5,4},{6,7},{7,6},{8,9},{9,8},{10,11... | collective-permute-start | bytes 12582920 | tf_op jit(solution)/shard_map/ppermute | solution.py:30
  3.9 0.1 collective-permute-start.2
  4.0 0.9 opening.1
  5.0 20.1 %all_to_all.40.begun_ref = bf16[8,3,16,512]{3,2,1,0:T(8,128)(2,1)S(1)} all-to-all(bf16[8,3,16,512]{3,2,1,0:T(8,128)(2,1)S(1)} %get-tuple-element.17), channel_id=1, replica_groups=mesh['sector'=8,'op_0'=4,'op_1'=4,'op_2'=2] {'sector'}, dimensions={0} | all-to-all | bytes 786432 | tf_op jit(solution)/shard_map/all_to_all | solution.py:26
  25.0 0.0 copy-start
  25.0 0.1 spreading.1
  25.1 0.0 copy-start.2
  25.2 24.2 %all_to_all.41.mine_ref = bf16[16,10,16,256]{3,2,1,0:T(8,128)(2,1)S(1)} all-to-all(bf16[16,10,16,256]{3,2,1,0:T(8,128)(2,1)S(1)} %spreading.1), channel_id=1, replica_groups=mesh['sector'=8,'op_0'=4,'op_1'=4,'op_2'=2] {'op_1','op_0'}, dimensions={0} | all-to-all | bytes 2621440 | tf_op jit(solution)/shard_map/all_to_all | solution.py:26
  49.4 3.3 %collective-permute-start = (bf16[16,10,16,256]{3,2,1,0:T(8,128)(2,1)S(1)}, bf16[16,10,16,256]{3,2,1,0:T(8,128)(2,1)S(1)}, u32[]{:S(2)}, u32[]{:S(2)}) collective-permute-start(bf16[16,10,16,256]{3,2,1,0:T(8,128)(2,1)S(1)} %all_to_all.41.mine_ref), channel_id=1, source_target_pairs={{0,1},{1,0},{2,3},{3,2},{4,5},{5,4},{6,7},{7,6},{8,9},{9,8},{10,11... | collective-permute-start | bytes 3932168 | tf_op jit(solution)/shard_map/ppermute | solution.py:30
  52.7 2.7 %collective-permute-done.theirs_ref = bf16[16,10,16,256]{3,2,1,0:T(8,128)(2,1)S(1)} collective-permute-done((bf16[16,10,16,256]{3,2,1,0:T(8,128)(2,1)S(1)}, bf16[16,10,16,256]{3,2,1,0:T(8,128)(2,1)S(1)}, u32[]{:S(2)}, u32[]{:S(2)}) %collective-permute-start) | collective-permute-done | bytes 1310752 | tf_op jit(solution)/shard_map/ppermute | solution.py:30
  55.3 0.0 collective-permute-done.1.left_b
  55.3 0.0 collective-permute-done.2.right_b
  55.3 0.0 copy-done
  55.3 0.0 copy-done.2
  55.4 7.5 %products.2 = (bf16[16,64,128]{2,1,0:T(8,128)(2,1)S(1)}, bf16[16,72,128]{2,1,0:T(8,128)(2,1)S(1)}) custom-call(s32[8,256]{1,0:T(8,128)S(1)} %copy-done.2, bf16[16,10,16,256]{3,2,1,0:T(8,128)(2,1)S(1)} %all_to_all.41.mine_ref, bf16[16,10,16,256]{3,2,1,0:T(8,128)(2,1)S(1)} %collective-permute-done.theirs_ref, bf16[8,512,512]{2,1,0:T(8,128)(2,1)S(1)} %copy-done, ...), custom_call_target="tpu_custom_call" | custom-call | tf_op jit(solution)/shard_map/products/pallas_call | solution.py:187
  62.8 0.0 copy-start.3
  62.8 0.5 collective-permute-start.3
  63.3 1.2 collective-permute-done.3.got_ref
  64.5 0.1 pairing.2
  64.6 0.0 copy-start.1
  64.6 14.7 %all_to_all.42.arrived_ref = bf16[16,136,128]{2,1,0:T(8,128)(2,1)S(1)} all-to-all(bf16[16,136,128]{2,1,0:T(8,128)(2,1)S(1)} %pairing.2), channel_id=1, replica_groups=mesh['sector'=8,'op_0'=4,'op_1'=4,'op_2'=2] {'op_1','op_0'}, dimensions={0} | all-to-all | bytes 1114112 | tf_op jit(solution)/shard_map/all_to_all | solution.py:26
  79.3 0.0 copy-done.3
  79.3 0.7 joining.2
  79.9 12.7 %all_to_all.43.arrived_ref = bf16[8,136,128]{2,1,0:T(8,128)(2,1)S(1)} all-to-all(bf16[8,136,128]{2,1,0:T(8,128)(2,1)S(1)} %joining.2), channel_id=1, replica_groups=mesh['sector'=8,'op_0'=4,'op_1'=4,'op_2'=2] {'sector'}, dimensions={0} | all-to-all | bytes 557056 | tf_op jit(solution)/shard_map/all_to_all | solution.py:26
  92.7 0.0 copy-done.1
  92.7 0.4 middle.1
  93.0 19.0 %all_to_all.44.mine_ref = bf16[16,10,16,256]{3,2,1,0:T(8,128)(2,1)S(1)} all-to-all(bf16[16,10,16,256]{3,2,1,0:T(8,128)(2,1)S(1)} %get-tuple-element.22), channel_id=1, replica_groups=mesh['sector'=8,'op_0'=4,'op_1'=4,'op_2'=2] {'op_1','op_0'}, dimensions={0} | all-to-all | bytes 2621440 | tf_op jit(solution)/shard_map/all_to_all | solution.py:26
  112.1 4.5 %collective-permute-start.4 = (bf16[16,10,16,256]{3,2,1,0:T(8,128)(2,1)S(1)}, bf16[16,10,16,256]{3,2,1,0:T(8,128)(2,1)S(1)}, u32[]{:S(2)}, u32[]{:S(2)}) collective-permute-start(bf16[16,10,16,256]{3,2,1,0:T(8,128)(2,1)S(1)} %all_to_all.44.mine_ref), channel_id=1, source_target_pairs={{0,1},{1,0},{2,3},{3,2},{4,5},{5,4},{6,7},{7,6},{8,9},{9,8},{10,11... | collective-permute-start | bytes 3932168 | tf_op jit(solution)/shard_map/ppermute | solution.py:30
  116.5 2.7 %collective-permute-done.4.theirs_ref = bf16[16,10,16,256]{3,2,1,0:T(8,128)(2,1)S(1)} collective-permute-done((bf16[16,10,16,256]{3,2,1,0:T(8,128)(2,1)S(1)}, bf16[16,10,16,256]{3,2,1,0:T(8,128)(2,1)S(1)}, u32[]{:S(2)}, u32[]{:S(2)}) %collective-permute-start.4) | collective-permute-done | bytes 1310752 | tf_op jit(solution)/shard_map/ppermute | solution.py:30
  119.2 7.5 %products.3 = (bf16[16,64,128]{2,1,0:T(8,128)(2,1)S(1)}, bf16[16,72,128]{2,1,0:T(8,128)(2,1)S(1)}) custom-call(s32[8,256]{1,0:T(8,128)S(1)} %copy-done.2, bf16[16,10,16,256]{3,2,1,0:T(8,128)(2,1)S(1)} %all_to_all.44.mine_ref, bf16[16,10,16,256]{3,2,1,0:T(8,128)(2,1)S(1)} %collective-permute-done.4.theirs_ref, bf16[8,512,512]{2,1,0:T(8,128)(2,1)S(1)} %copy-done, ...), custom_call_target="tpu_custom_call" | custom-call | tf_op jit(solution)/shard_map/products/pallas_call | solution.py:187
  126.7 0.5 collective-permute-start.5
  127.1 1.2 collective-permute-done.5.got_ref
  128.3 0.1 pairing.3
  128.4 14.6 %all_to_all.45.arrived_ref = bf16[16,136,128]{2,1,0:T(8,128)(2,1)S(1)} all-to-all(bf16[16,136,128]{2,1,0:T(8,128)(2,1)S(1)} %pairing.3), channel_id=1, replica_groups=mesh['sector'=8,'op_0'=4,'op_1'=4,'op_2'=2] {'op_1','op_0'}, dimensions={0} | all-to-all | bytes 1114112 | tf_op jit(solution)/shard_map/all_to_all | solution.py:26
  143.0 0.7 joining.3
  143.7 12.8 %all_to_all.46.arrived_ref = bf16[8,136,128]{2,1,0:T(8,128)(2,1)S(1)} all-to-all(bf16[8,136,128]{2,1,0:T(8,128)(2,1)S(1)} %joining.3), channel_id=1, replica_groups=mesh['sector'=8,'op_0'=4,'op_1'=4,'op_2'=2] {'sector'}, dimensions={0} | all-to-all | bytes 557056 | tf_op jit(solution)/shard_map/all_to_all | solution.py:26
  156.5 0.3 closing.1
  156.8 14.0 %all_to_all.47.arrived_ref = f32[32,8,128]{2,1,0:T(8,128)S(1)} all-to-all(f32[32,8,128]{2,1,0:T(8,128)S(1)} %get-tuple-element.29), channel_id=1, replica_groups=mesh['sector'=8,'op_0'=4,'op_1'=4,'op_2'=2] {'op_0','op_1','op_2'}, dimensions={0} | all-to-all | bytes 262144 | tf_op jit(solution)/shard_map/all_to_all | solution.py:26
  170.8 0.7 scaling.1
Async XLA Ops:
  0.6 54.7 %collective-permute-start.1 = (bf16[8,512,512]{2,1,0:T(8,128)(2,1)}, bf16[8,512,512]{2,1,0:T(8,128)(2,1)S(1)}, u32[]{:S(2)}, u32[]{:S(2)}) collective-permute-start(bf16[8,512,512]{2,1,0:T(8,128)(2,1)} %left_a.3), channel_id=1, source_target_pairs={{0,1},{1,0},{2,3},{3,2},{4,5},{5,4},{6,7},{7,6},{8,9},{9,8},{10,11... | collective-permute-start | bytes 12582920 | tf_op jit(solution)/shard_map/ppermute | solution.py:30
  3.9 51.4 %collective-permute-start.2 = (bf16[8,512,512]{2,1,0:T(8,128)(2,1)}, bf16[8,512,512]{2,1,0:T(8,128)(2,1)S(1)}, u32[]{:S(2)}, u32[]{:S(2)}) collective-permute-start(bf16[8,512,512]{2,1,0:T(8,128)(2,1)} %right_a.3), channel_id=1, source_target_pairs={{0,1},{1,0},{2,3},{3,2},{4,5},{5,4},{6,7},{7,6},{8,9},{9,8},{10,11... | collective-permute-start | bytes 12582920 | tf_op jit(solution)/shard_map/ppermute | solution.py:30
  25.0 30.3 %copy-start = (bf16[8,512,512]{2,1,0:T(8,128)(2,1)S(1)}, bf16[8,512,512]{2,1,0:T(8,128)(2,1)}, u32[]{:S(2)}) copy-start(bf16[8,512,512]{2,1,0:T(8,128)(2,1)} %left_a.3) | copy-start | bytes 12582916
  25.1 30.2 %copy-start.2 = (s32[8,256]{1,0:T(8,128)S(1)}, s32[8,256]{1,0:T(8,128)}, u32[]{:S(2)}) copy-start(s32[8,256]{1,0:T(8,128)} %coupling_ref.3) | copy-start | bytes 24580
  49.4 5.9 %collective-permute-start = (bf16[16,10,16,256]{3,2,1,0:T(8,128)(2,1)S(1)}, bf16[16,10,16,256]{3,2,1,0:T(8,128)(2,1)S(1)}, u32[]{:S(2)}, u32[]{:S(2)}) collective-permute-start(bf16[16,10,16,256]{3,2,1,0:T(8,128)(2,1)S(1)} %all_to_all.41.mine_ref), channel_id=1, source_target_pairs={{0,1},{1,0},{2,3},{3,2},{4,5},{5,4},{6,7},{7,6},{8,9},{9,8},{10,11... | collective-permute-start | bytes 3932168 | tf_op jit(solution)/shard_map/ppermute | solution.py:30
  62.8 16.4 %copy-start.3 = (s32[8]{0:T(128)S(1)}, s32[8]{0:T(128)}, u32[]{:S(2)}) copy-start(s32[8]{0:T(128)} %sizes_ref.5) | copy-start | bytes 100
  62.8 1.7 collective-permute-start.3
  64.6 28.1 %copy-start.1 = (f32[1,16,512]{2,1,0:T(8,128)S(1)}, f32[1,16,512]{2,1,0:T(8,128)}, u32[]{:S(2)}) copy-start(f32[1,16,512]{2,1,0:T(8,128)} %diag_ref.5) | copy-start | bytes 98308
  112.1 7.1 %collective-permute-start.4 = (bf16[16,10,16,256]{3,2,1,0:T(8,128)(2,1)S(1)}, bf16[16,10,16,256]{3,2,1,0:T(8,128)(2,1)S(1)}, u32[]{:S(2)}, u32[]{:S(2)}) collective-permute-start(bf16[16,10,16,256]{3,2,1,0:T(8,128)(2,1)S(1)} %all_to_all.44.mine_ref), channel_id=1, source_target_pairs={{0,1},{1,0},{2,3},{3,2},{4,5},{5,4},{6,7},{7,6},{8,9},{9,8},{10,11... | collective-permute-start | bytes 3932168 | tf_op jit(solution)/shard_map/ppermute | solution.py:30
  126.7 1.7 collective-permute-start.5

commit v12 on v11

--- a/solution.py
+++ b/solution.py
@@ -69,8 +69,15 @@
     return jnp.concatenate([value[j * rows : (j + 1) * rows] for j in range(parts)], axis=1)
 
 
-def opening_kernel(sizes_ref, wave_ref, diag_ref, send_ref, current_ref, square_ref):
+def opening_kernel(
+    sizes_ref, wave_ref, diag_ref, send_ref, current_ref, square_ref, extent_ref
+):
     z, chip, core = place()
+    row = lax.broadcasted_iota(jnp.int32, (8, LANES), 0)
+    extent = jnp.full((8, LANES), sizes_ref[0], jnp.int32)
+    for k in range(1, 8):
+        extent = jnp.where(row == k, sizes_ref[k], extent)
+    extent_ref[...] = extent
     wave = wave_ref[0]
     inside = live(wave.shape, (chip * 2 + core) * SHARE, sizes_ref[z])
     current = jnp.where(inside, wave, 0.0)
@@ -218,7 +225,7 @@
         send_ref[peer, 2 * half :, :] = extra
 
 
-def joining_kernel(sizes_ref, arrived_ref, send_ref):
+def joining_kernel(extent_ref, arrived_ref, send_ref):
     z, chip, core = place()
     total = arrived_ref[0].astype(F32)
     for peer in range(1, arrived_ref.shape[0]):
@@ -229,7 +236,8 @@
     for j in range(2):
         sigma = unstacked(total[j * half : (j + 1) * half], SHARE)
         first_row = (chip * 2 + core) * SHARE
-        inside = live(sigma.shape, first_row, sizes_ref[(z // 2) * 2 + j])
+        size = extent_ref[pl.ds((z // 2) * 2 + j, 1), :][:, :1]
+        inside = live(sigma.shape, first_row, size)
         low = jnp.where(inside, sigma, 0.0).astype(BF)
         for k in range(low.shape[1] // LANES):
             at = j * half + k * SHARE
@@ -341,9 +349,14 @@
     spread = ((chips, sectors + 2, share, width), BF)
     scalar = ((8, LANES), F32)
 
-    begin, current, square = call(
+    begin, current, square, extent = call(
         opening_kernel,
-        [((sectors, 3, share, block), BF), ((share, block), F32), scalar],
+        [
+            ((sectors, 3, share, block), BF),
+            ((share, block), F32),
+            scalar,
+            ((8, LANES), jnp.int32),
+        ],
         [SMEM, VMEM, VMEM],
         "opening",
     )(*opening_inputs)
@@ -365,9 +378,9 @@
         (send,) = call(
             joining_kernel,
             [((sectors, block // 4 + TILE, LANES), BF)],
-            [SMEM, VMEM],
+            [VMEM] * 2,
             "joining",
-        )(sector_sizes, swap_all(send, CHIP))
+        )(extent, swap_all(send, CHIP))
         return swap_all(send, "sector")
 
     arrived = sigma_step(outgoing, square)

time: 172 us -> 171 us (level)
  no operation moved by 1% of the time
where the time goes in v12:
time: 171 us; the launch traced here: 170 us
  blocking collectives  132 us (77%)
  Pallas kernels  17.8 us (10%)
  starting transfers between devices  12.1 us (7%)
  waiting for transfers between devices  7.75 us (5%)
    all_to_all x8, blocking collectives, swap_all(): return lax.all_to_all(x, axes, split_axis=0, concat_axis=0, tiled=True)  132 us
    pallas_call x2, Pallas kernels, products(): pl.pallas_call(product_kernel, in_specs=[SMEM, VMEM, VMEM, VMEM, VMEM, HB...  14.9 us
    ppermute x6, starting transfers between devices, other_core(): return lax.ppermute(x, CORE, [(0, 1), (1, 0)])  12.1 us
    ppermute x6, waiting for transfers between devices, other_core(): return lax.ppermute(x, CORE, [(0, 1), (1, 0)])  7.75 us
  transfers between devices with their start and end apart: 6, of which 4 were waited for; matrix products, arithmetic and copies ran while one was open for 0% of the time, Pallas kernels for 1%

profile of v12, /device:TPU:1, one launch (start us, length us, event | category | flops | bytes accessed | tf_op | source)
XLA Modules:
  0.0 170.4 jit_solution(18175236329696064501)
XLA Ops:
  0.6 3.3 %collective-permute-start.1 = (bf16[8,512,512]{2,1,0:T(8,128)(2,1)}, bf16[8,512,512]{2,1,0:T(8,128)(2,1)S(1)}, u32[]{:S(2)}, u32[]{:S(2)}) collective-permute-start(bf16[8,512,512]{2,1,0:T(8,128)(2,1)} %left_a.3), channel_id=1, source_target_pairs={{0,1},{1,0},{2,3},{3,2},{4,5},{5,4},{6,7},{7,6},{8,9},{9,8},{10,11... | collective-permute-start | bytes 12582920 | tf_op jit(solution)/shard_map/ppermute | solution.py:30
  3.9 0.1 collective-permute-start.2
  4.0 0.9 opening.1
  5.0 20.1 %all_to_all.40.begun_ref = bf16[8,3,16,512]{3,2,1,0:T(8,128)(2,1)S(1)} all-to-all(bf16[8,3,16,512]{3,2,1,0:T(8,128)(2,1)S(1)} %get-tuple-element.19), channel_id=1, replica_groups=mesh['sector'=8,'op_0'=4,'op_1'=4,'op_2'=2] {'sector'}, dimensions={0} | all-to-all | bytes 786432 | tf_op jit(solution)/shard_map/all_to_all | solution.py:26
  25.0 0.0 copy-start
  25.0 0.1 spreading.1
  25.1 0.0 copy-start.2
  25.2 24.2 %all_to_all.41.mine_ref = bf16[16,10,16,256]{3,2,1,0:T(8,128)(2,1)S(1)} all-to-all(bf16[16,10,16,256]{3,2,1,0:T(8,128)(2,1)S(1)} %spreading.1), channel_id=1, replica_groups=mesh['sector'=8,'op_0'=4,'op_1'=4,'op_2'=2] {'op_1','op_0'}, dimensions={0} | all-to-all | bytes 2621440 | tf_op jit(solution)/shard_map/all_to_all | solution.py:26
  49.4 3.3 %collective-permute-start = (bf16[16,10,16,256]{3,2,1,0:T(8,128)(2,1)S(1)}, bf16[16,10,16,256]{3,2,1,0:T(8,128)(2,1)S(1)}, u32[]{:S(2)}, u32[]{:S(2)}) collective-permute-start(bf16[16,10,16,256]{3,2,1,0:T(8,128)(2,1)S(1)} %all_to_all.41.mine_ref), channel_id=1, source_target_pairs={{0,1},{1,0},{2,3},{3,2},{4,5},{5,4},{6,7},{7,6},{8,9},{9,8},{10,11... | collective-permute-start | bytes 3932168 | tf_op jit(solution)/shard_map/ppermute | solution.py:30
  52.7 2.7 %collective-permute-done.theirs_ref = bf16[16,10,16,256]{3,2,1,0:T(8,128)(2,1)S(1)} collective-permute-done((bf16[16,10,16,256]{3,2,1,0:T(8,128)(2,1)S(1)}, bf16[16,10,16,256]{3,2,1,0:T(8,128)(2,1)S(1)}, u32[]{:S(2)}, u32[]{:S(2)}) %collective-permute-start) | collective-permute-done | bytes 1310752 | tf_op jit(solution)/shard_map/ppermute | solution.py:30
  55.3 0.0 collective-permute-done.1.left_b
  55.3 0.0 collective-permute-done.2.right_b
  55.3 0.0 copy-done
  55.3 0.0 copy-done.2
  55.4 7.5 %products.2 = (bf16[16,64,128]{2,1,0:T(8,128)(2,1)S(1)}, bf16[16,72,128]{2,1,0:T(8,128)(2,1)S(1)}) custom-call(s32[8,256]{1,0:T(8,128)S(1)} %copy-done.2, bf16[16,10,16,256]{3,2,1,0:T(8,128)(2,1)S(1)} %all_to_all.41.mine_ref, bf16[16,10,16,256]{3,2,1,0:T(8,128)(2,1)S(1)} %collective-permute-done.theirs_ref, bf16[8,512,512]{2,1,0:T(8,128)(2,1)S(1)} %copy-done, ...), custom_call_target="tpu_custom_call" | custom-call | tf_op jit(solution)/shard_map/products/pallas_call | solution.py:194
  62.8 0.5 collective-permute-start.3
  63.3 1.2 collective-permute-done.3.got_ref
  64.5 0.1 pairing.2
  64.6 0.0 copy-start.1
  64.6 14.7 %all_to_all.42.arrived_ref = bf16[16,136,128]{2,1,0:T(8,128)(2,1)S(1)} all-to-all(bf16[16,136,128]{2,1,0:T(8,128)(2,1)S(1)} %pairing.2), channel_id=1, replica_groups=mesh['sector'=8,'op_0'=4,'op_1'=4,'op_2'=2] {'op_1','op_0'}, dimensions={0} | all-to-all | bytes 1114112 | tf_op jit(solution)/shard_map/all_to_all | solution.py:26
  79.3 0.1 joining.2
  79.4 12.7 %all_to_all.43.arrived_ref = bf16[8,136,128]{2,1,0:T(8,128)(2,1)S(1)} all-to-all(bf16[8,136,128]{2,1,0:T(8,128)(2,1)S(1)} %joining.2), channel_id=1, replica_groups=mesh['sector'=8,'op_0'=4,'op_1'=4,'op_2'=2] {'sector'}, dimensions={0} | all-to-all | bytes 557056 | tf_op jit(solution)/shard_map/all_to_all | solution.py:26
  92.1 0.0 copy-done.1
  92.1 0.4 middle.1
  92.5 19.0 %all_to_all.44.mine_ref = bf16[16,10,16,256]{3,2,1,0:T(8,128)(2,1)S(1)} all-to-all(bf16[16,10,16,256]{3,2,1,0:T(8,128)(2,1)S(1)} %get-tuple-element.24), channel_id=1, replica_groups=mesh['sector'=8,'op_0'=4,'op_1'=4,'op_2'=2] {'op_1','op_0'}, dimensions={0} | all-to-all | bytes 2621440 | tf_op jit(solution)/shard_map/all_to_all | solution.py:26
  111.5 4.5 %collective-permute-start.4 = (bf16[16,10,16,256]{3,2,1,0:T(8,128)(2,1)S(1)}, bf16[16,10,16,256]{3,2,1,0:T(8,128)(2,1)S(1)}, u32[]{:S(2)}, u32[]{:S(2)}) collective-permute-start(bf16[16,10,16,256]{3,2,1,0:T(8,128)(2,1)S(1)} %all_to_all.44.mine_ref), channel_id=1, source_target_pairs={{0,1},{1,0},{2,3},{3,2},{4,5},{5,4},{6,7},{7,6},{8,9},{9,8},{10,11... | collective-permute-start | bytes 3932168 | tf_op jit(solution)/shard_map/ppermute | solution.py:30
  116.0 2.7 %collective-permute-done.4.theirs_ref = bf16[16,10,16,256]{3,2,1,0:T(8,128)(2,1)S(1)} collective-permute-done((bf16[16,10,16,256]{3,2,1,0:T(8,128)(2,1)S(1)}, bf16[16,10,16,256]{3,2,1,0:T(8,128)(2,1)S(1)}, u32[]{:S(2)}, u32[]{:S(2)}) %collective-permute-start.4) | collective-permute-done | bytes 1310752 | tf_op jit(solution)/shard_map/ppermute | solution.py:30
  118.6 7.5 %products.3 = (bf16[16,64,128]{2,1,0:T(8,128)(2,1)S(1)}, bf16[16,72,128]{2,1,0:T(8,128)(2,1)S(1)}) custom-call(s32[8,256]{1,0:T(8,128)S(1)} %copy-done.2, bf16[16,10,16,256]{3,2,1,0:T(8,128)(2,1)S(1)} %all_to_all.44.mine_ref, bf16[16,10,16,256]{3,2,1,0:T(8,128)(2,1)S(1)} %collective-permute-done.4.theirs_ref, bf16[8,512,512]{2,1,0:T(8,128)(2,1)S(1)} %copy-done, ...), custom_call_target="tpu_custom_call" | custom-call | tf_op jit(solution)/shard_map/products/pallas_call | solution.py:194
  126.1 0.5 collective-permute-start.5
  126.6 1.2 collective-permute-done.5.got_ref
  127.8 0.1 pairing.3
  127.9 14.6 %all_to_all.45.arrived_ref = bf16[16,136,128]{2,1,0:T(8,128)(2,1)S(1)} all-to-all(bf16[16,136,128]{2,1,0:T(8,128)(2,1)S(1)} %pairing.3), channel_id=1, replica_groups=mesh['sector'=8,'op_0'=4,'op_1'=4,'op_2'=2] {'op_1','op_0'}, dimensions={0} | all-to-all | bytes 1114112 | tf_op jit(solution)/shard_map/all_to_all | solution.py:26
  142.5 0.1 joining.3
  142.6 12.8 %all_to_all.46.arrived_ref = bf16[8,136,128]{2,1,0:T(8,128)(2,1)S(1)} all-to-all(bf16[8,136,128]{2,1,0:T(8,128)(2,1)S(1)} %joining.3), channel_id=1, replica_groups=mesh['sector'=8,'op_0'=4,'op_1'=4,'op_2'=2] {'sector'}, dimensions={0} | all-to-all | bytes 557056 | tf_op jit(solution)/shard_map/all_to_all | solution.py:26
  155.4 0.3 closing.1
  155.7 14.0 %all_to_all.47.arrived_ref = f32[32,8,128]{2,1,0:T(8,128)S(1)} all-to-all(f32[32,8,128]{2,1,0:T(8,128)S(1)} %get-tuple-element.31), channel_id=1, replica_groups=mesh['sector'=8,'op_0'=4,'op_1'=4,'op_2'=2] {'op_0','op_1','op_2'}, dimensions={0} | all-to-all | bytes 262144 | tf_op jit(solution)/shard_map/all_to_all | solution.py:26
  169.7 0.7 scaling.1
Async XLA Ops:
  0.6 54.7 %collective-permute-start.1 = (bf16[8,512,512]{2,1,0:T(8,128)(2,1)}, bf16[8,512,512]{2,1,0:T(8,128)(2,1)S(1)}, u32[]{:S(2)}, u32[]{:S(2)}) collective-permute-start(bf16[8,512,512]{2,1,0:T(8,128)(2,1)} %left_a.3), channel_id=1, source_target_pairs={{0,1},{1,0},{2,3},{3,2},{4,5},{5,4},{6,7},{7,6},{8,9},{9,8},{10,11... | collective-permute-start | bytes 12582920 | tf_op jit(solution)/shard_map/ppermute | solution.py:30
  3.9 51.4 %collective-permute-start.2 = (bf16[8,512,512]{2,1,0:T(8,128)(2,1)}, bf16[8,512,512]{2,1,0:T(8,128)(2,1)S(1)}, u32[]{:S(2)}, u32[]{:S(2)}) collective-permute-start(bf16[8,512,512]{2,1,0:T(8,128)(2,1)} %right_a.3), channel_id=1, source_target_pairs={{0,1},{1,0},{2,3},{3,2},{4,5},{5,4},{6,7},{7,6},{8,9},{9,8},{10,11... | collective-permute-start | bytes 12582920 | tf_op jit(solution)/shard_map/ppermute | solution.py:30
  25.0 30.3 %copy-start = (bf16[8,512,512]{2,1,0:T(8,128)(2,1)S(1)}, bf16[8,512,512]{2,1,0:T(8,128)(2,1)}, u32[]{:S(2)}) copy-start(bf16[8,512,512]{2,1,0:T(8,128)(2,1)} %left_a.3) | copy-start | bytes 12582916
  25.1 30.2 %copy-start.2 = (s32[8,256]{1,0:T(8,128)S(1)}, s32[8,256]{1,0:T(8,128)}, u32[]{:S(2)}) copy-start(s32[8,256]{1,0:T(8,128)} %coupling_ref.3) | copy-start | bytes 24580
  49.4 5.9 %collective-permute-start = (bf16[16,10,16,256]{3,2,1,0:T(8,128)(2,1)S(1)}, bf16[16,10,16,256]{3,2,1,0:T(8,128)(2,1)S(1)}, u32[]{:S(2)}, u32[]{:S(2)}) collective-permute-start(bf16[16,10,16,256]{3,2,1,0:T(8,128)(2,1)S(1)} %all_to_all.41.mine_ref), channel_id=1, source_target_pairs={{0,1},{1,0},{2,3},{3,2},{4,5},{5,4},{6,7},{7,6},{8,9},{9,8},{10,11... | collective-permute-start | bytes 3932168 | tf_op jit(solution)/shard_map/ppermute | solution.py:30
  62.8 1.7 collective-permute-start.3
  64.6 27.5 %copy-start.1 = (f32[1,16,512]{2,1,0:T(8,128)S(1)}, f32[1,16,512]{2,1,0:T(8,128)}, u32[]{:S(2)}) copy-start(f32[1,16,512]{2,1,0:T(8,128)} %diag_ref.5) | copy-start | bytes 98308
  111.5 7.1 %collective-permute-start.4 = (bf16[16,10,16,256]{3,2,1,0:T(8,128)(2,1)S(1)}, bf16[16,10,16,256]{3,2,1,0:T(8,128)(2,1)S(1)}, u32[]{:S(2)}, u32[]{:S(2)}) collective-permute-start(bf16[16,10,16,256]{3,2,1,0:T(8,128)(2,1)S(1)} %all_to_all.44.mine_ref), channel_id=1, source_target_pairs={{0,1},{1,0},{2,3},{3,2},{4,5},{5,4},{6,7},{7,6},{8,9},{9,8},{10,11... | collective-permute-start | bytes 3932168 | tf_op jit(solution)/shard_map/ppermute | solution.py:30
  126.1 1.7 collective-permute-start.5

commit v13 on v12

--- a/solution.py
+++ b/solution.py
@@ -147,7 +147,6 @@
     for pair in range(1, pairs):
         fetch(pair).start()
         move(pair).start()
-    total[...] = jnp.zeros_like(total)
 
     def first(pair):
         for j, (owner, left) in enumerate(((core, left_a), (1 - core, left_b))):
@@ -156,10 +155,11 @@
             half = jnp.dot(left[pair], vector, preferred_element_type=F32)
             halves[pair % LAG1, :, j * width : (j + 1) * width] = half.astype(BF)
 
-    def second(pair):
-        total[...] += lax.dot_general(
+    def second(pair, opening=False):
+        term = lax.dot_general(
             halves[pair % LAG1], rights[pair], (((1,), (1,)), ((), ())), preferred_element_type=F32
         )
+        total[...] = term if opening else total[...] + term
 
     def both(pair, _):
         fetch(pair - LAG).wait()
@@ -170,7 +170,11 @@
 
     for pair in range(LAG):
         first(pair)
-    lax.fori_loop(LAG, pairs, both, 0)
+    fetch(0).wait()
+    move(0).wait()
+    second(0, True)
+    first(LAG)
+    lax.fori_loop(LAG + 1, pairs, both, 0)
     for pair in range(pairs - LAG, pairs):
         fetch(pair).wait()
         move(pair).wait()

time: 171 us -> 171 us (level)
  no operation moved by 1% of the time
where the time goes in v13:
time: 171 us; the launch traced here: 170 us
  blocking collectives  132 us (77%)
  Pallas kernels  17.7 us (10%)
  starting transfers between devices  12 us (7%)
  waiting for transfers between devices  7.75 us (5%)
    all_to_all x8, blocking collectives, swap_all(): return lax.all_to_all(x, axes, split_axis=0, concat_axis=0, tiled=True)  132 us
    pallas_call x2, Pallas kernels, products(): pl.pallas_call(product_kernel, in_specs=[SMEM, VMEM, VMEM, VMEM, VMEM, HB...  14.8 us
    ppermute x6, starting transfers between devices, other_core(): return lax.ppermute(x, CORE, [(0, 1), (1, 0)])  12 us
    ppermute x6, waiting for transfers between devices, other_core(): return lax.ppermute(x, CORE, [(0, 1), (1, 0)])  7.75 us
  transfers between devices with their start and end apart: 6, of which 4 were waited for; matrix products, arithmetic and copies ran while one was open for 0% of the time, Pallas kernels for 1%

profile of v13, /device:TPU:1, one launch (start us, length us, event | category | flops | bytes accessed | tf_op | source)
XLA Modules:
  0.0 170.4 jit_solution(15262797921094062648)
XLA Ops:
  0.6 3.3 %collective-permute-start.1 = (bf16[8,512,512]{2,1,0:T(8,128)(2,1)}, bf16[8,512,512]{2,1,0:T(8,128)(2,1)S(1)}, u32[]{:S(2)}, u32[]{:S(2)}) collective-permute-start(bf16[8,512,512]{2,1,0:T(8,128)(2,1)} %left_a.3), channel_id=1, source_target_pairs={{0,1},{1,0},{2,3},{3,2},{4,5},{5,4},{6,7},{7,6},{8,9},{9,8},{10,11... | collective-permute-start | bytes 12582920 | tf_op jit(solution)/shard_map/ppermute | solution.py:30
  3.9 0.1 collective-permute-start.2
  4.0 0.9 opening.1
  5.0 20.1 %all_to_all.40.begun_ref = bf16[8,3,16,512]{3,2,1,0:T(8,128)(2,1)S(1)} all-to-all(bf16[8,3,16,512]{3,2,1,0:T(8,128)(2,1)S(1)} %get-tuple-element.19), channel_id=1, replica_groups=mesh['sector'=8,'op_0'=4,'op_1'=4,'op_2'=2] {'sector'}, dimensions={0} | all-to-all | bytes 786432 | tf_op jit(solution)/shard_map/all_to_all | solution.py:26
  25.0 0.0 copy-start
  25.0 0.1 spreading.1
  25.1 0.0 copy-start.2
  25.2 24.2 %all_to_all.41.mine_ref = bf16[16,10,16,256]{3,2,1,0:T(8,128)(2,1)S(1)} all-to-all(bf16[16,10,16,256]{3,2,1,0:T(8,128)(2,1)S(1)} %spreading.1), channel_id=1, replica_groups=mesh['sector'=8,'op_0'=4,'op_1'=4,'op_2'=2] {'op_1','op_0'}, dimensions={0} | all-to-all | bytes 2621440 | tf_op jit(solution)/shard_map/all_to_all | solution.py:26
  49.4 3.3 %collective-permute-start = (bf16[16,10,16,256]{3,2,1,0:T(8,128)(2,1)S(1)}, bf16[16,10,16,256]{3,2,1,0:T(8,128)(2,1)S(1)}, u32[]{:S(2)}, u32[]{:S(2)}) collective-permute-start(bf16[16,10,16,256]{3,2,1,0:T(8,128)(2,1)S(1)} %all_to_all.41.mine_ref), channel_id=1, source_target_pairs={{0,1},{1,0},{2,3},{3,2},{4,5},{5,4},{6,7},{7,6},{8,9},{9,8},{10,11... | collective-permute-start | bytes 3932168 | tf_op jit(solution)/shard_map/ppermute | solution.py:30
  52.7 2.7 %collective-permute-done.theirs_ref = bf16[16,10,16,256]{3,2,1,0:T(8,128)(2,1)S(1)} collective-permute-done((bf16[16,10,16,256]{3,2,1,0:T(8,128)(2,1)S(1)}, bf16[16,10,16,256]{3,2,1,0:T(8,128)(2,1)S(1)}, u32[]{:S(2)}, u32[]{:S(2)}) %collective-permute-start) | collective-permute-done | bytes 1310752 | tf_op jit(solution)/shard_map/ppermute | solution.py:30
  55.3 0.0 collective-permute-done.1.left_b
  55.3 0.0 collective-permute-done.2.right_b
  55.3 0.0 copy-done
  55.3 0.0 copy-done.2
  55.4 7.4 %products.2 = (bf16[16,64,128]{2,1,0:T(8,128)(2,1)S(1)}, bf16[16,72,128]{2,1,0:T(8,128)(2,1)S(1)}) custom-call(s32[8,256]{1,0:T(8,128)S(1)} %copy-done.2, bf16[16,10,16,256]{3,2,1,0:T(8,128)(2,1)S(1)} %all_to_all.41.mine_ref, bf16[16,10,16,256]{3,2,1,0:T(8,128)(2,1)S(1)} %collective-permute-done.theirs_ref, bf16[8,512,512]{2,1,0:T(8,128)(2,1)S(1)} %copy-done, ...), custom_call_target="tpu_custom_call" | custom-call | tf_op jit(solution)/shard_map/products/pallas_call | solution.py:198
  62.8 0.5 collective-permute-start.3
  63.2 1.2 collective-permute-done.3.got_ref
  64.5 0.1 pairing.2
  64.5 0.0 copy-start.1
  64.6 14.7 %all_to_all.42.arrived_ref = bf16[16,136,128]{2,1,0:T(8,128)(2,1)S(1)} all-to-all(bf16[16,136,128]{2,1,0:T(8,128)(2,1)S(1)} %pairing.2), channel_id=1, replica_groups=mesh['sector'=8,'op_0'=4,'op_1'=4,'op_2'=2] {'op_1','op_0'}, dimensions={0} | all-to-all | bytes 1114112 | tf_op jit(solution)/shard_map/all_to_all | solution.py:26
  79.2 0.1 joining.2
  79.3 12.7 %all_to_all.43.arrived_ref = bf16[8,136,128]{2,1,0:T(8,128)(2,1)S(1)} all-to-all(bf16[8,136,128]{2,1,0:T(8,128)(2,1)S(1)} %joining.2), channel_id=1, replica_groups=mesh['sector'=8,'op_0'=4,'op_1'=4,'op_2'=2] {'sector'}, dimensions={0} | all-to-all | bytes 557056 | tf_op jit(solution)/shard_map/all_to_all | solution.py:26
  92.1 0.0 copy-done.1
  92.1 0.4 middle.1
  92.4 19.0 %all_to_all.44.mine_ref = bf16[16,10,16,256]{3,2,1,0:T(8,128)(2,1)S(1)} all-to-all(bf16[16,10,16,256]{3,2,1,0:T(8,128)(2,1)S(1)} %get-tuple-element.24), channel_id=1, replica_groups=mesh['sector'=8,'op_0'=4,'op_1'=4,'op_2'=2] {'op_1','op_0'}, dimensions={0} | all-to-all | bytes 2621440 | tf_op jit(solution)/shard_map/all_to_all | solution.py:26
  111.5 4.5 %collective-permute-start.4 = (bf16[16,10,16,256]{3,2,1,0:T(8,128)(2,1)S(1)}, bf16[16,10,16,256]{3,2,1,0:T(8,128)(2,1)S(1)}, u32[]{:S(2)}, u32[]{:S(2)}) collective-permute-start(bf16[16,10,16,256]{3,2,1,0:T(8,128)(2,1)S(1)} %all_to_all.44.mine_ref), channel_id=1, source_target_pairs={{0,1},{1,0},{2,3},{3,2},{4,5},{5,4},{6,7},{7,6},{8,9},{9,8},{10,11... | collective-permute-start | bytes 3932168 | tf_op jit(solution)/shard_map/ppermute | solution.py:30
  115.9 2.7 %collective-permute-done.4.theirs_ref = bf16[16,10,16,256]{3,2,1,0:T(8,128)(2,1)S(1)} collective-permute-done((bf16[16,10,16,256]{3,2,1,0:T(8,128)(2,1)S(1)}, bf16[16,10,16,256]{3,2,1,0:T(8,128)(2,1)S(1)}, u32[]{:S(2)}, u32[]{:S(2)}) %collective-permute-start.4) | collective-permute-done | bytes 1310752 | tf_op jit(solution)/shard_map/ppermute | solution.py:30
  118.6 7.4 %products.3 = (bf16[16,64,128]{2,1,0:T(8,128)(2,1)S(1)}, bf16[16,72,128]{2,1,0:T(8,128)(2,1)S(1)}) custom-call(s32[8,256]{1,0:T(8,128)S(1)} %copy-done.2, bf16[16,10,16,256]{3,2,1,0:T(8,128)(2,1)S(1)} %all_to_all.44.mine_ref, bf16[16,10,16,256]{3,2,1,0:T(8,128)(2,1)S(1)} %collective-permute-done.4.theirs_ref, bf16[8,512,512]{2,1,0:T(8,128)(2,1)S(1)} %copy-done, ...), custom_call_target="tpu_custom_call" | custom-call | tf_op jit(solution)/shard_map/products/pallas_call | solution.py:198
  126.0 0.5 collective-permute-start.5
  126.5 1.2 collective-permute-done.5.got_ref
  127.7 0.1 pairing.3
  127.8 14.6 %all_to_all.45.arrived_ref = bf16[16,136,128]{2,1,0:T(8,128)(2,1)S(1)} all-to-all(bf16[16,136,128]{2,1,0:T(8,128)(2,1)S(1)} %pairing.3), channel_id=1, replica_groups=mesh['sector'=8,'op_0'=4,'op_1'=4,'op_2'=2] {'op_1','op_0'}, dimensions={0} | all-to-all | bytes 1114112 | tf_op jit(solution)/shard_map/all_to_all | solution.py:26
  142.4 0.1 joining.3
  142.5 12.8 %all_to_all.46.arrived_ref = bf16[8,136,128]{2,1,0:T(8,128)(2,1)S(1)} all-to-all(bf16[8,136,128]{2,1,0:T(8,128)(2,1)S(1)} %joining.3), channel_id=1, replica_groups=mesh['sector'=8,'op_0'=4,'op_1'=4,'op_2'=2] {'sector'}, dimensions={0} | all-to-all | bytes 557056 | tf_op jit(solution)/shard_map/all_to_all | solution.py:26
  155.3 0.3 closing.1
  155.6 14.0 %all_to_all.47.arrived_ref = f32[32,8,128]{2,1,0:T(8,128)S(1)} all-to-all(f32[32,8,128]{2,1,0:T(8,128)S(1)} %get-tuple-element.31), channel_id=1, replica_groups=mesh['sector'=8,'op_0'=4,'op_1'=4,'op_2'=2] {'op_0','op_1','op_2'}, dimensions={0} | all-to-all | bytes 262144 | tf_op jit(solution)/shard_map/all_to_all | solution.py:26
  169.6 0.7 scaling.1
Async XLA Ops:
  0.6 54.7 %collective-permute-start.1 = (bf16[8,512,512]{2,1,0:T(8,128)(2,1)}, bf16[8,512,512]{2,1,0:T(8,128)(2,1)S(1)}, u32[]{:S(2)}, u32[]{:S(2)}) collective-permute-start(bf16[8,512,512]{2,1,0:T(8,128)(2,1)} %left_a.3), channel_id=1, source_target_pairs={{0,1},{1,0},{2,3},{3,2},{4,5},{5,4},{6,7},{7,6},{8,9},{9,8},{10,11... | collective-permute-start | bytes 12582920 | tf_op jit(solution)/shard_map/ppermute | solution.py:30
  3.9 51.4 %collective-permute-start.2 = (bf16[8,512,512]{2,1,0:T(8,128)(2,1)}, bf16[8,512,512]{2,1,0:T(8,128)(2,1)S(1)}, u32[]{:S(2)}, u32[]{:S(2)}) collective-permute-start(bf16[8,512,512]{2,1,0:T(8,128)(2,1)} %right_a.3), channel_id=1, source_target_pairs={{0,1},{1,0},{2,3},{3,2},{4,5},{5,4},{6,7},{7,6},{8,9},{9,8},{10,11... | collective-permute-start | bytes 12582920 | tf_op jit(solution)/shard_map/ppermute | solution.py:30
  25.0 30.3 %copy-start = (bf16[8,512,512]{2,1,0:T(8,128)(2,1)S(1)}, bf16[8,512,512]{2,1,0:T(8,128)(2,1)}, u32[]{:S(2)}) copy-start(bf16[8,512,512]{2,1,0:T(8,128)(2,1)} %left_a.3) | copy-start | bytes 12582916
  25.1 30.2 %copy-start.2 = (s32[8,256]{1,0:T(8,128)S(1)}, s32[8,256]{1,0:T(8,128)}, u32[]{:S(2)}) copy-start(s32[8,256]{1,0:T(8,128)} %coupling_ref.3) | copy-start | bytes 24580
  49.4 5.9 %collective-permute-start = (bf16[16,10,16,256]{3,2,1,0:T(8,128)(2,1)S(1)}, bf16[16,10,16,256]{3,2,1,0:T(8,128)(2,1)S(1)}, u32[]{:S(2)}, u32[]{:S(2)}) collective-permute-start(bf16[16,10,16,256]{3,2,1,0:T(8,128)(2,1)S(1)} %all_to_all.41.mine_ref), channel_id=1, source_target_pairs={{0,1},{1,0},{2,3},{3,2},{4,5},{5,4},{6,7},{7,6},{8,9},{9,8},{10,11... | collective-permute-start | bytes 3932168 | tf_op jit(solution)/shard_map/ppermute | solution.py:30
  62.8 1.7 collective-permute-start.3
  64.5 27.5 %copy-start.1 = (f32[1,16,512]{2,1,0:T(8,128)S(1)}, f32[1,16,512]{2,1,0:T(8,128)}, u32[]{:S(2)}) copy-start(f32[1,16,512]{2,1,0:T(8,128)} %diag_ref.5) | copy-start | bytes 98308
  111.5 7.1 %collective-permute-start.4 = (bf16[16,10,16,256]{3,2,1,0:T(8,128)(2,1)S(1)}, bf16[16,10,16,256]{3,2,1,0:T(8,128)(2,1)S(1)}, u32[]{:S(2)}, u32[]{:S(2)}) collective-permute-start(bf16[16,10,16,256]{3,2,1,0:T(8,128)(2,1)S(1)} %all_to_all.44.mine_ref), channel_id=1, source_target_pairs={{0,1},{1,0},{2,3},{3,2},{4,5},{5,4},{6,7},{7,6},{8,9},{9,8},{10,11... | collective-permute-start | bytes 3932168 | tf_op jit(solution)/shard_map/ppermute | solution.py:30
  126.0 1.7 collective-permute-start.5
